TPU v7x, 128 devices: a whole 4x4x4 slice. The times are simulated.
128 devices in a mesh: gx: 8 (over y, core), gy: 4 (over z), gz: 4 (over x).
Axes of the slice: x: 4, y: 4, z: 4, core: 2. Of those that a mesh axis runs over, the one named last changes fastest.
Arguments:
- velocity: float32 [32768, 3, 128], P(('gx', 'gy', 'gz')), may hold values from -6 to 6
- cell_index: int32 [32768, 128], P(('gx', 'gy', 'gz')), may hold values from 0 to 5804
- block_target: int32 [32768, 1], P(('gx', 'gy', 'gz')), may hold values from 0 to 127; in each aligned block of 256 rows (0 to 255, 256 to 511, ...) at most 3 rows name the same one
- rotation_axis: int32 [32, 32, 32], replicated, may hold values from 0 to 63
- grid_shift: int32 [3], replicated, may hold values from 0 to 31
Outputs:
- brick_velocity: float32 [128, 128, 3, 3, 128], P(('gx', 'gy', 'gz'))
- cell_flow: float32 [3, 32, 32, 512], P(None, 'gx', 'gy', 'gz')
Inputs may be any that keep to these rules, and one draw needn't show every extreme that they name: `block_target`: among the blocks that one device holds, no brick is named by more than 3 blocks, a bound that some block reaches.
All inputs are finite; a program needn't handle non-finite values.
Results may differ from a plain program's by a relative error of at most 0.0003.
Values sent between devices are 32-bit elements; how exact they have to be, the bound alone decides.
No kernel may reach another device: no remote copies, remote signals or barrier semaphores. Data moves between devices by JAX's collectives and lax.ppermute only.
A program may use at most 64 MiB of HBM per device.

v0:
```python
import jax
import jax.numpy as jnp
from jax import lax
from jax.sharding import PartitionSpec as P

CX = 4
CY = 8
CZ = 128
NAX = 64
APER = 32


angle_cosine = -0.6427876096865393
angle_sine = 0.766044443118978
highest = lax.Precision.HIGHEST


def split_up(value, dim, length):
    before, after = (value.shape[:dim], value.shape[dim + 1 :])
    return jnp.moveaxis(value.reshape(*before, length, -1, *after), dim, 0)


def laid_out(tiles, dim):
    lengths = list(tiles.shape[1:])
    lengths[dim] *= tiles.shape[0]
    return jnp.moveaxis(tiles, 0, dim).reshape(lengths)


def one_exchange(value, axis, axes, splits, concats):
    sizes = [lax.axis_size(a) for a in axes]
    tiles = split_up(value, splits[0], sizes[0])
    tiles = jnp.moveaxis(split_up(tiles, splits[1] + 1, sizes[1]), 0, 1)
    inside = tiles.shape[2:]
    tiles = tiles.reshape(-1, *inside)
    tiles = lax.all_to_all(tiles, axis, split_axis=0, concat_axis=0, tiled=True)
    tiles = laid_out(tiles.reshape(*sizes, *inside), concats[0] + 1)
    return laid_out(tiles, concats[1])


def with_halo(cells, sides, width):
    for axis, dim in sides:
        count = lax.axis_size(axis)
        head = lax.slice_in_dim(cells, 0, width, axis=dim)
        tail = lax.slice_in_dim(cells, cells.shape[dim] - width, cells.shape[dim], axis=dim)
        cells = jnp.concatenate(
            [
                lax.ppermute(tail, axis, [(i, (i + 1) % count) for i in range(count)]),
                cells,
                lax.ppermute(head, axis, [((i + 1) % count, i) for i in range(count)]),
            ],
            axis=dim,
        )
    return cells


def axis_table():
    counter = jnp.arange(NAX, dtype=jnp.float32) + 0.5
    height = 1.0 - 2.0 * counter / NAX
    radius = jnp.sqrt(jnp.maximum(1.0 - height * height, 0.0))
    turning = counter * 2.399963229728653
    return jnp.stack([radius * jnp.cos(turning), radius * jnp.sin(turning), height])


def rotate_about(direction, relative):
    inner_product = (
        direction[0] * relative[0] + direction[1] * relative[1] + direction[2] * relative[2]
    )
    crossed = [
        direction[1] * relative[2] - direction[2] * relative[1],
        direction[2] * relative[0] - direction[0] * relative[2],
        direction[0] * relative[1] - direction[1] * relative[0],
    ]
    return [
        relative[component] * angle_cosine
        + crossed[component] * angle_sine
        + direction[component] * inner_product * (1.0 - angle_cosine)
        for component in range(3)
    ]


def fold_rims(padded, dimension, length):
    inside = lax.slice_in_dim(padded, 1, length + 1, axis=dimension)
    lowest = lax.slice_in_dim(padded, 0, 1, axis=dimension)
    highest_rim = lax.slice_in_dim(padded, length + 1, length + 2, axis=dimension)
    position = lax.broadcasted_iota(jnp.int32, inside.shape, dimension)
    return (
        inside
        + jnp.where(position == 0, lowest, 0.0)
        + jnp.where(position == length - 1, highest_rim, 0.0)
    )


def plane_onehot(labels, planes):
    plane = jnp.where(labels >= 0, labels // (CZ + 1), -1)
    return (jnp.arange(planes, dtype=jnp.int32)[:, None] == plane[None, :]).astype(jnp.float32)


def depth_onehot(labels):
    depth = jnp.where(labels >= 0, labels % (CZ + 1), -1)
    return (depth[:, None] == jnp.arange(CZ + 1, dtype=jnp.int32)[None, :]).astype(jnp.float32)


def lookup_table(rotation_axis, index_x, index_y, index_z):
    table = rotation_axis.astype(jnp.float32)
    pick_x = (index_x[:, None] == jnp.arange(APER, dtype=jnp.int32)[None, :]).astype(jnp.float32)
    pick_y = (index_y[:, None] == jnp.arange(APER, dtype=jnp.int32)[None, :]).astype(jnp.float32)
    pick_z = (index_z[:, None] == jnp.arange(APER, dtype=jnp.int32)[None, :]).astype(jnp.float32)
    section = jnp.einsum("xa,abc->xbc", pick_x, table, precision=highest)
    section = jnp.einsum("xbc,yb->xyc", section, pick_y, precision=highest)
    section = jnp.einsum("xyc,zc->xyz", section, pick_z, precision=highest)
    return (section + 0.5).astype(jnp.int32)


def shards(velocity, cell_index, block_target, rotation_axis, grid_shift):
    devices = lax.axis_size(("gx", "gy", "gz"))
    blocks = velocity.shape[0]
    block_rows = velocity.shape[2]
    capacity = 3 * blocks // (2 * devices)
    slots = devices * capacity
    target = block_target[:, 0]
    target_onehot = (target[:, None] == jnp.arange(devices, dtype=jnp.int32)[None, :]).astype(
        jnp.float32
    )
    row_iota = lax.broadcasted_iota(jnp.int32, (blocks, blocks), 0)
    col_iota = lax.broadcasted_iota(jnp.int32, (blocks, blocks), 1)
    earlier = (row_iota > col_iota).astype(jnp.float32)
    before = jnp.dot(earlier, target_onehot, precision=highest)
    ranking = (jnp.sum(before * target_onehot, axis=1) + 0.5).astype(jnp.int32)
    places = target * capacity + ranking
    placing = (jnp.arange(slots, dtype=jnp.int32)[:, None] == places[None, :]).astype(jnp.float32)
    outgoing = jnp.dot(placing, velocity.reshape(blocks, 3 * block_rows), precision=highest)
    outgoing = outgoing.reshape(devices, capacity, 3, block_rows)
    shifted = jnp.dot(placing, (cell_index + 1).astype(jnp.float32), precision=highest)
    labels = (shifted + 0.5).astype(jnp.int32) - 1
    labels = labels.reshape(devices, capacity, block_rows)
    across = lax.axis_size("gx")
    arriving = one_exchange(
        outgoing.reshape(across, devices // across, capacity, 3, block_rows),
        ("gx", "gy", "gz"),
        ("gx", ("gy", "gz")),
        (0, 1),
        (0, 1),
    )
    arriving = arriving.reshape(devices, capacity, 3, block_rows)
    received = one_exchange(
        labels.reshape(across, devices // across, capacity, block_rows),
        ("gx", "gy", "gz"),
        ("gx", ("gy", "gz")),
        (0, 1),
        (0, 1),
    )
    received = received.reshape(devices, capacity, block_rows)
    planes = (CX + 1) * (CY + 1)
    extended = planes * (CZ + 1)
    groups = 8
    group_labels = received.reshape(groups, -1)
    group_moving = jnp.transpose(
        arriving.reshape(groups, devices // groups, capacity, 3, block_rows), (0, 3, 1, 2, 4)
    ).reshape(groups, 3, -1)

    def add_group(totals, inputs):
        labels_here, moving_here = inputs
        filled_here = (labels_here >= 0).astype(jnp.float32)
        channels = jnp.concatenate([filled_here[None], moving_here], axis=0)
        weighted = (channels[:, None, :] * plane_onehot(labels_here, planes)[None]).reshape(
            4 * planes, -1
        )
        return (totals + jnp.dot(weighted, depth_onehot(labels_here), precision=highest), None)

    totals, unused = lax.scan(
        add_group, jnp.zeros((4 * planes, CZ + 1), jnp.float32), (group_labels, group_moving)
    )
    partial_value = totals.reshape(4, CX + 1, CY + 1, CZ + 1)
    folded = fold_rims(with_halo(partial_value, (("gx", 1),), 1), 1, CX + 1)
    folded = fold_rims(with_halo(folded, (("gy", 2),), 1), 2, CY + 1)
    folded = fold_rims(with_halo(folded, (("gz", 3),), 1), 3, CZ + 1)
    cell_means = folded[1:] / jnp.maximum(folded[0], 1.0)
    cell_flow = cell_means[:, :CX, :CY, :CZ]
    index_x = (
        (lax.axis_index("gx") * CX + jnp.arange(CX + 1, dtype=jnp.int32))
        % (CX * lax.axis_size("gx"))
        + grid_shift[0]
    ) % APER
    index_y = (
        (lax.axis_index("gy") * CY + jnp.arange(CY + 1, dtype=jnp.int32))
        % (CY * lax.axis_size("gy"))
        + grid_shift[1]
    ) % APER
    index_z = (
        (lax.axis_index("gz") * CZ + jnp.arange(CZ + 1, dtype=jnp.int32))
        % (CZ * lax.axis_size("gz"))
        + grid_shift[2]
    ) % APER
    picked = lookup_table(rotation_axis, index_x, index_y, index_z).reshape(-1)
    choose = (jnp.arange(NAX, dtype=jnp.int32)[:, None] == picked[None, :]).astype(jnp.float32)
    direction = jnp.dot(axis_table(), choose, precision=highest)
    cell_rows = jnp.concatenate([cell_means.reshape(3, extended), direction], axis=0)
    cell_rows = cell_rows.reshape(6 * planes, CZ + 1)

    def read_group(carry, labels_here):
        by_depth = jnp.dot(cell_rows, depth_onehot(labels_here).T, precision=highest)
        by_depth = by_depth.reshape(6, planes, -1)
        return (carry, jnp.sum(by_depth * plane_onehot(labels_here, planes)[None], axis=1))

    unused, picked_rows = lax.scan(read_group, jnp.zeros((), jnp.float32), group_labels)
    gathered = jnp.transpose(picked_rows, (1, 0, 2)).reshape(6, devices, capacity, block_rows)
    filled = received >= 0
    relative = [arriving[:, :, component, :] - gathered[component] for component in range(3)]
    turned = rotate_about([gathered[3], gathered[4], gathered[5]], relative)
    updated = jnp.stack(
        [jnp.where(filled, gathered[component] + turned[component], 0.0) for component in range(3)],
        axis=2,
    )
    return (updated[None], cell_flow)


def solution(mesh):
    return jax.shard_map(
        shards,
        mesh=mesh,
        in_specs=(
            P(("gx", "gy", "gz"), None, None),
            P(("gx", "gy", "gz"), None),
            P(("gx", "gy", "gz"), None),
            P(),
            P(),
        ),
        out_specs=(P(("gx", "gy", "gz"), None, None, None, None), P(None, "gx", "gy", "gz")),
        check_vma=False,
    )
```

profile of v0, /device:TPU:0, one launch (start us, length us, event | category | flops | bytes accessed | tf_op | source)
XLA Modules:
  0.0 312.4 jit_solution(15013714707818790698)
XLA Ops:
  4.2 11.2 %all-to-all-start = ((s32[128,1,1,3,128]{4,2,3,1,0:T(1,128)}), s32[128,1,1,3,128]{4,2,3,1,0:T(1,128)S(1)}, u32[]{:S(2)}, u32[]{:S(2)}) async-start(s32[128,1,1,3,128]{4,2,3,1,0:T(1,128)} %bitcast.5), calls=%async_computation | async-start | bytes 393216 | tf_op jit(solution)/shard_map/all_to_all | solution.py:35
  22.1 3.5 %all-to-all-done = s32[128,1,1,3,128]{4,2,3,1,0:T(1,128)S(1)} async-done(((s32[128,1,1,3,128]{4,2,3,1,0:T(1,128)}), s32[128,1,1,3,128]{4,2,3,1,0:T(1,128)S(1)}, u32[]{:S(2)}, u32[]{:S(2)}) %all-to-all-start) | async-done | bytes 196640 | tf_op jit(solution)/shard_map/all_to_all | solution.py:35
  25.6 6.3 %all-to-all-start.1 = ((f32[128,1,1,3,3,128]{5,2,4,3,1,0:T(1,128)}), f32[128,1,1,3,3,128]{5,2,4,3,1,0:T(1,128)S(1)}, u32[]{:S(2)}, u32[]{:S(2)}) async-start(f32[128,1,1,3,3,128]{5,2,4,3,1,0:T(1,128)} %copy.96), calls=%async_computation.1 | async-start | bytes 1179648 | tf_op jit(solution)/shard_map/all_to_all | solution.py:35
  33.7 12.5 %all-to-all-done.1 = f32[128,1,1,3,3,128]{5,2,4,3,1,0:T(1,128)S(1)} async-done(((f32[128,1,1,3,3,128]{5,2,4,3,1,0:T(1,128)}), f32[128,1,1,3,3,128]{5,2,4,3,1,0:T(1,128)S(1)}, u32[]{:S(2)}, u32[]{:S(2)}) %all-to-all-start.1) | async-done | bytes 589856 | tf_op jit(solution)/shard_map/all_to_all | solution.py:35
  46.7 107.4 %while.26 = (s32[]{:T(128)}, f32[180,129]{0,1:T(8,128)S(1)}, s32[8,6144]{1,0:T(8,128)S(1)}, f32[8,3,6144]{2,0,1:T(8,128)S(1)}, s32[]{:T(128)}, /*index=5*/s32[]{:T(128)}) while((s32[]{:T(128)}, f32[180,129]{0,1:T(8,128)S(1)}, s32[8,6144]{1,0:T(8,128)S(1)}, f32[8,3,6144]{2,0,1:T(8,128)S(1)}, s32[]{:T(128)}, ...), condition=%wide.region_2.3_spmd.clone, body=%wide.region_1.2_spmd.clone.sunk | while | flops 1714597248 | bytes 20915716 | solution.py:170
  49.9 5.0 %mul.310 = f32[180,6144]{1,0:T(8,128)} reshape(f32[4,45,6144]{2,1,0:T(8,128)} %broadcast_multiply_fusion.2) | data formatting | bytes 8847360 | tf_op jit(solution)/shard_map/while/body/eval_jaxpr/mul | solution.py:165
  54.9 5.2 %fusion.80 = f32[180,129]{0,1:T(8,128)S(1)} fusion(f32[180,6144]{1,0:T(8,128)} %mul.310, s32[6144]{0:T(1024)S(1)} %fusion.79, f32[180,129]{0,1:T(8,128)S(1)} %get-tuple-element.286, pred[]{:T(512)S(6)} %compare.27), kind=kOutput, calls=%fused_computation.19.clone.1 | convolution fusion | flops 1712803200 | bytes 4634017 | tf_op jit(solution)/shard_map/while/body/eval_jaxpr/dot_general | solution.py:168
  63.3 5.0 %mul.310 = f32[180,6144]{1,0:T(8,128)} reshape(f32[4,45,6144]{2,1,0:T(8,128)} %broadcast_multiply_fusion.2) | data formatting | bytes 8847360 | tf_op jit(solution)/shard_map/while/body/eval_jaxpr/mul | solution.py:165
  68.3 5.2 %fusion.80 = f32[180,129]{0,1:T(8,128)S(1)} fusion(f32[180,6144]{1,0:T(8,128)} %mul.310, s32[6144]{0:T(1024)S(1)} %fusion.79, f32[180,129]{0,1:T(8,128)S(1)} %get-tuple-element.286, pred[]{:T(512)S(6)} %compare.27), kind=kOutput, calls=%fused_computation.19.clone.1 | convolution fusion | flops 1712803200 | bytes 4634017 | tf_op jit(solution)/shard_map/while/body/eval_jaxpr/dot_general | solution.py:168
  76.7 5.0 %mul.310 = f32[180,6144]{1,0:T(8,128)} reshape(f32[4,45,6144]{2,1,0:T(8,128)} %broadcast_multiply_fusion.2) | data formatting | bytes 8847360 | tf_op jit(solution)/shard_map/while/body/eval_jaxpr/mul | solution.py:165
  81.7 5.2 %fusion.80 = f32[180,129]{0,1:T(8,128)S(1)} fusion(f32[180,6144]{1,0:T(8,128)} %mul.310, s32[6144]{0:T(1024)S(1)} %fusion.79, f32[180,129]{0,1:T(8,128)S(1)} %get-tuple-element.286, pred[]{:T(512)S(6)} %compare.27), kind=kOutput, calls=%fused_computation.19.clone.1 | convolution fusion | flops 1712803200 | bytes 4634017 | tf_op jit(solution)/shard_map/while/body/eval_jaxpr/dot_general | solution.py:168
  90.1 5.0 %mul.310 = f32[180,6144]{1,0:T(8,128)} reshape(f32[4,45,6144]{2,1,0:T(8,128)} %broadcast_multiply_fusion.2) | data formatting | bytes 8847360 | tf_op jit(solution)/shard_map/while/body/eval_jaxpr/mul | solution.py:165
  95.1 5.2 %fusion.80 = f32[180,129]{0,1:T(8,128)S(1)} fusion(f32[180,6144]{1,0:T(8,128)} %mul.310, s32[6144]{0:T(1024)S(1)} %fusion.79, f32[180,129]{0,1:T(8,128)S(1)} %get-tuple-element.286, pred[]{:T(512)S(6)} %compare.27), kind=kOutput, calls=%fused_computation.19.clone.1 | convolution fusion | flops 1712803200 | bytes 4634017 | tf_op jit(solution)/shard_map/while/body/eval_jaxpr/dot_general | solution.py:168
  103.6 5.0 %mul.310 = f32[180,6144]{1,0:T(8,128)} reshape(f32[4,45,6144]{2,1,0:T(8,128)} %broadcast_multiply_fusion.2) | data formatting | bytes 8847360 | tf_op jit(solution)/shard_map/while/body/eval_jaxpr/mul | solution.py:165
  108.6 5.2 %fusion.80 = f32[180,129]{0,1:T(8,128)S(1)} fusion(f32[180,6144]{1,0:T(8,128)} %mul.310, s32[6144]{0:T(1024)S(1)} %fusion.79, f32[180,129]{0,1:T(8,128)S(1)} %get-tuple-element.286, pred[]{:T(512)S(6)} %compare.27), kind=kOutput, calls=%fused_computation.19.clone.1 | convolution fusion | flops 1712803200 | bytes 4634017 | tf_op jit(solution)/shard_map/while/body/eval_jaxpr/dot_general | solution.py:168
  117.0 5.0 %mul.310 = f32[180,6144]{1,0:T(8,128)} reshape(f32[4,45,6144]{2,1,0:T(8,128)} %broadcast_multiply_fusion.2) | data formatting | bytes 8847360 | tf_op jit(solution)/shard_map/while/body/eval_jaxpr/mul | solution.py:165
  122.0 5.2 %fusion.80 = f32[180,129]{0,1:T(8,128)S(1)} fusion(f32[180,6144]{1,0:T(8,128)} %mul.310, s32[6144]{0:T(1024)S(1)} %fusion.79, f32[180,129]{0,1:T(8,128)S(1)} %get-tuple-element.286, pred[]{:T(512)S(6)} %compare.27), kind=kOutput, calls=%fused_computation.19.clone.1 | convolution fusion | flops 1712803200 | bytes 4634017 | tf_op jit(solution)/shard_map/while/body/eval_jaxpr/dot_general | solution.py:168
  130.4 5.0 %mul.310 = f32[180,6144]{1,0:T(8,128)} reshape(f32[4,45,6144]{2,1,0:T(8,128)} %broadcast_multiply_fusion.2) | data formatting | bytes 8847360 | tf_op jit(solution)/shard_map/while/body/eval_jaxpr/mul | solution.py:165
  135.4 5.2 %fusion.80 = f32[180,129]{0,1:T(8,128)S(1)} fusion(f32[180,6144]{1,0:T(8,128)} %mul.310, s32[6144]{0:T(1024)S(1)} %fusion.79, f32[180,129]{0,1:T(8,128)S(1)} %get-tuple-element.286, pred[]{:T(512)S(6)} %compare.27), kind=kOutput, calls=%fused_computation.19.clone.1 | convolution fusion | flops 1712803200 | bytes 4634017 | tf_op jit(solution)/shard_map/while/body/eval_jaxpr/dot_general | solution.py:168
  143.8 5.0 %mul.310 = f32[180,6144]{1,0:T(8,128)} reshape(f32[4,45,6144]{2,1,0:T(8,128)} %broadcast_multiply_fusion.2) | data formatting | bytes 8847360 | tf_op jit(solution)/shard_map/while/body/eval_jaxpr/mul | solution.py:165
  148.8 5.2 %fusion.80 = f32[180,129]{0,1:T(8,128)S(1)} fusion(f32[180,6144]{1,0:T(8,128)} %mul.310, s32[6144]{0:T(1024)S(1)} %fusion.79, f32[180,129]{0,1:T(8,128)S(1)} %get-tuple-element.286, pred[]{:T(512)S(6)} %compare.27), kind=kOutput, calls=%fused_computation.19.clone.1 | convolution fusion | flops 1712803200 | bytes 4634017 | tf_op jit(solution)/shard_map/while/body/eval_jaxpr/dot_general | solution.py:168
  156.8 3.0 collective-permute-done
  175.7 128.6 %while.25 = (s32[]{:T(128)}, f32[8,6,6144]{2,1,0:T(8,128)S(1)}, s32[8,6144]{1,0:T(8,128)S(1)}, f32[270,129]{1,0:T(8,128)S(1)}, s32[]{:T(128)}) while((s32[]{:T(128)}, f32[8,6,6144]{2,1,0:T(8,128)S(1)}, s32[8,6144]{1,0:T(8,128)S(1)}, f32[270,129]{1,0:T(8,128)S(1)}, s32[]{:T(128)}) %tuple.101), condition=%wide.region_5.6_spmd, body=%wide.region_3.5_spmd.sunk | while | flops 2572677120 | bytes 29642888 | solution.py:205
  176.0 4.9 %convolution_bitcast_fusion.4 = f32[270,6144]{1,0:T(8,128)} fusion(f32[270,129]{1,0:T(8,128)S(1)} %get-tuple-element.310, s32[6144]{0:T(1024)S(1)} %fusion.74), kind=kOutput, calls=%fused_computation.clone.1 | convolution fusion | flops 2568738816 | bytes 6799416 | tf_op jit(solution)/shard_map/while/body/eval_jaxpr/dot_general | solution.py:201
  180.9 6.6 %reshape.372 = f32[6,45,6144]{2,1,0:T(8,128)} reshape(f32[270,6144]{1,0:T(8,128)} %convolution_bitcast_fusion.4) | data formatting | bytes 13271040 | tf_op jit(solution)/shard_map/while/body/eval_jaxpr/reshape | solution.py:202
  187.6 4.1 %multiply_reduce_fusion.2 = f32[6,6144]{1,0:T(8,128)S(1)} fusion(f32[6,45,6144]{2,1,0:T(8,128)} %reshape.372, f32[45,6144]{1,0:T(8,128)S(1)} %fusion.75), kind=kLoop, calls=%fused_computation.1.clone.1 | loop fusion | flops 3280896 | bytes 7888896 | tf_op jit(solution)/shard_map/while/body/eval_jaxpr/reduce_sum | solution.py:203
  192.1 4.9 %convolution_bitcast_fusion.4 = f32[270,6144]{1,0:T(8,128)} fusion(f32[270,129]{1,0:T(8,128)S(1)} %get-tuple-element.310, s32[6144]{0:T(1024)S(1)} %fusion.74), kind=kOutput, calls=%fused_computation.clone.1 | convolution fusion | flops 2568738816 | bytes 6799416 | tf_op jit(solution)/shard_map/while/body/eval_jaxpr/dot_general | solution.py:201
  197.0 6.6 %reshape.372 = f32[6,45,6144]{2,1,0:T(8,128)} reshape(f32[270,6144]{1,0:T(8,128)} %convolution_bitcast_fusion.4) | data formatting | bytes 13271040 | tf_op jit(solution)/shard_map/while/body/eval_jaxpr/reshape | solution.py:202
  203.7 4.1 %multiply_reduce_fusion.2 = f32[6,6144]{1,0:T(8,128)S(1)} fusion(f32[6,45,6144]{2,1,0:T(8,128)} %reshape.372, f32[45,6144]{1,0:T(8,128)S(1)} %fusion.75), kind=kLoop, calls=%fused_computation.1.clone.1 | loop fusion | flops 3280896 | bytes 7888896 | tf_op jit(solution)/shard_map/while/body/eval_jaxpr/reduce_sum | solution.py:203
  208.2 4.9 %convolution_bitcast_fusion.4 = f32[270,6144]{1,0:T(8,128)} fusion(f32[270,129]{1,0:T(8,128)S(1)} %get-tuple-element.310, s32[6144]{0:T(1024)S(1)} %fusion.74), kind=kOutput, calls=%fused_computation.clone.1 | convolution fusion | flops 2568738816 | bytes 6799416 | tf_op jit(solution)/shard_map/while/body/eval_jaxpr/dot_general | solution.py:201
  213.0 6.6 %reshape.372 = f32[6,45,6144]{2,1,0:T(8,128)} reshape(f32[270,6144]{1,0:T(8,128)} %convolution_bitcast_fusion.4) | data formatting | bytes 13271040 | tf_op jit(solution)/shard_map/while/body/eval_jaxpr/reshape | solution.py:202
  219.7 4.1 %multiply_reduce_fusion.2 = f32[6,6144]{1,0:T(8,128)S(1)} fusion(f32[6,45,6144]{2,1,0:T(8,128)} %reshape.372, f32[45,6144]{1,0:T(8,128)S(1)} %fusion.75), kind=kLoop, calls=%fused_computation.1.clone.1 | loop fusion | flops 3280896 | bytes 7888896 | tf_op jit(solution)/shard_map/while/body/eval_jaxpr/reduce_sum | solution.py:203
  224.2 4.9 %convolution_bitcast_fusion.4 = f32[270,6144]{1,0:T(8,128)} fusion(f32[270,129]{1,0:T(8,128)S(1)} %get-tuple-element.310, s32[6144]{0:T(1024)S(1)} %fusion.74), kind=kOutput, calls=%fused_computation.clone.1 | convolution fusion | flops 2568738816 | bytes 6799416 | tf_op jit(solution)/shard_map/while/body/eval_jaxpr/dot_general | solution.py:201
  229.1 6.6 %reshape.372 = f32[6,45,6144]{2,1,0:T(8,128)} reshape(f32[270,6144]{1,0:T(8,128)} %convolution_bitcast_fusion.4) | data formatting | bytes 13271040 | tf_op jit(solution)/shard_map/while/body/eval_jaxpr/reshape | solution.py:202
  235.8 4.1 %multiply_reduce_fusion.2 = f32[6,6144]{1,0:T(8,128)S(1)} fusion(f32[6,45,6144]{2,1,0:T(8,128)} %reshape.372, f32[45,6144]{1,0:T(8,128)S(1)} %fusion.75), kind=kLoop, calls=%fused_computation.1.clone.1 | loop fusion | flops 3280896 | bytes 7888896 | tf_op jit(solution)/shard_map/while/body/eval_jaxpr/reduce_sum | solution.py:203
  240.3 4.9 %convolution_bitcast_fusion.4 = f32[270,6144]{1,0:T(8,128)} fusion(f32[270,129]{1,0:T(8,128)S(1)} %get-tuple-element.310, s32[6144]{0:T(1024)S(1)} %fusion.74), kind=kOutput, calls=%fused_computation.clone.1 | convolution fusion | flops 2568738816 | bytes 6799416 | tf_op jit(solution)/shard_map/while/body/eval_jaxpr/dot_general | solution.py:201
  245.2 6.6 %reshape.372 = f32[6,45,6144]{2,1,0:T(8,128)} reshape(f32[270,6144]{1,0:T(8,128)} %convolution_bitcast_fusion.4) | data formatting | bytes 13271040 | tf_op jit(solution)/shard_map/while/body/eval_jaxpr/reshape | solution.py:202
  251.9 4.1 %multiply_reduce_fusion.2 = f32[6,6144]{1,0:T(8,128)S(1)} fusion(f32[6,45,6144]{2,1,0:T(8,128)} %reshape.372, f32[45,6144]{1,0:T(8,128)S(1)} %fusion.75), kind=kLoop, calls=%fused_computation.1.clone.1 | loop fusion | flops 3280896 | bytes 7888896 | tf_op jit(solution)/shard_map/while/body/eval_jaxpr/reduce_sum | solution.py:203
  256.4 4.9 %convolution_bitcast_fusion.4 = f32[270,6144]{1,0:T(8,128)} fusion(f32[270,129]{1,0:T(8,128)S(1)} %get-tuple-element.310, s32[6144]{0:T(1024)S(1)} %fusion.74), kind=kOutput, calls=%fused_computation.clone.1 | convolution fusion | flops 2568738816 | bytes 6799416 | tf_op jit(solution)/shard_map/while/body/eval_jaxpr/dot_general | solution.py:201
  261.3 6.6 %reshape.372 = f32[6,45,6144]{2,1,0:T(8,128)} reshape(f32[270,6144]{1,0:T(8,128)} %convolution_bitcast_fusion.4) | data formatting | bytes 13271040 | tf_op jit(solution)/shard_map/while/body/eval_jaxpr/reshape | solution.py:202
  268.0 4.1 %multiply_reduce_fusion.2 = f32[6,6144]{1,0:T(8,128)S(1)} fusion(f32[6,45,6144]{2,1,0:T(8,128)} %reshape.372, f32[45,6144]{1,0:T(8,128)S(1)} %fusion.75), kind=kLoop, calls=%fused_computation.1.clone.1 | loop fusion | flops 3280896 | bytes 7888896 | tf_op jit(solution)/shard_map/while/body/eval_jaxpr/reduce_sum | solution.py:203
  272.5 4.9 %convolution_bitcast_fusion.4 = f32[270,6144]{1,0:T(8,128)} fusion(f32[270,129]{1,0:T(8,128)S(1)} %get-tuple-element.310, s32[6144]{0:T(1024)S(1)} %fusion.74), kind=kOutput, calls=%fused_computation.clone.1 | convolution fusion | flops 2568738816 | bytes 6799416 | tf_op jit(solution)/shard_map/while/body/eval_jaxpr/dot_general | solution.py:201
  277.3 6.6 %reshape.372 = f32[6,45,6144]{2,1,0:T(8,128)} reshape(f32[270,6144]{1,0:T(8,128)} %convolution_bitcast_fusion.4) | data formatting | bytes 13271040 | tf_op jit(solution)/shard_map/while/body/eval_jaxpr/reshape | solution.py:202
  284.1 4.1 %multiply_reduce_fusion.2 = f32[6,6144]{1,0:T(8,128)S(1)} fusion(f32[6,45,6144]{2,1,0:T(8,128)} %reshape.372, f32[45,6144]{1,0:T(8,128)S(1)} %fusion.75), kind=kLoop, calls=%fused_computation.1.clone.1 | loop fusion | flops 3280896 | bytes 7888896 | tf_op jit(solution)/shard_map/while/body/eval_jaxpr/reduce_sum | solution.py:203
  288.5 4.9 %convolution_bitcast_fusion.4 = f32[270,6144]{1,0:T(8,128)} fusion(f32[270,129]{1,0:T(8,128)S(1)} %get-tuple-element.310, s32[6144]{0:T(1024)S(1)} %fusion.74), kind=kOutput, calls=%fused_computation.clone.1 | convolution fusion | flops 2568738816 | bytes 6799416 | tf_op jit(solution)/shard_map/while/body/eval_jaxpr/dot_general | solution.py:201
  293.4 6.6 %reshape.372 = f32[6,45,6144]{2,1,0:T(8,128)} reshape(f32[270,6144]{1,0:T(8,128)} %convolution_bitcast_fusion.4) | data formatting | bytes 13271040 | tf_op jit(solution)/shard_map/while/body/eval_jaxpr/reshape | solution.py:202
  300.1 4.1 %multiply_reduce_fusion.2 = f32[6,6144]{1,0:T(8,128)S(1)} fusion(f32[6,45,6144]{2,1,0:T(8,128)} %reshape.372, f32[45,6144]{1,0:T(8,128)S(1)} %fusion.75), kind=kLoop, calls=%fused_computation.1.clone.1 | loop fusion | flops 3280896 | bytes 7888896 | tf_op jit(solution)/shard_map/while/body/eval_jaxpr/reduce_sum | solution.py:203
  304.3 3.4 %slice_reduce_fusion.1 = (f32[8,6144]{1,0:T(8,128)S(1)}, f32[8,6144]{1,0:T(8,128)S(1)}, f32[8,6144]{1,0:T(8,128)}, f32[8,6144]{1,0:T(8,128)S(1)}, f32[8,6144]{1,0:T(8,128)}, /*index=5*/f32[8,6144]{1,0:T(8,128)S(1)}) fusion(f32[6,8,6144]{2,0,1:T(8,128)S(1)} %bitcast.118), kind=kLoop, calls=%fused_computation.65 | loop fusion | bytes 2359296 | tf_op jit(solution)/shard_map/slice | solution.py:208
  (183 shorter events, 63.9 us)
Async XLA Ops:
  0.6 15.9 %copy-start.3 = (s32[3]{0:T(128)S(1)}, s32[3]{0:T(128)}, u32[]{:S(2)}) copy-start(s32[3]{0:T(128)} %param.13) | copy-start | bytes 40
  0.6 16.5 %copy-start.1 = (f32[256,3,128]{2,0,1:T(8,128)S(1)}, f32[256,3,128]{2,0,1:T(8,128)}, u32[]{:S(2)}) copy-start(f32[256,3,128]{2,0,1:T(8,128)} %param.9) | copy-start | bytes 1179652
  4.2 21.4 %all-to-all-start = ((s32[128,1,1,3,128]{4,2,3,1,0:T(1,128)}), s32[128,1,1,3,128]{4,2,3,1,0:T(1,128)S(1)}, u32[]{:S(2)}, u32[]{:S(2)}) async-start(s32[128,1,1,3,128]{4,2,3,1,0:T(1,128)} %bitcast.5), calls=%async_computation | async-start | bytes 393216 | tf_op jit(solution)/shard_map/all_to_all | solution.py:35
  25.6 20.6 %all-to-all-start.1 = ((f32[128,1,1,3,3,128]{5,2,4,3,1,0:T(1,128)}), f32[128,1,1,3,3,128]{5,2,4,3,1,0:T(1,128)S(1)}, u32[]{:S(2)}, u32[]{:S(2)}) async-start(f32[128,1,1,3,3,128]{5,2,4,3,1,0:T(1,128)} %copy.96), calls=%async_computation.1 | async-start | bytes 1179648 | tf_op jit(solution)/shard_map/all_to_all | solution.py:35
  154.2 2.5 collective-permute-start.1
  154.9 4.9 %collective-permute-start = (f32[4,1,9,129]{3,2,1,0:T(8,128)S(1)}, f32[4,1,9,129]{3,2,1,0:T(8,128)S(1)}, u32[]{:S(2)}, u32[]{:S(2)}) collective-permute-start(f32[4,1,9,129]{3,2,1,0:T(8,128)S(1)} %get-tuple-element.204), channel_id=1, source_target_pairs={{0,16},{16,32},{32,48},{48,64},{64,80},{80,96},{96,112},{112,0},{1... | collective-permute-start | bytes 55736 | tf_op jit(solution)/shard_map/ppermute | solution.py:47
  159.9 3.9 %collective-permute-start.3 = (f32[4,5,1,129]{3,2,1,0:T(1,128)S(1)}, f32[4,5,1,129]{3,2,1,0:T(1,128)S(1)}, u32[]{:S(2)}, u32[]{:S(2)}) collective-permute-start(f32[4,5,1,129]{3,2,1,0:T(1,128)S(1)} %get-tuple-element.203), channel_id=1, source_target_pairs={{4,0},{8,4},{12,8},{0,12},{5,1},{9,5},{13,9},{1,13},{6,2},{10,6},{... | collective-permute-start | bytes 30968 | tf_op jit(solution)/shard_map/ppermute | solution.py:49
  160.4 5.0 %collective-permute-start.2 = (f32[4,5,1,129]{3,2,1,0:T(1,128)S(1)}, f32[4,5,1,129]{3,2,1,0:T(1,128)S(1)}, u32[]{:S(2)}, u32[]{:S(2)}) collective-permute-start(f32[4,5,1,129]{3,2,1,0:T(1,128)S(1)} %get-tuple-element.202), channel_id=1, source_target_pairs={{0,4},{4,8},{8,12},{12,0},{1,5},{5,9},{9,13},{13,1},{2,6},{6,10},{... | collective-permute-start | bytes 30968 | tf_op jit(solution)/shard_map/ppermute | solution.py:47
  165.7 5.4 %collective-permute-start.5 = (f32[4,5,9,1]{3,2,1,0:T(8,128)S(1)}, f32[4,5,9,1]{3,2,1,0:T(8,128)S(1)}, u32[]{:S(2)}, u32[]{:S(2)}) collective-permute-start(f32[4,5,9,1]{3,2,1,0:T(8,128)S(1)} %get-tuple-element.201), channel_id=1, source_target_pairs={{1,0},{2,1},{3,2},{0,3},{5,4},{6,5},{7,6},{4,7},{9,8},{10,9},{11,1... | collective-permute-start | bytes 2168 | tf_op jit(solution)/shard_map/ppermute | solution.py:49
  166.7 6.5 %collective-permute-start.4 = (f32[4,5,9,1]{3,2,1,0:T(8,128)S(1)}, f32[4,5,9,1]{3,2,1,0:T(8,128)S(1)}, u32[]{:S(2)}, u32[]{:S(2)}) collective-permute-start(f32[4,5,9,1]{3,2,1,0:T(8,128)S(1)} %get-tuple-element.200), channel_id=1, source_target_pairs={{0,1},{1,2},{2,3},{3,0},{4,5},{5,6},{6,7},{7,4},{8,9},{9,10},{10,1... | collective-permute-start | bytes 2168 | tf_op jit(solution)/shard_map/ppermute | solution.py:47
  171.3 4.4 %copy-start = (f32[8,6,6144]{2,1,0:T(8,128)S(1)}, f32[8,6,6144]{2,1,0:T(8,128)}, u32[]{:S(2)}) copy-start(f32[8,6,6144]{2,1,0:T(8,128)} %custom-call.1) | copy-start | bytes 3538948
  307.8 2.9 copy-start.2
where the time goes:
time: 314 us; the launch traced here: 312 us
  local copies, waits for them, and re-layouts  106 us (34%)
  matrix products  86.4 us (28%)
  other arithmetic  67.4 us (21%)
  waiting for transfers between devices  28.8 us (9%)
  starting transfers between devices  22.3 us (7%)
    reshape x8, local copies, waits for them, and re-layouts, read_group(): by_depth = by_depth.reshape(6, planes, -1)  53 us
    dot_general x8, matrix products, add_group(): jnp.dot(weighted, depth_onehot(labels_here), precision=highest)  41.7 us
    mul x8, local copies, waits for them, and re-layouts, add_group(): channels[:, None, :] * plane_onehot(labels_here, planes)[None]  39.8 us
    dot_general x8, matrix products, read_group(): jnp.dot(cell_rows, depth_onehot(labels_here).T, precision=highest)  39 us
    reduce_sum x8, other arithmetic, read_group(): jnp.sum(by_depth * plane_onehot(labels_here, planes)[None], axis=1)  33.2 us
    mul x8, other arithmetic, add_group(): channels[:, None, :] * plane_onehot(labels_here, planes)[None]  21.3 us
    all_to_all x2, starting transfers between devices, one_exchange(): tiles = lax.all_to_all(tiles, axis, split_axis=0, concat_axis=0, tiled=True)  17.4 us
    all_to_all x2, waiting for transfers between devices, one_exchange(): tiles = lax.all_to_all(tiles, axis, split_axis=0, concat_axis=0, tiled=True)  16 us
  transfers between devices with their start and end apart: 8, of which 8 were waited for; matrix products, arithmetic and copies ran while one was open for 3% of the time, Pallas kernels for 0%

commit v1 on v0

v1 whole, which is shorter than its diff:
```python
import functools

import jax
import jax.numpy as jnp
from jax import lax
from jax.experimental import pallas as pl
from jax.experimental.pallas import tpu as pltpu
from jax.sharding import PartitionSpec as P

CX = 4
CY = 8
CZ = 128
NAX = 64
APER = 32
MOST = 3
PX = CX + 1
PY = CY + 1
PLANES = PX * PY
ROWS = PLANES + 1
PADROWS = 48
EMPTY = 6400.0

angle_cosine = -0.6427876096865393
angle_sine = 0.766044443118978

f32 = jnp.float32
bf16 = jnp.bfloat16
i32 = jnp.int32


def iota(shape, dim):
    return lax.broadcasted_iota(i32, shape, dim)


def axis_table():
    counter = jnp.arange(NAX, dtype=f32) + 0.5
    height = 1.0 - 2.0 * counter / NAX
    radius = jnp.sqrt(jnp.maximum(1.0 - height * height, 0.0))
    turning = counter * 2.399963229728653
    return jnp.stack([radius * jnp.cos(turning), radius * jnp.sin(turning), height])


def split3(value):
    high = value.astype(bf16)
    rest = value - high.astype(f32)
    middle = rest.astype(bf16)
    return high, middle, (rest - middle.astype(f32)).astype(bf16)


def call(body, out_shape, **kw):
    return pl.pallas_call(
        body,
        out_shape=out_shape,
        compiler_params=pltpu.CompilerParams(vmem_limit_bytes=48 * 1024 * 1024),
        **kw,
    )


def pack_body(target_ref, velocity_ref, index_ref, out_ref):
    bricks = 128
    blocks = target_ref.shape[1]
    target = jnp.broadcast_to(target_ref[...], (bricks, blocks))
    onehot = target == iota((bricks, blocks), 0)
    onehot_bf = jnp.where(onehot, 1.0, 0.0).astype(bf16)
    earlier = jnp.where(iota((blocks, blocks), 0) < iota((blocks, blocks), 1), 1.0, 0.0)
    before = jnp.dot(onehot_bf, earlier.astype(bf16), preferred_element_type=f32)
    index = index_ref[...]
    plane = (index * 8129) >> 20
    depth = index - plane * (CZ + 1)
    top = depth == CZ
    label = jnp.where(top, PLANES * 128 + plane, plane * 128 + depth)
    parts = [velocity_ref[c] for c in range(3)] + [label.astype(f32) - EMPTY]
    splits = split3(jnp.concatenate(parts, axis=1))
    for rank in range(MOST):
        place = jnp.where(onehot & (before == float(rank)), 1.0, 0.0).astype(bf16)
        moved = sum(jnp.dot(place, s, preferred_element_type=f32) for s in reversed(splits))
        for c in range(4):
            value = moved[:, c * 128 : (c + 1) * 128]
            if c == 3:
                value = value + EMPTY
            out_ref[pl.ds(rank * 4 + c, bricks, stride=4 * MOST), :] = value


def axes_body(shift_ref, rotation_ref, out_ref, rows):
    base_x = lax.axis_index("gx") * CX + shift_ref[0]
    base_y = lax.axis_index("gy") * CY + shift_ref[1]
    rows[...] = jnp.zeros(rows.shape, i32)
    for ex in range(PX):
        for ey in range(PY):
            a = (base_x + ex) & (APER - 1)
            b = (base_y + ey) & (APER - 1)
            rows[pl.ds(ex * PY + ey, 1), :APER] = rotation_ref[a, pl.ds(b, 1), :]
    value = rows[...].astype(f32)
    value = value + pltpu.roll(value, 32, 1)
    value = value + pltpu.roll(value, 64, 1)
    value = pltpu.roll(value, (128 - shift_ref[2]) & 127, 1)
    first = column_as_row(value)
    out_ref[...] = jnp.where(iota(value.shape, 0) == PLANES, first, value)


def column_as_row(value):
    column = jnp.broadcast_to(value[:, 0:1], value.shape)
    same = iota(value.shape, 0) == iota(value.shape, 1)
    return jnp.sum(jnp.where(same, column, 0.0), axis=0, keepdims=True)


def gather_x_faces(total, c, head_ref, tail_ref):
    head_ref[c, 0:PY] = total[0:PY]
    head_ref[c, PY : PY + 1] = total[PLANES:ROWS]
    tail_ref[c, 0:PY] = total[PLANES - PY : PLANES]
    tail_ref[c, PY : PY + 1] = total[PLANES:ROWS]


SLOTS_STEP = 8


def deposit_body(slots_ref, total_ref, head_ref, tail_ref, acc, rows_q, rows_l):
    slots = slots_ref.shape[0] // 4
    label = slots_ref[pl.ds(3, slots, stride=4), :].astype(i32)
    rows_q[...] = (label >> 7).astype(f32)
    rows_l[...] = (label & 127).astype(f32)
    acc[...] = jnp.zeros(acc.shape, f32)
    sub8 = iota((8, 128), 0)
    sub16 = iota((16, 128), 0)
    half = jnp.where(sub16 >= 8, 1.0, 0.0).astype(bf16)
    step16 = sub16.astype(f32).astype(bf16)
    one = jnp.ones((16, 128), bf16)
    zero = jnp.zeros((16, 128), bf16)

    def step(i, carry):
        weighted, depths = [], []
        for k in range(SLOTS_STEP):
            slot = i * SLOTS_STEP + k
            own = slots_ref[pl.ds(pl.multiple_of(i * SLOTS_STEP * 4, 8) + 4 * k, 4), :]
            own = jnp.concatenate([own, own], axis=0)
            high = own.astype(bf16).astype(f32)
            value = jnp.where(sub8 < 4, high, own - high)
            value = jnp.where(sub8 == 3, 1.0, jnp.where(sub8 == 7, 0.0, value))
            value = jnp.concatenate([value, value], axis=0).astype(bf16)
            q = jnp.broadcast_to(rows_q[pl.ds(slot, 1), :], (16, 128)).astype(bf16) - half
            l = jnp.broadcast_to(rows_l[pl.ds(slot, 1), :], (16, 128)).astype(bf16) - step16
            weighted.append(
                jnp.concatenate(
                    [jnp.where(q == float(2 * j), value, zero) for j in range(ROWS // 2)], axis=0
                )
            )
            depths.append(
                jnp.concatenate(
                    [jnp.where(l == float(16 * j), one, zero) for j in range(8)], axis=0
                )
            )
        acc[...] += lax.dot_general(
            jnp.concatenate(weighted, axis=1),
            jnp.concatenate(depths, axis=1),
            (((1,), (1,)), ((), ())),
            preferred_element_type=f32,
        )
        return carry

    lax.fori_loop(0, slots // SLOTS_STEP, step, 0)
    for c in range(4):
        total = acc[pl.ds(c, ROWS, stride=8), :]
        if c < 3:
            total = total + acc[pl.ds(c + 4, ROWS, stride=8), :]
        total_ref[c, 0:ROWS] = total
        total_ref[c, ROWS:PADROWS] = jnp.zeros((PADROWS - ROWS, 128), f32)
        gather_x_faces(total, c, head_ref, tail_ref)


def moved_lanes(row, first, count, shift):
    lane = iota(row.shape, 1)
    rolled = pltpu.roll(row, shift % 128, 1)
    return jnp.where((lane >= first) & (lane < first + count), rolled, 0.0)


def fold_x_body(total_ref, up_ref, down_ref, out_ref, head_ref, tail_ref):
    last = PLANES - PY
    for c in range(4):
        out_ref[c] = total_ref[c]
        out_ref[c, 0:PY] = total_ref[c, 0:PY] + down_ref[c, 0:PY]
        out_ref[c, last:PLANES] = total_ref[c, last:PLANES] + up_ref[c, 0:PY]
        out_ref[c, PLANES:ROWS] = (
            total_ref[c, PLANES:ROWS]
            + moved_lanes(up_ref[c, PY : PY + 1], last, PY, last)
            + moved_lanes(down_ref[c, PY : PY + 1], 0, PY, -last)
        )
        head_ref[c, 0:PX] = out_ref[c, pl.ds(0, PX, stride=PY)]
        head_ref[c, PX : PX + 1] = out_ref[c, PLANES:ROWS]
        tail_ref[c, 0:PX] = out_ref[c, pl.ds(CY, PX, stride=PY)]
        tail_ref[c, PX : PX + 1] = out_ref[c, PLANES:ROWS]


def fold_y_body(total_ref, up_ref, down_ref, out_ref, head_ref, tail_ref):
    lane = iota((1, 128), 1)
    for c in range(4):
        out_ref[c] = total_ref[c]
        out_ref[c, pl.ds(CY, PX, stride=PY)] = (
            total_ref[c, pl.ds(CY, PX, stride=PY)] + up_ref[c, 0:PX]
        )
        out_ref[c, pl.ds(0, PX, stride=PY)] = (
            total_ref[c, pl.ds(0, PX, stride=PY)] + down_ref[c, 0:PX]
        )
        up = pltpu.roll(up_ref[c, PX : PX + 1], CY, 1)
        down = pltpu.roll(down_ref[c, PX : PX + 1], 128 - CY, 1)
        edge = lane % PY
        out_ref[c, PLANES:ROWS] = (
            total_ref[c, PLANES:ROWS]
            + jnp.where((edge == CY) & (lane < PLANES), up, 0.0)
            + jnp.where((edge == 0) & (lane < PLANES), down, 0.0)
        )
        total = out_ref[c]
        head_ref[c : c + 1] = column_as_row(total)
        tail_ref[c : c + 1] = total[PLANES:ROWS]
        head_ref[4 + c : 5 + c] = jnp.zeros((1, 128), f32)
        tail_ref[4 + c : 5 + c] = jnp.zeros((1, 128), f32)


GROUP = 4


def collide_body(
    total_ref, up_ref, down_ref, axes_ref, units_ref, slots_ref, out_ref, flow_ref, cells
):
    shape = (PADROWS, 128)
    row = iota(shape, 0)
    lane = iota(shape, 1)
    top = (row == PLANES) & (lane < PLANES)
    totals = []
    for c in range(4):
        own = total_ref[c]
        column = jnp.sum(
            jnp.where((row == lane) & (row < PLANES), down_ref[c : c + 1], 0.0),
            axis=1,
            keepdims=True,
        )
        own = own + jnp.where(lane == 0, column, 0.0)
        totals.append(own + jnp.where(top, up_ref[c : c + 1], 0.0))
    count = jnp.maximum(totals[3], 1.0)
    for c in range(3):
        mean = totals[c] / count
        cells[c] = mean
        for ex in range(CX):
            flow_ref[c, ex] = mean[ex * PY : ex * PY + CY]
    cells[3] = axes_ref[...]
    units = [jnp.broadcast_to(units_ref[c : c + 1], (8, 128)) for c in range(3)]

    def step(i, carry):
        places = []
        for k in range(GROUP):
            first = pl.multiple_of((i % (16 // GROUP)) * (8 * GROUP * 12), 8 * GROUP * 12)
            first = first + (i // (16 // GROUP)) * 4 + k * 8 * 12
            places.append(first)
        labels = [slots_ref[pl.ds(p + 3, 8, stride=12), :].astype(i32) for p in places]
        rows = [label >> 7 for label in labels]
        lanes = [label & 127 for label in labels]
        found = [[jnp.zeros((8, 128), f32) for c in range(4)] for k in range(GROUP)]
        for q in range(ROWS):
            for c in range(4):
                table = jnp.broadcast_to(cells[c, q : q + 1], (8, 128))
                for k in range(GROUP):
                    read = jnp.take_along_axis(table, lanes[k], axis=1)
                    found[k][c] = jnp.where(rows[k] == q, read, found[k][c])
        for k in range(GROUP):
            which = found[k][3].astype(i32)
            n = [jnp.take_along_axis(units[c], which, axis=1) for c in range(3)]
            u = found[k][:3]
            w = [slots_ref[pl.ds(places[k] + c, 8, stride=12), :] - u[c] for c in range(3)]
            inner = n[0] * w[0] + n[1] * w[1] + n[2] * w[2]
            crossed = [
                n[1] * w[2] - n[2] * w[1],
                n[2] * w[0] - n[0] * w[2],
                n[0] * w[1] - n[1] * w[0],
            ]
            rank = i // (16 // GROUP)
            source = pl.multiple_of((i % (16 // GROUP)) * (8 * GROUP) + 8 * k, 8)
            for c in range(3):
                out_ref[rank, c, pl.ds(source, 8), :] = (
                    u[c]
                    + w[c] * angle_cosine
                    + crossed[c] * angle_sine
                    + n[c] * inner * (1.0 - angle_cosine)
                )
        return carry

    lax.fori_loop(0, MOST * 16 // GROUP, step, 0)


def both_ways(head, tail, axis):
    count = lax.axis_size(axis)
    up = lax.ppermute(head, axis, [((i + 1) % count, i) for i in range(count)])
    down = lax.ppermute(tail, axis, [(i, (i + 1) % count) for i in range(count)])
    return up, down


def shards(velocity, cell_index, block_target, rotation_axis, grid_shift):
    devices = 128
    shape = jax.ShapeDtypeStruct
    vmem = pl.BlockSpec(memory_space=pltpu.VMEM)
    smem = pl.BlockSpec(memory_space=pltpu.SMEM)
    send = call(pack_body, shape((devices * MOST * 4, 128), f32), name="pack")(
        block_target.reshape(1, -1), jnp.transpose(velocity, (1, 0, 2)), cell_index
    )
    axes = call(
        axes_body,
        shape((PADROWS, 128), f32),
        in_specs=[smem, vmem],
        scratch_shapes=[pltpu.VMEM((PADROWS, 128), i32)],
        name="axes",
    )(grid_shift, rotation_axis)
    units = jnp.pad(axis_table(), ((0, 5), (0, 128 - NAX)))
    slots = lax.all_to_all(
        send.reshape(devices, MOST * 4, 128), ("gx", "gy", "gz"), split_axis=0, concat_axis=0, tiled=True
    ).reshape(devices * MOST * 4, 128)
    total_shape = shape((4, PADROWS, 128), f32)
    x_face = shape((4, 16, 128), f32)
    y_face = shape((4, 8, 128), f32)
    z_face = shape((8, 128), f32)
    total, head, tail = call(
        deposit_body,
        [total_shape, x_face, x_face],
        scratch_shapes=[
            pltpu.VMEM((ROWS * 8, 128), f32),
            pltpu.VMEM((devices * MOST, 128), f32),
            pltpu.VMEM((devices * MOST, 128), f32),
        ],
        name="deposit",
    )(slots)
    up, down = both_ways(head, tail, "gx")
    total, head, tail = call(fold_x_body, [total_shape, y_face, y_face], name="fold_x")(
        total, up, down
    )
    up, down = both_ways(head, tail, "gy")
    total, head, tail = call(fold_y_body, [total_shape, z_face, z_face], name="fold_y")(
        total, up, down
    )
    up, down = both_ways(head, tail, "gz")
    updated, cell_flow = call(
        collide_body,
        [shape((MOST, 3, devices, 128), f32), shape((3, CX, CY, CZ), f32)],
        scratch_shapes=[pltpu.VMEM((4, PADROWS, 128), f32)],
        name="collide",
    )(total, up, down, axes, units, slots)
    return jnp.transpose(updated, (2, 0, 1, 3))[None], cell_flow


def solution(mesh):
    return jax.shard_map(
        shards,
        mesh=mesh,
        in_specs=(
            P(("gx", "gy", "gz"), None, None),
            P(("gx", "gy", "gz"), None),
            P(("gx", "gy", "gz"), None),
            P(),
            P(),
        ),
        out_specs=(P(("gx", "gy", "gz"), None, None, None, None), P(None, "gx", "gy", "gz")),
        check_vma=False,
    )
```

time: 314 us -> 96.3 us (0.31)
  local copies, waits for them, and re-layouts: 106 us -> 3.35 us
  matrix products: 86.4 us -> 0 us
  other arithmetic: 67.4 us -> 0.07 us
  Pallas kernels: 0 us -> 46.9 us
  blocking collectives: 0 us -> 30 us
  waiting for transfers between devices: 28.8 us -> 10.4 us
  starting transfers between devices: 22.3 us -> 4.71 us
    dot_general x23 -> x0, matrix products: 86.4 us -> none  [the longest x8 41.7 us: add_group(): jnp.dot(weighted, depth_onehot(labels_here), precision=highest)]
    reshape x14 -> x2, local copies, waits for them, and re-layouts: 54 us -> 0.14 us  [the longest x1 0.07 us: shards(): send.reshape(devices, MOST * 4, 128)]
    pallas_call x0 -> x6, Pallas kernels: none -> 46.9 us  [the longest x1 27.4 us: shards(): call(collide_body, [shape((MOST, 3, devices, 128), f32), shape((3, CX, CY...]
    mul x8 -> x0, local copies, waits for them, and re-layouts: 39.8 us -> none  [add_group(): channels[:, None, :] * plane_onehot(labels_here, planes)[None]]
    reduce_sum x8 -> x0, other arithmetic: 33.2 us -> none  [read_group(): jnp.sum(by_depth * plane_onehot(labels_here, planes)[None], axis=1)]
    all_to_all x0 -> x1, blocking collectives: none -> 30 us  [shards(): lax.all_to_all(send.reshape(devices, MOST * 4, 128), ('gx', 'gy', 'gz'),...]
    mul x8 -> x0, other arithmetic: 21.3 us -> none  [add_group(): channels[:, None, :] * plane_onehot(labels_here, planes)[None]]
    all_to_all x2 -> x0, starting transfers between devices: 17.4 us -> none  [one_exchange(): tiles = lax.all_to_all(tiles, axis, split_axis=0, concat_axis=0, tiled=True)]
  transfers between devices with their start and end apart: 8 -> 6, of which waited for: 8 -> 5; matrix products, arithmetic and copies ran while one was open for 3% -> 0% of each run, Pallas kernels for 0% -> 1%
where the time goes in v1:
time: 96.3 us; the launch traced here: 96.1 us
  Pallas kernels  46.9 us (49%)
  blocking collectives  30 us (31%)
  waiting for transfers between devices  10.4 us (11%)
  starting transfers between devices  4.71 us (5%)
  local copies, waits for them, and re-layouts  3.35 us (3%)
    all_to_all x1, blocking collectives, shards(): lax.all_to_all(send.reshape(devices, MOST * 4, 128), ('gx', 'gy', 'gz'),...  30 us
    pallas_call x1, Pallas kernels, shards(): call(collide_body, [shape((MOST, 3, devices, 128), f32), shape((3, CX, CY...  27.4 us
    pallas_call x1, Pallas kernels, shards(): call(deposit_body, [total_shape, x_face, x_face], scratch_shapes=[pltpu.V...  17.8 us
    ppermute x3, waiting for transfers between devices, both_ways(): lax.ppermute(tail, axis, [(i, (i + 1) % count) for i in range(count)])  7.09 us
    ppermute x3, waiting for transfers between devices, both_ways(): up = lax.ppermute(head, axis, [((i + 1) % count, i) for i in range(count)])  3.27 us
    unnamed x10, local copies, waits for them, and re-layouts  3.21 us
    ppermute x3, starting transfers between devices, both_ways(): lax.ppermute(tail, axis, [(i, (i + 1) % count) for i in range(count)])  2.36 us
    ppermute x3, starting transfers between devices, both_ways(): up = lax.ppermute(head, axis, [((i + 1) % count, i) for i in range(count)])  2.35 us
  transfers between devices with their start and end apart: 6, of which 5 were waited for; matrix products, arithmetic and copies ran while one was open for 0% of the time, Pallas kernels for 1%

profile of v1, /device:TPU:0, one launch (start us, length us, event | category | flops | bytes accessed | tf_op | source)
XLA Modules:
  0.0 96.1 jit_solution(16042828549677540605)
XLA Ops:
  0.6 0.0 copy-start.3
  0.6 0.7 copy-done.3
  1.3 0.0 copy-start.1
  1.3 1.0 %copy-done.1 = f32[256,3,128]{2,0,1:T(8,128)S(1)} copy-done((f32[256,3,128]{2,0,1:T(8,128)S(1)}, f32[256,3,128]{2,0,1:T(8,128)}, u32[]{:S(2)}) %copy-start.1) | copy-done | bytes 393240
  2.3 0.0 copy-start.2
  2.3 0.9 copy-done.2
  3.2 0.6 pack.1
  3.8 0.1 reshape.56
  3.9 30.0 %all_to_all.5 = f32[128,12,128]{2,1,0:T(8,128)S(1)} all-to-all(f32[128,12,128]{2,1,0:T(8,128)S(1)} %reshape.56), channel_id=1, replica_groups=mesh['gx'=8,'gy'=4,'gz'=4] {'gx','gy','gz'}, dimensions={0} | all-to-all | bytes 1572864 | tf_op jit(solution)/shard_map/all_to_all | solution.py:311
  33.9 0.1 reshape.57.slots_ref
  34.0 0.0 copy-start
  34.0 17.8 %deposit.1 = (f32[4,48,128]{2,1,0:T(8,128)S(1)}, f32[4,16,128]{2,1,0:T(8,128)S(1)}, f32[4,16,128]{2,1,0:T(8,128)S(1)}) custom-call(f32[1536,128]{1,0:T(8,128)S(1)} %reshape.57.slots_ref), custom_call_target="tpu_custom_call" | custom-call | tf_op jit(solution)/shard_map/deposit/pallas_call | solution.py:318
  51.8 0.5 collective-permute-start
  52.3 0.0 collective-permute-start.1
  52.3 1.5 %collective-permute-done.up_ref = f32[4,16,128]{2,1,0:T(8,128)S(1)} collective-permute-done((f32[4,16,128]{2,1,0:T(8,128)S(1)}, f32[4,16,128]{2,1,0:T(8,128)S(1)}, u32[]{:S(2)}, u32[]{:S(2)}) %collective-permute-start) | collective-permute-done | bytes 32800 | tf_op jit(solution)/shard_map/ppermute | solution.py:290
  53.9 3.0 %collective-permute-done.1.down_ref = f32[4,16,128]{2,1,0:T(8,128)S(1)} collective-permute-done((f32[4,16,128]{2,1,0:T(8,128)S(1)}, f32[4,16,128]{2,1,0:T(8,128)S(1)}, u32[]{:S(2)}, u32[]{:S(2)}) %collective-permute-start.1) | collective-permute-done | bytes 32800 | tf_op jit(solution)/shard_map/ppermute | solution.py:291
  56.8 0.1 fold_x.1
  56.9 0.7 collective-permute-start.2
  57.6 1.4 %collective-permute-start.3 = (f32[4,8,128]{2,1,0:T(8,128)S(1)}, f32[4,8,128]{2,1,0:T(8,128)S(1)}, u32[]{:S(2)}, u32[]{:S(2)}) collective-permute-start(f32[4,8,128]{2,1,0:T(8,128)S(1)} %get-tuple-element.18), channel_id=1, source_target_pairs={{0,4},{4,8},{8,12},{12,0},{1,5},{5,9},{9,13},{13,1},{2,6},{6,10},{... | collective-permute-start | bytes 49160 | tf_op jit(solution)/shard_map/ppermute | solution.py:291
  59.0 1.7 %collective-permute-done.2.up_ref = f32[4,8,128]{2,1,0:T(8,128)S(1)} collective-permute-done((f32[4,8,128]{2,1,0:T(8,128)S(1)}, f32[4,8,128]{2,1,0:T(8,128)S(1)}, u32[]{:S(2)}, u32[]{:S(2)}) %collective-permute-start.2) | collective-permute-done | bytes 16416 | tf_op jit(solution)/shard_map/ppermute | solution.py:290
  60.7 1.8 %collective-permute-done.3.down_ref = f32[4,8,128]{2,1,0:T(8,128)S(1)} collective-permute-done((f32[4,8,128]{2,1,0:T(8,128)S(1)}, f32[4,8,128]{2,1,0:T(8,128)S(1)}, u32[]{:S(2)}, u32[]{:S(2)}) %collective-permute-start.3) | collective-permute-done | bytes 16416 | tf_op jit(solution)/shard_map/ppermute | solution.py:291
  62.5 0.2 fold_y.1
  62.7 1.2 %collective-permute-start.4 = (f32[8,128]{1,0:T(8,128)S(1)}, f32[8,128]{1,0:T(8,128)S(1)}, u32[]{:S(2)}, u32[]{:S(2)}) collective-permute-start(f32[8,128]{1,0:T(8,128)S(1)} %get-tuple-element.20), channel_id=1, source_target_pairs={{1,0},{2,1},{3,2},{0,3},{5,4},{6,5},{7,6},{4,7},{9,8},{10,9},{11,1... | collective-permute-start | bytes 12296 | tf_op jit(solution)/shard_map/ppermute | solution.py:290
  63.9 0.9 collective-permute-start.5
  64.8 0.0 copy-start.4
  64.8 0.0 copy-done
  64.8 0.6 copy-done.4
  65.4 0.9 axes.1.axes_ref
  66.3 0.0 collective-permute-done.4.up_ref
  66.3 2.3 %collective-permute-done.5.down_ref = f32[8,128]{1,0:T(8,128)S(1)} collective-permute-done((f32[8,128]{1,0:T(8,128)S(1)}, f32[8,128]{1,0:T(8,128)S(1)}, u32[]{:S(2)}, u32[]{:S(2)}) %collective-permute-start.5) | collective-permute-done | bytes 4128 | tf_op jit(solution)/shard_map/ppermute | solution.py:291
  68.7 27.4 %collide.1 = (f32[3,3,128,128]{3,2,1,0:T(8,128)}, f32[3,4,8,128]{3,2,1,0:T(8,128)}) custom-call(f32[4,48,128]{2,1,0:T(8,128)S(1)} %get-tuple-element.19.total_ref, f32[8,128]{1,0:T(8,128)S(1)} %collective-permute-done.4.up_ref, f32[8,128]{1,0:T(8,128)S(1)} %collective-permute-done.5.down_ref, f32[48,128]{1,0:T(8,128)S(1)} %axes.1.axes_ref, ...), custom_call_target="tpu_custom_call" | custom-call | tf_op jit(solution)/shard_map/collide/pallas_call | solution.py:337
  (3 shorter events, 0.1 us)
Async XLA Ops:
  0.6 0.7 copy-start.3
  1.3 1.0 %copy-start.1 = (f32[256,3,128]{2,0,1:T(8,128)S(1)}, f32[256,3,128]{2,0,1:T(8,128)}, u32[]{:S(2)}) copy-start(f32[256,3,128]{2,0,1:T(8,128)} %param.5) | copy-start | bytes 1179652
  2.3 0.9 copy-start.2
  34.0 30.8 %copy-start = (s32[32,32,32]{2,1,0:T(8,128)S(1)}, s32[32,32,32]{2,1,0:T(8,128)}, u32[]{:S(2)}) copy-start(s32[32,32,32]{2,1,0:T(8,128)} %rotation_ref.1) | copy-start | bytes 393220
  51.8 2.1 %collective-permute-start = (f32[4,16,128]{2,1,0:T(8,128)S(1)}, f32[4,16,128]{2,1,0:T(8,128)S(1)}, u32[]{:S(2)}, u32[]{:S(2)}) collective-permute-start(f32[4,16,128]{2,1,0:T(8,128)S(1)} %get-tuple-element.14), channel_id=1, source_target_pairs={{16,0},{32,16},{48,32},{64,48},{80,64},{96,80},{112,96},{0,112},{1... | collective-permute-start | bytes 98312 | tf_op jit(solution)/shard_map/ppermute | solution.py:290
  52.3 4.6 %collective-permute-start.1 = (f32[4,16,128]{2,1,0:T(8,128)S(1)}, f32[4,16,128]{2,1,0:T(8,128)S(1)}, u32[]{:S(2)}, u32[]{:S(2)}) collective-permute-start(f32[4,16,128]{2,1,0:T(8,128)S(1)} %get-tuple-element.15), channel_id=1, source_target_pairs={{0,16},{16,32},{32,48},{48,64},{64,80},{80,96},{96,112},{112,0},{1... | collective-permute-start | bytes 98312 | tf_op jit(solution)/shard_map/ppermute | solution.py:291
  56.9 3.8 %collective-permute-start.2 = (f32[4,8,128]{2,1,0:T(8,128)S(1)}, f32[4,8,128]{2,1,0:T(8,128)S(1)}, u32[]{:S(2)}, u32[]{:S(2)}) collective-permute-start(f32[4,8,128]{2,1,0:T(8,128)S(1)} %get-tuple-element.17), channel_id=1, source_target_pairs={{4,0},{8,4},{12,8},{0,12},{5,1},{9,5},{13,9},{1,13},{6,2},{10,6},{... | collective-permute-start | bytes 49160 | tf_op jit(solution)/shard_map/ppermute | solution.py:290
  57.6 4.9 %collective-permute-start.3 = (f32[4,8,128]{2,1,0:T(8,128)S(1)}, f32[4,8,128]{2,1,0:T(8,128)S(1)}, u32[]{:S(2)}, u32[]{:S(2)}) collective-permute-start(f32[4,8,128]{2,1,0:T(8,128)S(1)} %get-tuple-element.18), channel_id=1, source_target_pairs={{0,4},{4,8},{8,12},{12,0},{1,5},{5,9},{9,13},{13,1},{2,6},{6,10},{... | collective-permute-start | bytes 49160 | tf_op jit(solution)/shard_map/ppermute | solution.py:291
  62.7 3.7 %collective-permute-start.4 = (f32[8,128]{1,0:T(8,128)S(1)}, f32[8,128]{1,0:T(8,128)S(1)}, u32[]{:S(2)}, u32[]{:S(2)}) collective-permute-start(f32[8,128]{1,0:T(8,128)S(1)} %get-tuple-element.20), channel_id=1, source_target_pairs={{1,0},{2,1},{3,2},{0,3},{5,4},{6,5},{7,6},{4,7},{9,8},{10,9},{11,1... | collective-permute-start | bytes 12296 | tf_op jit(solution)/shard_map/ppermute | solution.py:290
  63.9 4.8 %collective-permute-start.5 = (f32[8,128]{1,0:T(8,128)S(1)}, f32[8,128]{1,0:T(8,128)S(1)}, u32[]{:S(2)}, u32[]{:S(2)}) collective-permute-start(f32[8,128]{1,0:T(8,128)S(1)} %get-tuple-element.21), channel_id=1, source_target_pairs={{0,1},{1,2},{2,3},{3,0},{4,5},{5,6},{6,7},{7,4},{8,9},{9,10},{10,1... | collective-permute-start | bytes 12296 | tf_op jit(solution)/shard_map/ppermute | solution.py:291
  64.8 0.7 copy-start.4

commit v2 on v1

--- a/solution.py
+++ b/solution.py
@@ -111,60 +111,69 @@
     tail_ref[c, PY : PY + 1] = total[PLANES:ROWS]
 
 
-SLOTS_STEP = 8
+STEP = 96
+Q2 = ROWS // 2
+
+
+def slot_places(slots_ref, rows_q, rows_l):
+    slots = slots_ref.shape[0] // 4
+    label = slots_ref[pl.ds(3, slots, stride=4), :].astype(i32)
+    rows_q[...] = (label >> 8).astype(f32)
+    rows_l[...] = (label & 255).astype(f32)
+
+
+def lane_onehot(rows_l, slot):
+    step = iota((16, 128), 0).astype(f32).astype(bf16)
+    lane = jnp.broadcast_to(rows_l[pl.ds(slot, 1), :], (16, 128)).astype(bf16) - step
+    one = jnp.ones((16, 128), bf16)
+    zero = jnp.zeros((16, 128), bf16)
+    return jnp.concatenate([jnp.where(lane == float(16 * j), one, zero) for j in range(16)], axis=0)
 
 
 def deposit_body(slots_ref, total_ref, head_ref, tail_ref, acc, rows_q, rows_l):
     slots = slots_ref.shape[0] // 4
-    label = slots_ref[pl.ds(3, slots, stride=4), :].astype(i32)
-    rows_q[...] = (label >> 7).astype(f32)
-    rows_l[...] = (label & 127).astype(f32)
+    slot_places(slots_ref, rows_q, rows_l)
     acc[...] = jnp.zeros(acc.shape, f32)
     sub8 = iota((8, 128), 0)
-    sub16 = iota((16, 128), 0)
-    half = jnp.where(sub16 >= 8, 1.0, 0.0).astype(bf16)
-    step16 = sub16.astype(f32).astype(bf16)
-    one = jnp.ones((16, 128), bf16)
+    half = jnp.where(iota((16, 128), 0) >= 8, 1.0, 0.0).astype(bf16)
     zero = jnp.zeros((16, 128), bf16)
 
     def step(i, carry):
         weighted, depths = [], []
-        for k in range(SLOTS_STEP):
-            slot = i * SLOTS_STEP + k
-            own = slots_ref[pl.ds(pl.multiple_of(i * SLOTS_STEP * 4, 8) + 4 * k, 4), :]
+        for k in range(STEP):
+            slot = i * STEP + k
+            own = slots_ref[pl.ds(pl.multiple_of(i * STEP * 4, 8) + 4 * k, 4), :]
             own = jnp.concatenate([own, own], axis=0)
             high = own.astype(bf16).astype(f32)
             value = jnp.where(sub8 < 4, high, own - high)
             value = jnp.where(sub8 == 3, 1.0, jnp.where(sub8 == 7, 0.0, value))
             value = jnp.concatenate([value, value], axis=0).astype(bf16)
             q = jnp.broadcast_to(rows_q[pl.ds(slot, 1), :], (16, 128)).astype(bf16) - half
-            l = jnp.broadcast_to(rows_l[pl.ds(slot, 1), :], (16, 128)).astype(bf16) - step16
             weighted.append(
                 jnp.concatenate(
-                    [jnp.where(q == float(2 * j), value, zero) for j in range(ROWS // 2)], axis=0
+                    [jnp.where(q == float(2 * j), value, zero) for j in range(12)], axis=0
                 )
             )
-            depths.append(
-                jnp.concatenate(
-                    [jnp.where(l == float(16 * j), one, zero) for j in range(8)], axis=0
-                )
-            )
-        acc[...] += lax.dot_general(
+            depths.append(lane_onehot(rows_l, slot))
+        got = lax.dot_general(
             jnp.concatenate(weighted, axis=1),
             jnp.concatenate(depths, axis=1),
             (((1,), (1,)), ((), ())),
             preferred_element_type=f32,
         )
+        acc[0] += got[:, :128]
+        acc[1] += got[:, 128:]
         return carry
 
-    lax.fori_loop(0, slots // SLOTS_STEP, step, 0)
+    lax.fori_loop(0, slots // STEP, step, 0)
     for c in range(4):
-        total = acc[pl.ds(c, ROWS, stride=8), :]
-        if c < 3:
-            total = total + acc[pl.ds(c + 4, ROWS, stride=8), :]
-        total_ref[c, 0:ROWS] = total
+        for odd in range(2):
+            total = acc[odd, pl.ds(c, Q2, stride=8), :]
+            if c < 3:
+                total = total + acc[odd, pl.ds(c + 4, Q2, stride=8), :]
+            total_ref[c, pl.ds(odd, Q2, stride=2)] = total
         total_ref[c, ROWS:PADROWS] = jnp.zeros((PADROWS - ROWS, 128), f32)
-        gather_x_faces(total, c, head_ref, tail_ref)
+        gather_x_faces(total_ref[c], c, head_ref, tail_ref)
 
 
 def moved_lanes(row, first, count, shift):
@@ -219,8 +228,10 @@
 
 
 def collide_body(
-    total_ref, up_ref, down_ref, axes_ref, units_ref, slots_ref, out_ref, flow_ref, cells
+    total_ref, up_ref, down_ref, axes_ref, units_ref, slots_ref, out_ref, flow_ref,
+    cells, wide, found, rows_q, rows_l,
 ):
+    slots = slots_ref.shape[0] // 4
     shape = (PADROWS, 128)
     row = iota(shape, 0)
     lane = iota(shape, 1)
@@ -236,43 +247,60 @@
         own = own + jnp.where(lane == 0, column, 0.0)
         totals.append(own + jnp.where(top, up_ref[c : c + 1], 0.0))
     count = jnp.maximum(totals[3], 1.0)
+    wide[...] = jnp.zeros(wide.shape, f32)
+
+    def tabulate(value, line):
+        cells[...] = value
+        for odd in range(2):
+            wide[odd, pl.ds(line, Q2, stride=8), :] = cells[pl.ds(odd, Q2, stride=2)]
+
     for c in range(3):
         mean = totals[c] / count
-        cells[c] = mean
         for ex in range(CX):
             flow_ref[c, ex] = mean[ex * PY : ex * PY + CY]
-    cells[3] = axes_ref[...]
+        high = mean.astype(bf16).astype(f32)
+        tabulate(high, c)
+        tabulate(mean - high, c + 4)
+    tabulate(axes_ref[...], 3)
+    table = jnp.concatenate([wide[0], wide[1]], axis=1).astype(bf16)
+    slot_places(slots_ref, rows_q, rows_l)
+    sub8 = iota((8, 128), 0)
+
+    def look(i, carry):
+        for k in range(STEP // 2):
+            pair = [i * STEP + 2 * k, i * STEP + 2 * k + 1]
+            hot = jnp.concatenate([lane_onehot(rows_l, slot) for slot in pair], axis=1)
+            read = jnp.dot(table, hot, preferred_element_type=f32)
+            got = []
+            for h in range(2):
+                q = jnp.broadcast_to(rows_q[pl.ds(pair[h], 1), :], (8, 128))
+                value = jnp.zeros((8, 128), f32)
+                for j in range(Q2):
+                    own = read[8 * j : 8 * j + 8, 128 * h : 128 * h + 128]
+                    value = jnp.where(q == float(j), own, value)
+                got.append(value + pltpu.roll(value, 4, 0))
+            place = pl.multiple_of((i * STEP + 2 * k) * 4, 8)
+            found[pl.ds(place, 8), :] = jnp.where(sub8 < 4, got[0], got[1])
+        return carry
+
+    lax.fori_loop(0, slots // STEP, look, 0)
     units = [jnp.broadcast_to(units_ref[c : c + 1], (8, 128)) for c in range(3)]
 
-    def step(i, carry):
-        places = []
+    def turn(i, carry):
+        rank = i // (16 // GROUP)
         for k in range(GROUP):
-            first = pl.multiple_of((i % (16 // GROUP)) * (8 * GROUP * 12), 8 * GROUP * 12)
-            first = first + (i // (16 // GROUP)) * 4 + k * 8 * 12
-            places.append(first)
-        labels = [slots_ref[pl.ds(p + 3, 8, stride=12), :].astype(i32) for p in places]
-        rows = [label >> 7 for label in labels]
-        lanes = [label & 127 for label in labels]
-        found = [[jnp.zeros((8, 128), f32) for c in range(4)] for k in range(GROUP)]
-        for q in range(ROWS):
-            for c in range(4):
-                table = jnp.broadcast_to(cells[c, q : q + 1], (8, 128))
-                for k in range(GROUP):
-                    read = jnp.take_along_axis(table, lanes[k], axis=1)
-                    found[k][c] = jnp.where(rows[k] == q, read, found[k][c])
-        for k in range(GROUP):
-            which = found[k][3].astype(i32)
+            source = pl.multiple_of((i % (16 // GROUP)) * (8 * GROUP) + 8 * k, 8)
+            place = source * 12 + rank * 4
+            which = found[pl.ds(place + 3, 8, stride=12), :].astype(i32)
             n = [jnp.take_along_axis(units[c], which, axis=1) for c in range(3)]
-            u = found[k][:3]
-            w = [slots_ref[pl.ds(places[k] + c, 8, stride=12), :] - u[c] for c in range(3)]
+            u = [found[pl.ds(place + c, 8, stride=12), :] for c in range(3)]
+            w = [slots_ref[pl.ds(place + c, 8, stride=12), :] - u[c] for c in range(3)]
             inner = n[0] * w[0] + n[1] * w[1] + n[2] * w[2]
             crossed = [
                 n[1] * w[2] - n[2] * w[1],
                 n[2] * w[0] - n[0] * w[2],
                 n[0] * w[1] - n[1] * w[0],
             ]
-            rank = i // (16 // GROUP)
-            source = pl.multiple_of((i % (16 // GROUP)) * (8 * GROUP) + 8 * k, 8)
             for c in range(3):
                 out_ref[rank, c, pl.ds(source, 8), :] = (
                     u[c]
@@ -282,7 +310,7 @@
                 )
         return carry
 
-    lax.fori_loop(0, MOST * 16 // GROUP, step, 0)
+    lax.fori_loop(0, MOST * 16 // GROUP, turn, 0)
 
 
 def both_ways(head, tail, axis):
@@ -309,7 +337,7 @@
     )(grid_shift, rotation_axis)
     units = jnp.pad(axis_table(), ((0, 5), (0, 128 - NAX)))
     slots = lax.all_to_all(
-        send.reshape(devices, MOST * 4, 128), ("gx", "gy", "gz"), split_axis=0, concat_axis=0, tiled=True
+        send.reshape(devices, MOST, 4, 128), ("gx", "gy", "gz"), split_axis=0, concat_axis=0, tiled=True
     ).reshape(devices * MOST * 4, 128)
     total_shape = shape((4, PADROWS, 128), f32)
     x_face = shape((4, 16, 128), f32)
@@ -319,7 +347,7 @@
         deposit_body,
         [total_shape, x_face, x_face],
         scratch_shapes=[
-            pltpu.VMEM((ROWS * 8, 128), f32),
+            pltpu.VMEM((2, 192, 128), f32),
             pltpu.VMEM((devices * MOST, 128), f32),
             pltpu.VMEM((devices * MOST, 128), f32),
         ],
@@ -337,7 +365,13 @@
     updated, cell_flow = call(
         collide_body,
         [shape((MOST, 3, devices, 128), f32), shape((3, CX, CY, CZ), f32)],
-        scratch_shapes=[pltpu.VMEM((4, PADROWS, 128), f32)],
+        scratch_shapes=[
+            pltpu.VMEM((PADROWS, 128), f32),
+            pltpu.VMEM((2, Q2 * 8, 128), f32),
+            pltpu.VMEM((devices * MOST * 4, 128), f32),
+            pltpu.VMEM((devices * MOST, 128), f32),
+            pltpu.VMEM((devices * MOST, 128), f32),
+        ],
         name="collide",
     )(total, up, down, axes, units, slots)
     return jnp.transpose(updated, (2, 0, 1, 3))[None], cell_flow

time: 96.3 us -> 64.9 us (0.67)
  Pallas kernels: 46.9 us -> 18.5 us
  blocking collectives: 30 us -> 27.3 us
    pallas_call x1, Pallas kernels: 27.4 us -> 7.91 us  [shards(): call(collide_body, [shape((MOST, 3, devices, 128), f32), shape((3, CX, CY...]
    pallas_call x1, Pallas kernels: 17.8 us -> 8.84 us  [shards(): call(deposit_body, [total_shape, x_face, x_face], scratch_shapes=[pltpu.V...]
    all_to_all x1, blocking collectives: 30 us -> 27.3 us  [shards(): lax.all_to_all(send.reshape(devices, MOST, 4, 128), ('gx', 'gy', 'gz'), s...]
where the time goes in v2:
time: 64.9 us; the launch traced here: 64.7 us
  blocking collectives  27.3 us (42%)
  Pallas kernels  18.5 us (29%)
  waiting for transfers between devices  10.2 us (16%)
  starting transfers between devices  4.78 us (7%)
  local copies, waits for them, and re-layouts  3.21 us (5%)
  between operations  0.68 us (1%)
    all_to_all x1, blocking collectives, shards(): lax.all_to_all(send.reshape(devices, MOST, 4, 128), ('gx', 'gy', 'gz'), s...  27.3 us
    pallas_call x1, Pallas kernels, shards(): call(deposit_body, [total_shape, x_face, x_face], scratch_shapes=[pltpu.V...  8.84 us
    pallas_call x1, Pallas kernels, shards(): call(collide_body, [shape((MOST, 3, devices, 128), f32), shape((3, CX, CY...  7.91 us
    ppermute x3, waiting for transfers between devices, both_ways(): lax.ppermute(tail, axis, [(i, (i + 1) % count) for i in range(count)])  6.89 us
    ppermute x3, waiting for transfers between devices, both_ways(): up = lax.ppermute(head, axis, [((i + 1) % count, i) for i in range(count)])  3.3 us
    unnamed x10, local copies, waits for them, and re-layouts  3.21 us
    ppermute x3, starting transfers between devices, both_ways(): lax.ppermute(tail, axis, [(i, (i + 1) % count) for i in range(count)])  2.54 us
    ppermute x3, starting transfers between devices, both_ways(): up = lax.ppermute(head, axis, [((i + 1) % count, i) for i in range(count)])  2.24 us
  transfers between devices with their start and end apart: 6, of which 5 were waited for; matrix products, arithmetic and copies ran while one was open for 0% of the time, Pallas kernels for 1%

profile of v2, /device:TPU:0, one launch (start us, length us, event | category | flops | bytes accessed | tf_op | source)
XLA Modules:
  0.0 64.7 jit_solution(18324812814345628420)
XLA Ops:
  0.6 0.0 copy-start.3
  0.6 0.7 %copy-done.3 = s32[256,1]{0,1:T(1,128)S(1)} copy-done((s32[256,1]{0,1:T(1,128)S(1)}, s32[256,1]{0,1:T(1,128)}, u32[]{:S(2)}) %copy-start.3) | copy-done | bytes 1048
  1.3 0.0 copy-start.1
  1.3 1.0 %copy-done.1 = f32[256,3,128]{2,0,1:T(8,128)S(1)} copy-done((f32[256,3,128]{2,0,1:T(8,128)S(1)}, f32[256,3,128]{2,0,1:T(8,128)}, u32[]{:S(2)}) %copy-start.1) | copy-done | bytes 393240
  2.3 0.0 copy-start.2
  2.3 0.9 %copy-done.2 = s32[256,128]{1,0:T(8,128)S(1)} copy-done((s32[256,128]{1,0:T(8,128)S(1)}, s32[256,128]{1,0:T(8,128)}, u32[]{:S(2)}) %copy-start.2) | copy-done | bytes 131096
  3.2 0.6 pack.1
  3.8 27.3 %all_to_all.5 = f32[128,3,4,128]{3,2,1,0:T(4,128)S(1)} all-to-all(f32[128,3,4,128]{3,2,1,0:T(4,128)S(1)} %bitcast.9), channel_id=1, replica_groups=mesh['gx'=8,'gy'=4,'gz'=4] {'gx','gy','gz'}, dimensions={0} | all-to-all | bytes 1572864 | tf_op jit(solution)/shard_map/all_to_all | solution.py:339
  31.2 0.0 copy-start
  31.2 8.8 %deposit.1 = (f32[4,48,128]{2,1,0:T(8,128)S(1)}, f32[4,16,128]{2,1,0:T(8,128)S(1)}, f32[4,16,128]{2,1,0:T(8,128)S(1)}) custom-call(f32[1536,128]{1,0:T(8,128)S(1)} %bitcast.7), custom_call_target="tpu_custom_call" | custom-call | tf_op jit(solution)/shard_map/deposit/pallas_call | solution.py:346
  40.0 0.6 collective-permute-start
  40.6 0.0 collective-permute-start.1
  40.6 1.5 %collective-permute-done.up_ref = f32[4,16,128]{2,1,0:T(8,128)S(1)} collective-permute-done((f32[4,16,128]{2,1,0:T(8,128)S(1)}, f32[4,16,128]{2,1,0:T(8,128)S(1)}, u32[]{:S(2)}, u32[]{:S(2)}) %collective-permute-start) | collective-permute-done | bytes 32800 | tf_op jit(solution)/shard_map/ppermute | solution.py:318
  42.2 3.0 %collective-permute-done.1.down_ref = f32[4,16,128]{2,1,0:T(8,128)S(1)} collective-permute-done((f32[4,16,128]{2,1,0:T(8,128)S(1)}, f32[4,16,128]{2,1,0:T(8,128)S(1)}, u32[]{:S(2)}, u32[]{:S(2)}) %collective-permute-start.1) | collective-permute-done | bytes 32800 | tf_op jit(solution)/shard_map/ppermute | solution.py:319
  45.1 0.1 fold_x.1
  45.2 0.7 %collective-permute-start.2 = (f32[4,8,128]{2,1,0:T(8,128)S(1)}, f32[4,8,128]{2,1,0:T(8,128)S(1)}, u32[]{:S(2)}, u32[]{:S(2)}) collective-permute-start(f32[4,8,128]{2,1,0:T(8,128)S(1)} %get-tuple-element.17), channel_id=1, source_target_pairs={{4,0},{8,4},{12,8},{0,12},{5,1},{9,5},{13,9},{1,13},{6,2},{10,6},{... | collective-permute-start | bytes 49160 | tf_op jit(solution)/shard_map/ppermute | solution.py:318
  45.9 1.4 %collective-permute-start.3 = (f32[4,8,128]{2,1,0:T(8,128)S(1)}, f32[4,8,128]{2,1,0:T(8,128)S(1)}, u32[]{:S(2)}, u32[]{:S(2)}) collective-permute-start(f32[4,8,128]{2,1,0:T(8,128)S(1)} %get-tuple-element.18), channel_id=1, source_target_pairs={{0,4},{4,8},{8,12},{12,0},{1,5},{5,9},{9,13},{13,1},{2,6},{6,10},{... | collective-permute-start | bytes 49160 | tf_op jit(solution)/shard_map/ppermute | solution.py:319
  47.3 1.7 %collective-permute-done.2.up_ref = f32[4,8,128]{2,1,0:T(8,128)S(1)} collective-permute-done((f32[4,8,128]{2,1,0:T(8,128)S(1)}, f32[4,8,128]{2,1,0:T(8,128)S(1)}, u32[]{:S(2)}, u32[]{:S(2)}) %collective-permute-start.2) | collective-permute-done | bytes 16416 | tf_op jit(solution)/shard_map/ppermute | solution.py:318
  49.0 1.8 %collective-permute-done.3.down_ref = f32[4,8,128]{2,1,0:T(8,128)S(1)} collective-permute-done((f32[4,8,128]{2,1,0:T(8,128)S(1)}, f32[4,8,128]{2,1,0:T(8,128)S(1)}, u32[]{:S(2)}, u32[]{:S(2)}) %collective-permute-start.3) | collective-permute-done | bytes 16416 | tf_op jit(solution)/shard_map/ppermute | solution.py:319
  50.8 0.2 fold_y.1
  51.0 1.0 %collective-permute-start.4 = (f32[8,128]{1,0:T(8,128)S(1)}, f32[8,128]{1,0:T(8,128)S(1)}, u32[]{:S(2)}, u32[]{:S(2)}) collective-permute-start(f32[8,128]{1,0:T(8,128)S(1)} %get-tuple-element.20), channel_id=1, source_target_pairs={{1,0},{2,1},{3,2},{0,3},{5,4},{6,5},{7,6},{4,7},{9,8},{10,9},{11,1... | collective-permute-start | bytes 12296 | tf_op jit(solution)/shard_map/ppermute | solution.py:318
  52.0 1.1 %collective-permute-start.5 = (f32[8,128]{1,0:T(8,128)S(1)}, f32[8,128]{1,0:T(8,128)S(1)}, u32[]{:S(2)}, u32[]{:S(2)}) collective-permute-start(f32[8,128]{1,0:T(8,128)S(1)} %get-tuple-element.21), channel_id=1, source_target_pairs={{0,1},{1,2},{2,3},{3,0},{4,5},{5,6},{6,7},{7,4},{8,9},{9,10},{10,1... | collective-permute-start | bytes 12296 | tf_op jit(solution)/shard_map/ppermute | solution.py:319
  53.1 0.0 copy-start.4
  53.1 0.0 copy-done
  53.1 0.6 copy-done.4
  53.7 0.9 %axes.1.axes_ref = f32[48,128]{1,0:T(8,128)S(1)} custom-call(s32[3]{0:T(128)S(1)} %copy-done.4, s32[32,32,32]{2,1,0:T(8,128)S(1)} %copy-done), custom_call_target="tpu_custom_call" | custom-call | tf_op jit(solution)/shard_map/axes/pallas_call | solution.py:331
  54.6 0.0 collective-permute-done.4.up_ref
  54.7 2.1 %collective-permute-done.5.down_ref = f32[8,128]{1,0:T(8,128)S(1)} collective-permute-done((f32[8,128]{1,0:T(8,128)S(1)}, f32[8,128]{1,0:T(8,128)S(1)}, u32[]{:S(2)}, u32[]{:S(2)}) %collective-permute-start.5) | collective-permute-done | bytes 4128 | tf_op jit(solution)/shard_map/ppermute | solution.py:319
  56.8 7.9 %collide.1 = (f32[3,3,128,128]{3,2,1,0:T(8,128)}, f32[3,4,8,128]{3,2,1,0:T(8,128)}) custom-call(f32[4,48,128]{2,1,0:T(8,128)S(1)} %get-tuple-element.19.total_ref, f32[8,128]{1,0:T(8,128)S(1)} %collective-permute-done.4.up_ref, f32[8,128]{1,0:T(8,128)S(1)} %collective-permute-done.5.down_ref, f32[48,128]{1,0:T(8,128)S(1)} %axes.1.axes_ref, ...), custom_call_target="tpu_custom_call" | custom-call | tf_op jit(solution)/shard_map/collide/pallas_call | solution.py:365
  (3 shorter events, 0.1 us)
Async XLA Ops:
  0.6 0.7 %copy-start.3 = (s32[256,1]{0,1:T(1,128)S(1)}, s32[256,1]{0,1:T(1,128)}, u32[]{:S(2)}) copy-start(s32[256,1]{0,1:T(1,128)} %param.7) | copy-start | bytes 3076
  1.3 1.0 %copy-start.1 = (f32[256,3,128]{2,0,1:T(8,128)S(1)}, f32[256,3,128]{2,0,1:T(8,128)}, u32[]{:S(2)}) copy-start(f32[256,3,128]{2,0,1:T(8,128)} %param.5) | copy-start | bytes 1179652
  2.3 0.9 %copy-start.2 = (s32[256,128]{1,0:T(8,128)S(1)}, s32[256,128]{1,0:T(8,128)}, u32[]{:S(2)}) copy-start(s32[256,128]{1,0:T(8,128)} %index_ref.1) | copy-start | bytes 393220
  31.2 21.9 %copy-start = (s32[32,32,32]{2,1,0:T(8,128)S(1)}, s32[32,32,32]{2,1,0:T(8,128)}, u32[]{:S(2)}) copy-start(s32[32,32,32]{2,1,0:T(8,128)} %rotation_ref.1) | copy-start | bytes 393220
  40.0 2.2 %collective-permute-start = (f32[4,16,128]{2,1,0:T(8,128)S(1)}, f32[4,16,128]{2,1,0:T(8,128)S(1)}, u32[]{:S(2)}, u32[]{:S(2)}) collective-permute-start(f32[4,16,128]{2,1,0:T(8,128)S(1)} %get-tuple-element.14), channel_id=1, source_target_pairs={{16,0},{32,16},{48,32},{64,48},{80,64},{96,80},{112,96},{0,112},{1... | collective-permute-start | bytes 98312 | tf_op jit(solution)/shard_map/ppermute | solution.py:318
  40.6 4.6 %collective-permute-start.1 = (f32[4,16,128]{2,1,0:T(8,128)S(1)}, f32[4,16,128]{2,1,0:T(8,128)S(1)}, u32[]{:S(2)}, u32[]{:S(2)}) collective-permute-start(f32[4,16,128]{2,1,0:T(8,128)S(1)} %get-tuple-element.15), channel_id=1, source_target_pairs={{0,16},{16,32},{32,48},{48,64},{64,80},{80,96},{96,112},{112,0},{1... | collective-permute-start | bytes 98312 | tf_op jit(solution)/shard_map/ppermute | solution.py:319
  45.2 3.8 %collective-permute-start.2 = (f32[4,8,128]{2,1,0:T(8,128)S(1)}, f32[4,8,128]{2,1,0:T(8,128)S(1)}, u32[]{:S(2)}, u32[]{:S(2)}) collective-permute-start(f32[4,8,128]{2,1,0:T(8,128)S(1)} %get-tuple-element.17), channel_id=1, source_target_pairs={{4,0},{8,4},{12,8},{0,12},{5,1},{9,5},{13,9},{1,13},{6,2},{10,6},{... | collective-permute-start | bytes 49160 | tf_op jit(solution)/shard_map/ppermute | solution.py:318
  45.9 4.9 %collective-permute-start.3 = (f32[4,8,128]{2,1,0:T(8,128)S(1)}, f32[4,8,128]{2,1,0:T(8,128)S(1)}, u32[]{:S(2)}, u32[]{:S(2)}) collective-permute-start(f32[4,8,128]{2,1,0:T(8,128)S(1)} %get-tuple-element.18), channel_id=1, source_target_pairs={{0,4},{4,8},{8,12},{12,0},{1,5},{5,9},{9,13},{13,1},{2,6},{6,10},{... | collective-permute-start | bytes 49160 | tf_op jit(solution)/shard_map/ppermute | solution.py:319
  51.0 3.7 %collective-permute-start.4 = (f32[8,128]{1,0:T(8,128)S(1)}, f32[8,128]{1,0:T(8,128)S(1)}, u32[]{:S(2)}, u32[]{:S(2)}) collective-permute-start(f32[8,128]{1,0:T(8,128)S(1)} %get-tuple-element.20), channel_id=1, source_target_pairs={{1,0},{2,1},{3,2},{0,3},{5,4},{6,5},{7,6},{4,7},{9,8},{10,9},{11,1... | collective-permute-start | bytes 12296 | tf_op jit(solution)/shard_map/ppermute | solution.py:318
  52.0 4.8 %collective-permute-start.5 = (f32[8,128]{1,0:T(8,128)S(1)}, f32[8,128]{1,0:T(8,128)S(1)}, u32[]{:S(2)}, u32[]{:S(2)}) collective-permute-start(f32[8,128]{1,0:T(8,128)S(1)} %get-tuple-element.21), channel_id=1, source_target_pairs={{0,1},{1,2},{2,3},{3,0},{4,5},{5,6},{6,7},{7,4},{8,9},{9,10},{10,1... | collective-permute-start | bytes 12296 | tf_op jit(solution)/shard_map/ppermute | solution.py:319
  53.1 0.7 %copy-start.4 = (s32[3]{0:T(128)S(1)}, s32[3]{0:T(128)}, u32[]{:S(2)}) copy-start(s32[3]{0:T(128)} %shift_ref.1) | copy-start | bytes 40

commit v3 on v2

--- a/solution.py
+++ b/solution.py
@@ -56,24 +56,37 @@
     )
 
 
-def pack_body(target_ref, velocity_ref, index_ref, out_ref):
+def pack_body(target_hbm, velocity_hbm, index_hbm, out_ref, target_ref, velocity_ref, index_ref, sems):
+    sources = (target_hbm, index_hbm, velocity_hbm)
+    sinks = (target_ref, index_ref, velocity_ref)
+    copies = [
+        pltpu.make_async_copy(source, sink, sems.at[k])
+        for k, (source, sink) in enumerate(zip(sources, sinks))
+    ]
+    for copy in copies:
+        copy.start()
     bricks = 128
     blocks = target_ref.shape[1]
+    copies[0].wait()
     target = jnp.broadcast_to(target_ref[...], (bricks, blocks))
     onehot = target == iota((bricks, blocks), 0)
     onehot_bf = jnp.where(onehot, 1.0, 0.0).astype(bf16)
     earlier = jnp.where(iota((blocks, blocks), 0) < iota((blocks, blocks), 1), 1.0, 0.0)
     before = jnp.dot(onehot_bf, earlier.astype(bf16), preferred_element_type=f32)
+    places = [
+        jnp.where(onehot & (before == float(rank)), 1.0, 0.0).astype(bf16) for rank in range(MOST)
+    ]
+    copies[1].wait()
     index = index_ref[...]
     plane = (index * 8129) >> 20
     depth = index - plane * (CZ + 1)
     top = depth == CZ
     label = jnp.where(top, PLANES * 128 + plane, plane * 128 + depth)
-    parts = [velocity_ref[c] for c in range(3)] + [label.astype(f32) - EMPTY]
-    splits = split3(jnp.concatenate(parts, axis=1))
+    label = label.astype(f32) - EMPTY
+    copies[2].wait()
+    splits = split3(jnp.concatenate([velocity_ref[c] for c in range(3)] + [label], axis=1))
     for rank in range(MOST):
-        place = jnp.where(onehot & (before == float(rank)), 1.0, 0.0).astype(bf16)
-        moved = sum(jnp.dot(place, s, preferred_element_type=f32) for s in reversed(splits))
+        moved = sum(jnp.dot(places[rank], s, preferred_element_type=f32) for s in reversed(splits))
         for c in range(4):
             value = moved[:, c * 128 : (c + 1) * 128]
             if c == 3:
@@ -111,6 +124,7 @@
     tail_ref[c, PY : PY + 1] = total[PLANES:ROWS]
 
 
+DEPOSIT_STEP = 128
 STEP = 96
 Q2 = ROWS // 2
 
@@ -118,8 +132,8 @@
 def slot_places(slots_ref, rows_q, rows_l):
     slots = slots_ref.shape[0] // 4
     label = slots_ref[pl.ds(3, slots, stride=4), :].astype(i32)
-    rows_q[...] = (label >> 8).astype(f32)
-    rows_l[...] = (label & 255).astype(f32)
+    rows_q[...] = (label >> 8).astype(rows_q.dtype)
+    rows_l[...] = jnp.where(label >= PADROWS * 128, 512, label & 255).astype(f32)
 
 
 def lane_onehot(rows_l, slot):
@@ -140,9 +154,9 @@
 
     def step(i, carry):
         weighted, depths = [], []
-        for k in range(STEP):
-            slot = i * STEP + k
-            own = slots_ref[pl.ds(pl.multiple_of(i * STEP * 4, 8) + 4 * k, 4), :]
+        for k in range(DEPOSIT_STEP):
+            slot = i * DEPOSIT_STEP + k
+            own = slots_ref[pl.ds(pl.multiple_of(i * DEPOSIT_STEP * 4, 8) + 4 * k, 4), :]
             own = jnp.concatenate([own, own], axis=0)
             high = own.astype(bf16).astype(f32)
             value = jnp.where(sub8 < 4, high, own - high)
@@ -154,7 +168,7 @@
                     [jnp.where(q == float(2 * j), value, zero) for j in range(12)], axis=0
                 )
             )
-            depths.append(lane_onehot(rows_l, slot))
+            depths.append(lane_onehot(rows_l, slot).astype(jnp.float8_e4m3fn))
         got = lax.dot_general(
             jnp.concatenate(weighted, axis=1),
             jnp.concatenate(depths, axis=1),
@@ -165,7 +179,7 @@
         acc[1] += got[:, 128:]
         return carry
 
-    lax.fori_loop(0, slots // STEP, step, 0)
+    lax.fori_loop(0, slots // DEPOSIT_STEP, step, 0)
     for c in range(4):
         for odd in range(2):
             total = acc[odd, pl.ds(c, Q2, stride=8), :]
@@ -224,12 +238,18 @@
         tail_ref[4 + c : 5 + c] = jnp.zeros((1, 128), f32)
 
 
-GROUP = 4
+def select_row(rows, bits):
+    for bit in bits:
+        rows = [
+            jnp.where(bit, rows[j + 1], rows[j]) if j + 1 < len(rows) else rows[j]
+            for j in range(0, len(rows), 2)
+        ]
+    return rows[0]
 
 
 def collide_body(
-    total_ref, up_ref, down_ref, axes_ref, units_ref, slots_ref, out_ref, flow_ref,
-    cells, wide, found, rows_q, rows_l,
+    total_ref, up_ref, down_ref, axes_ref, units_ref, slots_ref, out_hbm, flow_ref,
+    cells, wide, found, rows_q, rows_l, out_ref, sems,
 ):
     slots = slots_ref.shape[0] // 4
     shape = (PADROWS, 128)
@@ -266,7 +286,9 @@
     slot_places(slots_ref, rows_q, rows_l)
     sub8 = iota((8, 128), 0)
 
-    def look(i, carry):
+    units = [jnp.broadcast_to(units_ref[c : c + 1], (8, 128)) for c in range(3)]
+
+    def look(i):
         for k in range(STEP // 2):
             pair = [i * STEP + 2 * k, i * STEP + 2 * k + 1]
             hot = jnp.concatenate([lane_onehot(rows_l, slot) for slot in pair], axis=1)
@@ -274,43 +296,52 @@
             got = []
             for h in range(2):
                 q = jnp.broadcast_to(rows_q[pl.ds(pair[h], 1), :], (8, 128))
-                value = jnp.zeros((8, 128), f32)
-                for j in range(Q2):
-                    own = read[8 * j : 8 * j + 8, 128 * h : 128 * h + 128]
-                    value = jnp.where(q == float(j), own, value)
+                bits = [(q & (1 << b)) != 0 for b in range(5)]
+                lines = [read[8 * j : 8 * j + 8, 128 * h : 128 * h + 128] for j in range(Q2)]
+                value = select_row(lines, bits)
                 got.append(value + pltpu.roll(value, 4, 0))
-            place = pl.multiple_of((i * STEP + 2 * k) * 4, 8)
-            found[pl.ds(place, 8), :] = jnp.where(sub8 < 4, got[0], got[1])
-        return carry
-
-    lax.fori_loop(0, slots // STEP, look, 0)
-    units = [jnp.broadcast_to(units_ref[c : c + 1], (8, 128)) for c in range(3)]
-
-    def turn(i, carry):
-        rank = i // (16 // GROUP)
-        for k in range(GROUP):
-            source = pl.multiple_of((i % (16 // GROUP)) * (8 * GROUP) + 8 * k, 8)
-            place = source * 12 + rank * 4
-            which = found[pl.ds(place + 3, 8, stride=12), :].astype(i32)
-            n = [jnp.take_along_axis(units[c], which, axis=1) for c in range(3)]
-            u = [found[pl.ds(place + c, 8, stride=12), :] for c in range(3)]
-            w = [slots_ref[pl.ds(place + c, 8, stride=12), :] - u[c] for c in range(3)]
-            inner = n[0] * w[0] + n[1] * w[1] + n[2] * w[2]
-            crossed = [
-                n[1] * w[2] - n[2] * w[1],
-                n[2] * w[0] - n[0] * w[2],
-                n[0] * w[1] - n[1] * w[0],
-            ]
-            for c in range(3):
-                out_ref[rank, c, pl.ds(source, 8), :] = (
-                    u[c]
-                    + w[c] * angle_cosine
-                    + crossed[c] * angle_sine
-                    + n[c] * inner * (1.0 - angle_cosine)
-                )
-        return carry
-
-    lax.fori_loop(0, MOST * 16 // GROUP, turn, 0)
+            found[pl.ds((i * STEP + 2 * k) * 4, 8), :] = jnp.where(sub8 < 4, got[0], got[1])
+
+    senders = STEP // MOST
+
+    def copy(i):
+        part = pl.ds(i * senders, senders)
+        return pltpu.make_async_copy(
+            out_ref.at[:, :, part, :], out_hbm.at[:, :, part, :], sems.at[i]
+        )
+
+    def turn(i):
+        for rank in range(MOST):
+            for k in range(senders // 8):
+                source = i * senders + 8 * k
+                place = (source * MOST + rank) * 4
+                which = found[pl.ds(place + 3, 8, stride=12), :].astype(i32)
+                n = [jnp.take_along_axis(units[c], which, axis=1) for c in range(3)]
+                u = [found[pl.ds(place + c, 8, stride=12), :] for c in range(3)]
+                w = [slots_ref[pl.ds(place + c, 8, stride=12), :] - u[c] for c in range(3)]
+                inner = n[0] * w[0] + n[1] * w[1] + n[2] * w[2]
+                crossed = [
+                    n[1] * w[2] - n[2] * w[1],
+                    n[2] * w[0] - n[0] * w[2],
+                    n[0] * w[1] - n[1] * w[0],
+                ]
+                for c in range(3):
+                    out_ref[rank, c, pl.ds(source, 8), :] = (
+                        u[c]
+                        + w[c] * angle_cosine
+                        + crossed[c] * angle_sine
+                        + n[c] * inner * (1.0 - angle_cosine)
+                    )
+        copy(i).start()
+
+    steps = slots // STEP
+    for i in range(steps):
+        if i > 0:
+            turn(i - 1)
+        look(i)
+    turn(steps - 1)
+    for i in range(steps):
+        copy(i).wait()
 
 
 def both_ways(head, tail, axis):
@@ -325,8 +356,24 @@
     shape = jax.ShapeDtypeStruct
     vmem = pl.BlockSpec(memory_space=pltpu.VMEM)
     smem = pl.BlockSpec(memory_space=pltpu.SMEM)
-    send = call(pack_body, shape((devices * MOST * 4, 128), f32), name="pack")(
-        block_target.reshape(1, -1), jnp.transpose(velocity, (1, 0, 2)), cell_index
+    hbm = pl.BlockSpec(memory_space=pltpu.HBM)
+    blocks = velocity.shape[0]
+    send = call(
+        pack_body,
+        shape((devices * MOST * 4, 128), f32),
+        in_specs=[hbm, hbm, hbm],
+        scratch_shapes=[
+            pltpu.VMEM((1, blocks), i32),
+            pltpu.VMEM((3, blocks, 128), f32),
+            pltpu.VMEM((blocks, 128), i32),
+            pltpu.SemaphoreType.DMA((3,)),
+        ],
+        name="pack",
+    )(
+        *(
+            pltpu.with_memory_space_constraint(x, pltpu.HBM)
+            for x in (block_target.reshape(1, -1), jnp.transpose(velocity, (1, 0, 2)), cell_index)
+        )
     )
     axes = call(
         axes_body,
@@ -365,12 +412,15 @@
     updated, cell_flow = call(
         collide_body,
         [shape((MOST, 3, devices, 128), f32), shape((3, CX, CY, CZ), f32)],
+        out_specs=[hbm, vmem],
         scratch_shapes=[
             pltpu.VMEM((PADROWS, 128), f32),
             pltpu.VMEM((2, Q2 * 8, 128), f32),
             pltpu.VMEM((devices * MOST * 4, 128), f32),
+            pltpu.VMEM((devices * MOST, 128), i32),
             pltpu.VMEM((devices * MOST, 128), f32),
-            pltpu.VMEM((devices * MOST, 128), f32),
+            pltpu.VMEM((MOST, 3, devices, 128), f32),
+            pltpu.SemaphoreType.DMA((devices * MOST // STEP,)),
         ],
         name="collide",
     )(total, up, down, axes, units, slots)

time: 64.9 us -> 58.8 us (0.906)
  Pallas kernels: 18.5 us -> 15 us
  local copies, waits for them, and re-layouts: 3.21 us -> 0.64 us
    pallas_call x1, Pallas kernels: 8.84 us -> 5.5 us  [shards(): call(deposit_body, [total_shape, x_face, x_face], scratch_shapes=[pltpu.V...]
    unnamed x10 -> x4, local copies, waits for them, and re-layouts: 3.21 us -> 0.64 us
    pallas_call x1, Pallas kernels: 7.91 us -> 6.76 us  [shards(): call(collide_body, [shape((MOST, 3, devices, 128), f32), shape((3, CX, CY...]
    pallas_call x1, Pallas kernels: 0.62 us -> 1.66 us  [shards(): call(pack_body, shape((devices * MOST * 4, 128), f32), in_specs=[hbm, hbm...]
where the time goes in v3:
time: 58.8 us; the launch traced here: 58.7 us
  blocking collectives  27.3 us (46%)
  Pallas kernels  15 us (26%)
  waiting for transfers between devices  10.2 us (17%)
  starting transfers between devices  4.78 us (8%)
  between operations  0.67 us (1%)
  local copies, waits for them, and re-layouts  0.64 us (1%)
    all_to_all x1, blocking collectives, shards(): lax.all_to_all(send.reshape(devices, MOST, 4, 128), ('gx', 'gy', 'gz'), s...  27.3 us
    ppermute x3, waiting for transfers between devices, both_ways(): lax.ppermute(tail, axis, [(i, (i + 1) % count) for i in range(count)])  6.88 us
    pallas_call x1, Pallas kernels, shards(): call(collide_body, [shape((MOST, 3, devices, 128), f32), shape((3, CX, CY...  6.76 us
    pallas_call x1, Pallas kernels, shards(): call(deposit_body, [total_shape, x_face, x_face], scratch_shapes=[pltpu.V...  5.5 us
    ppermute x3, waiting for transfers between devices, both_ways(): up = lax.ppermute(head, axis, [((i + 1) % count, i) for i in range(count)])  3.3 us
    ppermute x3, starting transfers between devices, both_ways(): lax.ppermute(tail, axis, [(i, (i + 1) % count) for i in range(count)])  2.55 us
    ppermute x3, starting transfers between devices, both_ways(): up = lax.ppermute(head, axis, [((i + 1) % count, i) for i in range(count)])  2.23 us
    pallas_call x1, Pallas kernels, shards(): call(pack_body, shape((devices * MOST * 4, 128), f32), in_specs=[hbm, hbm...  1.66 us
  transfers between devices with their start and end apart: 6, of which 5 were waited for; matrix products, arithmetic and copies ran while one was open for 0% of the time, Pallas kernels for 1%

profile of v3, /device:TPU:0, one launch (start us, length us, event | category | flops | bytes accessed | tf_op | source)
XLA Modules:
  0.0 58.7 jit_solution(11527994068962878945)
XLA Ops:
  0.6 1.7 %pack.1 = f32[1536,128]{1,0:T(8,128)S(1)} custom-call(s32[1,256]{1,0:T(1,128)} %bitcast.11, f32[3,256,128]{2,1,0:T(8,128)} %bitcast.10, s32[256,128]{1,0:T(8,128)} %index_hbm.1), custom_call_target="tpu_custom_call" | custom-call | tf_op jit(solution)/shard_map/pack/pallas_call | solution.py:361
  2.3 27.3 %all_to_all.5 = f32[128,3,4,128]{3,2,1,0:T(4,128)S(1)} all-to-all(f32[128,3,4,128]{3,2,1,0:T(4,128)S(1)} %bitcast.9), channel_id=1, replica_groups=mesh['gx'=8,'gy'=4,'gz'=4] {'gx','gy','gz'}, dimensions={0} | all-to-all | bytes 1572864 | tf_op jit(solution)/shard_map/all_to_all | solution.py:386
  29.6 0.0 copy-start
  29.6 5.5 %deposit.1 = (f32[4,48,128]{2,1,0:T(8,128)S(1)}, f32[4,16,128]{2,1,0:T(8,128)S(1)}, f32[4,16,128]{2,1,0:T(8,128)S(1)}) custom-call(f32[1536,128]{1,0:T(8,128)S(1)} %bitcast.7), custom_call_target="tpu_custom_call" | custom-call | tf_op jit(solution)/shard_map/deposit/pallas_call | solution.py:393
  35.1 0.6 %collective-permute-start = (f32[4,16,128]{2,1,0:T(8,128)S(1)}, f32[4,16,128]{2,1,0:T(8,128)S(1)}, u32[]{:S(2)}, u32[]{:S(2)}) collective-permute-start(f32[4,16,128]{2,1,0:T(8,128)S(1)} %get-tuple-element.14), channel_id=1, source_target_pairs={{16,0},{32,16},{48,32},{64,48},{80,64},{96,80},{112,96},{0,112},{1... | collective-permute-start | bytes 98312 | tf_op jit(solution)/shard_map/ppermute | solution.py:349
  35.7 0.0 collective-permute-start.1
  35.7 1.5 %collective-permute-done.up_ref = f32[4,16,128]{2,1,0:T(8,128)S(1)} collective-permute-done((f32[4,16,128]{2,1,0:T(8,128)S(1)}, f32[4,16,128]{2,1,0:T(8,128)S(1)}, u32[]{:S(2)}, u32[]{:S(2)}) %collective-permute-start) | collective-permute-done | bytes 32800 | tf_op jit(solution)/shard_map/ppermute | solution.py:349
  37.3 3.0 %collective-permute-done.1.down_ref = f32[4,16,128]{2,1,0:T(8,128)S(1)} collective-permute-done((f32[4,16,128]{2,1,0:T(8,128)S(1)}, f32[4,16,128]{2,1,0:T(8,128)S(1)}, u32[]{:S(2)}, u32[]{:S(2)}) %collective-permute-start.1) | collective-permute-done | bytes 32800 | tf_op jit(solution)/shard_map/ppermute | solution.py:350
  40.2 0.1 fold_x.1
  40.3 0.7 %collective-permute-start.2 = (f32[4,8,128]{2,1,0:T(8,128)S(1)}, f32[4,8,128]{2,1,0:T(8,128)S(1)}, u32[]{:S(2)}, u32[]{:S(2)}) collective-permute-start(f32[4,8,128]{2,1,0:T(8,128)S(1)} %get-tuple-element.17), channel_id=1, source_target_pairs={{4,0},{8,4},{12,8},{0,12},{5,1},{9,5},{13,9},{1,13},{6,2},{10,6},{... | collective-permute-start | bytes 49160 | tf_op jit(solution)/shard_map/ppermute | solution.py:349
  41.0 1.4 %collective-permute-start.3 = (f32[4,8,128]{2,1,0:T(8,128)S(1)}, f32[4,8,128]{2,1,0:T(8,128)S(1)}, u32[]{:S(2)}, u32[]{:S(2)}) collective-permute-start(f32[4,8,128]{2,1,0:T(8,128)S(1)} %get-tuple-element.18), channel_id=1, source_target_pairs={{0,4},{4,8},{8,12},{12,0},{1,5},{5,9},{9,13},{13,1},{2,6},{6,10},{... | collective-permute-start | bytes 49160 | tf_op jit(solution)/shard_map/ppermute | solution.py:350
  42.4 1.7 %collective-permute-done.2.up_ref = f32[4,8,128]{2,1,0:T(8,128)S(1)} collective-permute-done((f32[4,8,128]{2,1,0:T(8,128)S(1)}, f32[4,8,128]{2,1,0:T(8,128)S(1)}, u32[]{:S(2)}, u32[]{:S(2)}) %collective-permute-start.2) | collective-permute-done | bytes 16416 | tf_op jit(solution)/shard_map/ppermute | solution.py:349
  44.1 1.8 %collective-permute-done.3.down_ref = f32[4,8,128]{2,1,0:T(8,128)S(1)} collective-permute-done((f32[4,8,128]{2,1,0:T(8,128)S(1)}, f32[4,8,128]{2,1,0:T(8,128)S(1)}, u32[]{:S(2)}, u32[]{:S(2)}) %collective-permute-start.3) | collective-permute-done | bytes 16416 | tf_op jit(solution)/shard_map/ppermute | solution.py:350
  45.9 0.2 fold_y.1
  46.1 1.0 %collective-permute-start.4 = (f32[8,128]{1,0:T(8,128)S(1)}, f32[8,128]{1,0:T(8,128)S(1)}, u32[]{:S(2)}, u32[]{:S(2)}) collective-permute-start(f32[8,128]{1,0:T(8,128)S(1)} %get-tuple-element.20), channel_id=1, source_target_pairs={{1,0},{2,1},{3,2},{0,3},{5,4},{6,5},{7,6},{4,7},{9,8},{10,9},{11,1... | collective-permute-start | bytes 12296 | tf_op jit(solution)/shard_map/ppermute | solution.py:349
  47.1 1.1 %collective-permute-start.5 = (f32[8,128]{1,0:T(8,128)S(1)}, f32[8,128]{1,0:T(8,128)S(1)}, u32[]{:S(2)}, u32[]{:S(2)}) collective-permute-start(f32[8,128]{1,0:T(8,128)S(1)} %get-tuple-element.21), channel_id=1, source_target_pairs={{0,1},{1,2},{2,3},{3,0},{4,5},{5,6},{6,7},{7,4},{8,9},{9,10},{10,1... | collective-permute-start | bytes 12296 | tf_op jit(solution)/shard_map/ppermute | solution.py:350
  48.2 0.0 copy-start.1
  48.2 0.0 copy-done
  48.2 0.6 %copy-done.1 = s32[3]{0:T(128)S(1)} copy-done((s32[3]{0:T(128)S(1)}, s32[3]{0:T(128)}, u32[]{:S(2)}) %copy-start.1) | copy-done | bytes 36
  48.8 0.9 %axes.1.axes_ref = f32[48,128]{1,0:T(8,128)S(1)} custom-call(s32[3]{0:T(128)S(1)} %copy-done.1, s32[32,32,32]{2,1,0:T(8,128)S(1)} %copy-done), custom_call_target="tpu_custom_call" | custom-call | tf_op jit(solution)/shard_map/axes/pallas_call | solution.py:378
  49.7 0.0 collective-permute-done.4.up_ref
  49.8 2.1 %collective-permute-done.5.down_ref = f32[8,128]{1,0:T(8,128)S(1)} collective-permute-done((f32[8,128]{1,0:T(8,128)S(1)}, f32[8,128]{1,0:T(8,128)S(1)}, u32[]{:S(2)}, u32[]{:S(2)}) %collective-permute-start.5) | collective-permute-done | bytes 4128 | tf_op jit(solution)/shard_map/ppermute | solution.py:350
  51.9 6.8 %collide.1 = (f32[3,3,128,128]{3,2,1,0:T(8,128)}, f32[3,4,8,128]{3,2,1,0:T(8,128)}) custom-call(f32[4,48,128]{2,1,0:T(8,128)S(1)} %get-tuple-element.19.total_ref, f32[8,128]{1,0:T(8,128)S(1)} %collective-permute-done.4.up_ref, f32[8,128]{1,0:T(8,128)S(1)} %collective-permute-done.5.down_ref, f32[48,128]{1,0:T(8,128)S(1)} %axes.1.axes_ref, ...), custom_call_target="tpu_custom_call" | custom-call | tf_op jit(solution)/shard_map/collide/pallas_call | solution.py:412
  (3 shorter events, 0.1 us)
Async XLA Ops:
  29.6 18.6 %copy-start = (s32[32,32,32]{2,1,0:T(8,128)S(1)}, s32[32,32,32]{2,1,0:T(8,128)}, u32[]{:S(2)}) copy-start(s32[32,32,32]{2,1,0:T(8,128)} %rotation_ref.1) | copy-start | bytes 393220
  35.1 2.2 %collective-permute-start = (f32[4,16,128]{2,1,0:T(8,128)S(1)}, f32[4,16,128]{2,1,0:T(8,128)S(1)}, u32[]{:S(2)}, u32[]{:S(2)}) collective-permute-start(f32[4,16,128]{2,1,0:T(8,128)S(1)} %get-tuple-element.14), channel_id=1, source_target_pairs={{16,0},{32,16},{48,32},{64,48},{80,64},{96,80},{112,96},{0,112},{1... | collective-permute-start | bytes 98312 | tf_op jit(solution)/shard_map/ppermute | solution.py:349
  35.7 4.6 %collective-permute-start.1 = (f32[4,16,128]{2,1,0:T(8,128)S(1)}, f32[4,16,128]{2,1,0:T(8,128)S(1)}, u32[]{:S(2)}, u32[]{:S(2)}) collective-permute-start(f32[4,16,128]{2,1,0:T(8,128)S(1)} %get-tuple-element.15), channel_id=1, source_target_pairs={{0,16},{16,32},{32,48},{48,64},{64,80},{80,96},{96,112},{112,0},{1... | collective-permute-start | bytes 98312 | tf_op jit(solution)/shard_map/ppermute | solution.py:350
  40.3 3.8 %collective-permute-start.2 = (f32[4,8,128]{2,1,0:T(8,128)S(1)}, f32[4,8,128]{2,1,0:T(8,128)S(1)}, u32[]{:S(2)}, u32[]{:S(2)}) collective-permute-start(f32[4,8,128]{2,1,0:T(8,128)S(1)} %get-tuple-element.17), channel_id=1, source_target_pairs={{4,0},{8,4},{12,8},{0,12},{5,1},{9,5},{13,9},{1,13},{6,2},{10,6},{... | collective-permute-start | bytes 49160 | tf_op jit(solution)/shard_map/ppermute | solution.py:349
  41.0 4.9 %collective-permute-start.3 = (f32[4,8,128]{2,1,0:T(8,128)S(1)}, f32[4,8,128]{2,1,0:T(8,128)S(1)}, u32[]{:S(2)}, u32[]{:S(2)}) collective-permute-start(f32[4,8,128]{2,1,0:T(8,128)S(1)} %get-tuple-element.18), channel_id=1, source_target_pairs={{0,4},{4,8},{8,12},{12,0},{1,5},{5,9},{9,13},{13,1},{2,6},{6,10},{... | collective-permute-start | bytes 49160 | tf_op jit(solution)/shard_map/ppermute | solution.py:350
  46.1 3.7 %collective-permute-start.4 = (f32[8,128]{1,0:T(8,128)S(1)}, f32[8,128]{1,0:T(8,128)S(1)}, u32[]{:S(2)}, u32[]{:S(2)}) collective-permute-start(f32[8,128]{1,0:T(8,128)S(1)} %get-tuple-element.20), channel_id=1, source_target_pairs={{1,0},{2,1},{3,2},{0,3},{5,4},{6,5},{7,6},{4,7},{9,8},{10,9},{11,1... | collective-permute-start | bytes 12296 | tf_op jit(solution)/shard_map/ppermute | solution.py:349
  47.1 4.8 %collective-permute-start.5 = (f32[8,128]{1,0:T(8,128)S(1)}, f32[8,128]{1,0:T(8,128)S(1)}, u32[]{:S(2)}, u32[]{:S(2)}) collective-permute-start(f32[8,128]{1,0:T(8,128)S(1)} %get-tuple-element.21), channel_id=1, source_target_pairs={{0,1},{1,2},{2,3},{3,0},{4,5},{5,6},{6,7},{7,4},{8,9},{9,10},{10,1... | collective-permute-start | bytes 12296 | tf_op jit(solution)/shard_map/ppermute | solution.py:350
  48.2 0.7 %copy-start.1 = (s32[3]{0:T(128)S(1)}, s32[3]{0:T(128)}, u32[]{:S(2)}) copy-start(s32[3]{0:T(128)} %shift_ref.1) | copy-start | bytes 40

commit v4 on v3

--- a/solution.py
+++ b/solution.py
@@ -125,7 +125,6 @@
 
 
 DEPOSIT_STEP = 128
-STEP = 96
 Q2 = ROWS // 2
 
 
@@ -247,11 +246,46 @@
     return rows[0]
 
 
-def collide_body(
-    total_ref, up_ref, down_ref, axes_ref, units_ref, slots_ref, out_hbm, flow_ref,
-    cells, wide, found, rows_q, rows_l, out_ref, sems,
+def look_body(total_ref, axes_ref, slots_ref, found, cells, wide, rows_q, rows_l):
+    slots = slots_ref.shape[0] // 4
+    count = jnp.maximum(total_ref[3], 1.0)
+    wide[...] = jnp.zeros(wide.shape, f32)
+
+    def tabulate(value, line):
+        cells[...] = value
+        for odd in range(2):
+            wide[odd, pl.ds(line, Q2, stride=8), :] = cells[pl.ds(odd, Q2, stride=2)]
+
+    for c in range(3):
+        mean = total_ref[c] / count
+        high = mean.astype(bf16).astype(f32)
+        tabulate(high, c)
+        tabulate(mean - high, c + 4)
+    tabulate(axes_ref[...], 3)
+    table = jnp.concatenate([wide[0], wide[1]], axis=1).astype(bf16)
+    slot_places(slots_ref, rows_q, rows_l)
+    sub8 = iota((8, 128), 0)
+    for k in range(slots // 2):
+        pair = [2 * k, 2 * k + 1]
+        hot = jnp.concatenate([lane_onehot(rows_l, slot) for slot in pair], axis=1)
+        read = jnp.dot(table, hot, preferred_element_type=f32)
+        got = []
+        for h in range(2):
+            q = jnp.broadcast_to(rows_q[pl.ds(pair[h], 1), :], (8, 128))
+            bits = [(q & (1 << b)) != 0 for b in range(5)]
+            lines = [read[8 * j : 8 * j + 8, 128 * h : 128 * h + 128] for j in range(Q2)]
+            value = select_row(lines, bits)
+            got.append(value + pltpu.roll(value, 4, 0))
+        found[pl.ds(8 * k, 8), :] = jnp.where(sub8 < 4, got[0], got[1])
+
+
+SENDERS = 32
+
+
+def turn_body(
+    total_ref, up_ref, down_ref, units_ref, slots_ref, found, out_hbm, flow_ref, out_ref, sems
 ):
-    slots = slots_ref.shape[0] // 4
+    devices = out_ref.shape[2]
     shape = (PADROWS, 128)
     row = iota(shape, 0)
     lane = iota(shape, 1)
@@ -267,57 +301,43 @@
         own = own + jnp.where(lane == 0, column, 0.0)
         totals.append(own + jnp.where(top, up_ref[c : c + 1], 0.0))
     count = jnp.maximum(totals[3], 1.0)
-    wide[...] = jnp.zeros(wide.shape, f32)
-
-    def tabulate(value, line):
-        cells[...] = value
-        for odd in range(2):
-            wide[odd, pl.ds(line, Q2, stride=8), :] = cells[pl.ds(odd, Q2, stride=2)]
-
+    rims = []
     for c in range(3):
         mean = totals[c] / count
         for ex in range(CX):
             flow_ref[c, ex] = mean[ex * PY : ex * PY + CY]
-        high = mean.astype(bf16).astype(f32)
-        tabulate(high, c)
-        tabulate(mean - high, c + 4)
-    tabulate(axes_ref[...], 3)
-    table = jnp.concatenate([wide[0], wide[1]], axis=1).astype(bf16)
-    slot_places(slots_ref, rows_q, rows_l)
-    sub8 = iota((8, 128), 0)
-
+        low = pltpu.roll(column_as_row(mean), 64, 1)
+        rim = jnp.where(iota((1, 128), 1) < 64, mean[PLANES:ROWS], low)
+        rims.append(jnp.broadcast_to(rim, (8, 128)))
     units = [jnp.broadcast_to(units_ref[c : c + 1], (8, 128)) for c in range(3)]
 
-    def look(i):
-        for k in range(STEP // 2):
-            pair = [i * STEP + 2 * k, i * STEP + 2 * k + 1]
-            hot = jnp.concatenate([lane_onehot(rows_l, slot) for slot in pair], axis=1)
-            read = jnp.dot(table, hot, preferred_element_type=f32)
-            got = []
-            for h in range(2):
-                q = jnp.broadcast_to(rows_q[pl.ds(pair[h], 1), :], (8, 128))
-                bits = [(q & (1 << b)) != 0 for b in range(5)]
-                lines = [read[8 * j : 8 * j + 8, 128 * h : 128 * h + 128] for j in range(Q2)]
-                value = select_row(lines, bits)
-                got.append(value + pltpu.roll(value, 4, 0))
-            found[pl.ds((i * STEP + 2 * k) * 4, 8), :] = jnp.where(sub8 < 4, got[0], got[1])
-
-    senders = STEP // MOST
-
     def copy(i):
-        part = pl.ds(i * senders, senders)
+        part = pl.ds(i * SENDERS, SENDERS)
         return pltpu.make_async_copy(
             out_ref.at[:, :, part, :], out_hbm.at[:, :, part, :], sems.at[i]
         )
 
-    def turn(i):
+    for i in range(devices // SENDERS):
         for rank in range(MOST):
-            for k in range(senders // 8):
-                source = i * senders + 8 * k
+            for k in range(SENDERS // 8):
+                source = i * SENDERS + 8 * k
                 place = (source * MOST + rank) * 4
+                label = slots_ref[pl.ds(place + 3, 8, stride=12), :].astype(i32)
+                q = label >> 7
+                l = label & 127
+                above = q == PLANES
+                below = (l == 0) & (q < PLANES)
+                rim_lane = jnp.where(above, l, (q + 64) & 127)
                 which = found[pl.ds(place + 3, 8, stride=12), :].astype(i32)
                 n = [jnp.take_along_axis(units[c], which, axis=1) for c in range(3)]
-                u = [found[pl.ds(place + c, 8, stride=12), :] for c in range(3)]
+                u = [
+                    jnp.where(
+                        above | below,
+                        jnp.take_along_axis(rims[c], rim_lane, axis=1),
+                        found[pl.ds(place + c, 8, stride=12), :],
+                    )
+                    for c in range(3)
+                ]
                 w = [slots_ref[pl.ds(place + c, 8, stride=12), :] - u[c] for c in range(3)]
                 inner = n[0] * w[0] + n[1] * w[1] + n[2] * w[2]
                 crossed = [
@@ -333,14 +353,7 @@
                         + n[c] * inner * (1.0 - angle_cosine)
                     )
         copy(i).start()
-
-    steps = slots // STEP
-    for i in range(steps):
-        if i > 0:
-            turn(i - 1)
-        look(i)
-    turn(steps - 1)
-    for i in range(steps):
+    for i in range(devices // SENDERS):
         copy(i).wait()
 
 
@@ -405,25 +418,32 @@
         total, up, down
     )
     up, down = both_ways(head, tail, "gy")
+    up, down, axes, units = lax.optimization_barrier((up, down, axes, units))
     total, head, tail = call(fold_y_body, [total_shape, z_face, z_face], name="fold_y")(
         total, up, down
     )
     up, down = both_ways(head, tail, "gz")
+    found = call(
+        look_body,
+        shape((devices * MOST * 4, 128), f32),
+        scratch_shapes=[
+            pltpu.VMEM((PADROWS, 128), f32),
+            pltpu.VMEM((2, Q2 * 8, 128), f32),
+            pltpu.VMEM((devices * MOST, 128), i32),
+            pltpu.VMEM((devices * MOST, 128), f32),
+        ],
+        name="look",
+    )(total, axes, slots)
     updated, cell_flow = call(
-        collide_body,
+        turn_body,
         [shape((MOST, 3, devices, 128), f32), shape((3, CX, CY, CZ), f32)],
         out_specs=[hbm, vmem],
         scratch_shapes=[
-            pltpu.VMEM((PADROWS, 128), f32),
-            pltpu.VMEM((2, Q2 * 8, 128), f32),
-            pltpu.VMEM((devices * MOST * 4, 128), f32),
-            pltpu.VMEM((devices * MOST, 128), i32),
-            pltpu.VMEM((devices * MOST, 128), f32),
             pltpu.VMEM((MOST, 3, devices, 128), f32),
-            pltpu.SemaphoreType.DMA((devices * MOST // STEP,)),
+            pltpu.SemaphoreType.DMA((devices // SENDERS,)),
         ],
-        name="collide",
-    )(total, up, down, axes, units, slots)
+        name="turn",
+    )(total, up, down, units, slots, found)
     return jnp.transpose(updated, (2, 0, 1, 3))[None], cell_flow
 
 

time: 58.8 us -> 56.9 us (0.968)
  blocking collectives: 27.3 us -> 0 us
  waiting for transfers between devices: 10.2 us -> 22.8 us
  starting transfers between devices: 4.78 us -> 15.9 us
  Pallas kernels: 15 us -> 16.6 us
    all_to_all x1 -> x0, blocking collectives: 27.3 us -> none  [shards(): lax.all_to_all(send.reshape(devices, MOST, 4, 128), ('gx', 'gy', 'gz'), s...]
    all_to_all x0 -> x1, waiting for transfers between devices: none -> 16.3 us  [shards(): lax.all_to_all(send.reshape(devices, MOST, 4, 128), ('gx', 'gy', 'gz'), s...]
    all_to_all x0 -> x1, starting transfers between devices: none -> 11.2 us  [shards(): lax.all_to_all(send.reshape(devices, MOST, 4, 128), ('gx', 'gy', 'gz'), s...]
    ppermute x3, waiting for transfers between devices: 6.88 us -> 4.75 us  [both_ways(): lax.ppermute(tail, axis, [(i, (i + 1) % count) for i in range(count)])]
    ppermute x3, waiting for transfers between devices: 3.3 us -> 1.77 us  [both_ways(): up = lax.ppermute(head, axis, [((i + 1) % count, i) for i in range(count)])]
    pallas_call x1, Pallas kernels: 1.66 us -> 2.57 us  [shards(): call(pack_body, shape((devices * MOST * 4, 128), f32), in_specs=[hbm, hbm...]
    pallas_call x1 -> x2, Pallas kernels: 6.76 us -> 7.39 us  [the longest x1 5.18 us: shards(): call(look_body, shape((devices * MOST * 4, 128), f32), scratch_shapes=[pl...]
  transfers between devices with their start and end apart: 6 -> 7, of which waited for: 5 -> 5; matrix products, arithmetic and copies ran while one was open for 0% -> 0% of each run, Pallas kernels for 1% -> 11%
where the time goes in v4:
time: 56.9 us; the launch traced here: 56.7 us
  waiting for transfers between devices  22.8 us (40%)
  Pallas kernels  16.6 us (29%)
  starting transfers between devices  15.9 us (28%)
  between operations  0.7 us (1%)
  local copies, waits for them, and re-layouts  0.64 us (1%)
    all_to_all x1, waiting for transfers between devices, shards(): lax.all_to_all(send.reshape(devices, MOST, 4, 128), ('gx', 'gy', 'gz'), s...  16.3 us
    all_to_all x1, starting transfers between devices, shards(): lax.all_to_all(send.reshape(devices, MOST, 4, 128), ('gx', 'gy', 'gz'), s...  11.2 us
    pallas_call x1, Pallas kernels, shards(): call(deposit_body, [total_shape, x_face, x_face], scratch_shapes=[pltpu.V...  5.5 us
    pallas_call x1, Pallas kernels, shards(): call(look_body, shape((devices * MOST * 4, 128), f32), scratch_shapes=[pl...  5.18 us
    ppermute x3, waiting for transfers between devices, both_ways(): lax.ppermute(tail, axis, [(i, (i + 1) % count) for i in range(count)])  4.75 us
    pallas_call x1, Pallas kernels, shards(): call(pack_body, shape((devices * MOST * 4, 128), f32), in_specs=[hbm, hbm...  2.57 us
    ppermute x3, starting transfers between devices, both_ways(): lax.ppermute(tail, axis, [(i, (i + 1) % count) for i in range(count)])  2.54 us
    ppermute x3, starting transfers between devices, both_ways(): up = lax.ppermute(head, axis, [((i + 1) % count, i) for i in range(count)])  2.24 us
  transfers between devices with their start and end apart: 7, of which 5 were waited for; matrix products, arithmetic and copies ran while one was open for 0% of the time, Pallas kernels for 11%

profile of v4, /device:TPU:0, one launch (start us, length us, event | category | flops | bytes accessed | tf_op | source)
XLA Modules:
  0.0 56.7 jit_solution(166865347125404069)
XLA Ops:
  0.6 2.6 %pack.1 = f32[1536,128]{1,0:T(8,128)} custom-call(s32[1,256]{1,0:T(1,128)} %bitcast.11, f32[3,256,128]{2,1,0:T(8,128)} %bitcast.10, s32[256,128]{1,0:T(8,128)} %index_hbm.1), custom_call_target="tpu_custom_call" | custom-call | tf_op jit(solution)/shard_map/pack/pallas_call | solution.py:374
  3.2 11.2 %all-to-all-start = ((f32[128,3,4,128]{3,2,1,0:T(4,128)}), f32[128,3,4,128]{3,2,1,0:T(4,128)S(1)}, u32[]{:S(2)}, u32[]{:S(2)}) async-start(f32[128,3,4,128]{3,2,1,0:T(4,128)} %bitcast.2), calls=%async_computation | async-start | bytes 1572864 | tf_op jit(solution)/shard_map/all_to_all | solution.py:399
  14.4 0.0 copy-start
  14.4 16.3 %all-to-all-done = f32[128,3,4,128]{3,2,1,0:T(4,128)S(1)} async-done(((f32[128,3,4,128]{3,2,1,0:T(4,128)}), f32[128,3,4,128]{3,2,1,0:T(4,128)S(1)}, u32[]{:S(2)}, u32[]{:S(2)}) %all-to-all-start) | async-done | bytes 786464 | tf_op jit(solution)/shard_map/all_to_all | solution.py:399
  30.7 5.5 %deposit.1 = (f32[4,48,128]{2,1,0:T(8,128)S(1)}, f32[4,16,128]{2,1,0:T(8,128)S(1)}, f32[4,16,128]{2,1,0:T(8,128)S(1)}) custom-call(f32[1536,128]{1,0:T(8,128)S(1)} %bitcast.7), custom_call_target="tpu_custom_call" | custom-call | tf_op jit(solution)/shard_map/deposit/pallas_call | solution.py:406
  36.2 0.6 %collective-permute-start = (f32[4,16,128]{2,1,0:T(8,128)S(1)}, f32[4,16,128]{2,1,0:T(8,128)S(1)}, u32[]{:S(2)}, u32[]{:S(2)}) collective-permute-start(f32[4,16,128]{2,1,0:T(8,128)S(1)} %get-tuple-element.18), channel_id=1, source_target_pairs={{16,0},{32,16},{48,32},{64,48},{80,64},{96,80},{112,96},{0,112},{1... | collective-permute-start | bytes 98312 | tf_op jit(solution)/shard_map/ppermute | solution.py:362
  36.8 0.0 collective-permute-start.1
  36.8 1.6 %collective-permute-done.up_ref = f32[4,16,128]{2,1,0:T(8,128)S(1)} collective-permute-done((f32[4,16,128]{2,1,0:T(8,128)S(1)}, f32[4,16,128]{2,1,0:T(8,128)S(1)}, u32[]{:S(2)}, u32[]{:S(2)}) %collective-permute-start) | collective-permute-done | bytes 32800 | tf_op jit(solution)/shard_map/ppermute | solution.py:362
  38.4 3.0 %collective-permute-done.1.down_ref = f32[4,16,128]{2,1,0:T(8,128)S(1)} collective-permute-done((f32[4,16,128]{2,1,0:T(8,128)S(1)}, f32[4,16,128]{2,1,0:T(8,128)S(1)}, u32[]{:S(2)}, u32[]{:S(2)}) %collective-permute-start.1) | collective-permute-done | bytes 32800 | tf_op jit(solution)/shard_map/ppermute | solution.py:363
  41.4 0.1 fold_x.1
  41.4 0.7 %collective-permute-start.2 = (f32[4,8,128]{2,1,0:T(8,128)S(1)}, f32[4,8,128]{2,1,0:T(8,128)S(1)}, u32[]{:S(2)}, u32[]{:S(2)}) collective-permute-start(f32[4,8,128]{2,1,0:T(8,128)S(1)} %get-tuple-element.21), channel_id=1, source_target_pairs={{4,0},{8,4},{12,8},{0,12},{5,1},{9,5},{13,9},{1,13},{6,2},{10,6},{... | collective-permute-start | bytes 49160 | tf_op jit(solution)/shard_map/ppermute | solution.py:362
  42.1 1.4 %collective-permute-start.3 = (f32[4,8,128]{2,1,0:T(8,128)S(1)}, f32[4,8,128]{2,1,0:T(8,128)S(1)}, u32[]{:S(2)}, u32[]{:S(2)}) collective-permute-start(f32[4,8,128]{2,1,0:T(8,128)S(1)} %get-tuple-element.22), channel_id=1, source_target_pairs={{0,4},{4,8},{8,12},{12,0},{1,5},{5,9},{9,13},{13,1},{2,6},{6,10},{... | collective-permute-start | bytes 49160 | tf_op jit(solution)/shard_map/ppermute | solution.py:363
  43.5 0.0 copy-start.1
  43.6 0.0 copy-done
  43.6 0.6 %copy-done.1 = s32[3]{0:T(128)S(1)} copy-done((s32[3]{0:T(128)S(1)}, s32[3]{0:T(128)}, u32[]{:S(2)}) %copy-start.1) | copy-done | bytes 36
  44.2 0.9 %axes.1.axes_ref = f32[48,128]{1,0:T(8,128)S(1)} custom-call(s32[3]{0:T(128)S(1)} %copy-done.1, s32[32,32,32]{2,1,0:T(8,128)S(1)} %copy-done), custom_call_target="tpu_custom_call" | custom-call | tf_op jit(solution)/shard_map/axes/pallas_call | solution.py:391
  45.1 0.2 collective-permute-done.2.up_ref
  45.3 1.8 %collective-permute-done.3.down_ref = f32[4,8,128]{2,1,0:T(8,128)S(1)} collective-permute-done((f32[4,8,128]{2,1,0:T(8,128)S(1)}, f32[4,8,128]{2,1,0:T(8,128)S(1)}, u32[]{:S(2)}, u32[]{:S(2)}) %collective-permute-start.3) | collective-permute-done | bytes 16416 | tf_op jit(solution)/shard_map/ppermute | solution.py:363
  47.0 0.2 fold_y.1
  47.2 1.0 %collective-permute-start.4 = (f32[8,128]{1,0:T(8,128)S(1)}, f32[8,128]{1,0:T(8,128)S(1)}, u32[]{:S(2)}, u32[]{:S(2)}) collective-permute-start(f32[8,128]{1,0:T(8,128)S(1)} %get-tuple-element.26), channel_id=1, source_target_pairs={{1,0},{2,1},{3,2},{0,3},{5,4},{6,5},{7,6},{4,7},{9,8},{10,9},{11,1... | collective-permute-start | bytes 12296 | tf_op jit(solution)/shard_map/ppermute | solution.py:362
  48.2 1.1 %collective-permute-start.5 = (f32[8,128]{1,0:T(8,128)S(1)}, f32[8,128]{1,0:T(8,128)S(1)}, u32[]{:S(2)}, u32[]{:S(2)}) collective-permute-start(f32[8,128]{1,0:T(8,128)S(1)} %get-tuple-element.27), channel_id=1, source_target_pairs={{0,1},{1,2},{2,3},{3,0},{4,5},{5,6},{6,7},{7,4},{8,9},{9,10},{10,1... | collective-permute-start | bytes 12296 | tf_op jit(solution)/shard_map/ppermute | solution.py:363
  49.3 5.2 %look.1.found = f32[1536,128]{1,0:T(8,128)S(1)} custom-call(f32[4,48,128]{2,1,0:T(8,128)S(1)} %get-tuple-element.25.total_ref, f32[48,128]{1,0:T(8,128)S(1)} %axes.1.axes_ref, f32[1536,128]{1,0:T(8,128)S(1)} %bitcast.8), custom_call_target="tpu_custom_call" | custom-call | tf_op jit(solution)/shard_map/look/pallas_call | solution.py:426
  54.5 0.0 collective-permute-done.4.up_ref
  54.5 0.0 collective-permute-done.5.down_ref
  54.5 2.2 %turn.1 = (f32[3,3,128,128]{3,2,1,0:T(8,128)}, f32[3,4,8,128]{3,2,1,0:T(8,128)}) custom-call(f32[4,48,128]{2,1,0:T(8,128)S(1)} %get-tuple-element.25.total_ref, f32[8,128]{1,0:T(8,128)S(1)} %collective-permute-done.4.up_ref, f32[8,128]{1,0:T(8,128)S(1)} %collective-permute-done.5.down_ref, f32[8,128]{1,0:T(8,128)S(1)} %select_maximum_fusion.units_ref, ...), custom_call_target="tpu_custom_call" | custom-call | tf_op jit(solution)/shard_map/turn/pallas_call | solution.py:437
  (3 shorter events, 0.1 us)
Async XLA Ops:
  3.2 27.5 %all-to-all-start = ((f32[128,3,4,128]{3,2,1,0:T(4,128)}), f32[128,3,4,128]{3,2,1,0:T(4,128)S(1)}, u32[]{:S(2)}, u32[]{:S(2)}) async-start(f32[128,3,4,128]{3,2,1,0:T(4,128)} %bitcast.2), calls=%async_computation | async-start | bytes 1572864 | tf_op jit(solution)/shard_map/all_to_all | solution.py:399
  14.4 29.2 %copy-start = (s32[32,32,32]{2,1,0:T(8,128)S(1)}, s32[32,32,32]{2,1,0:T(8,128)}, u32[]{:S(2)}) copy-start(s32[32,32,32]{2,1,0:T(8,128)} %rotation_ref.1) | copy-start | bytes 393220
  36.2 2.2 %collective-permute-start = (f32[4,16,128]{2,1,0:T(8,128)S(1)}, f32[4,16,128]{2,1,0:T(8,128)S(1)}, u32[]{:S(2)}, u32[]{:S(2)}) collective-permute-start(f32[4,16,128]{2,1,0:T(8,128)S(1)} %get-tuple-element.18), channel_id=1, source_target_pairs={{16,0},{32,16},{48,32},{64,48},{80,64},{96,80},{112,96},{0,112},{1... | collective-permute-start | bytes 98312 | tf_op jit(solution)/shard_map/ppermute | solution.py:362
  36.8 4.6 %collective-permute-start.1 = (f32[4,16,128]{2,1,0:T(8,128)S(1)}, f32[4,16,128]{2,1,0:T(8,128)S(1)}, u32[]{:S(2)}, u32[]{:S(2)}) collective-permute-start(f32[4,16,128]{2,1,0:T(8,128)S(1)} %get-tuple-element.19), channel_id=1, source_target_pairs={{0,16},{16,32},{32,48},{48,64},{64,80},{80,96},{96,112},{112,0},{1... | collective-permute-start | bytes 98312 | tf_op jit(solution)/shard_map/ppermute | solution.py:363
  41.4 3.8 %collective-permute-start.2 = (f32[4,8,128]{2,1,0:T(8,128)S(1)}, f32[4,8,128]{2,1,0:T(8,128)S(1)}, u32[]{:S(2)}, u32[]{:S(2)}) collective-permute-start(f32[4,8,128]{2,1,0:T(8,128)S(1)} %get-tuple-element.21), channel_id=1, source_target_pairs={{4,0},{8,4},{12,8},{0,12},{5,1},{9,5},{13,9},{1,13},{6,2},{10,6},{... | collective-permute-start | bytes 49160 | tf_op jit(solution)/shard_map/ppermute | solution.py:362
  42.1 4.9 %collective-permute-start.3 = (f32[4,8,128]{2,1,0:T(8,128)S(1)}, f32[4,8,128]{2,1,0:T(8,128)S(1)}, u32[]{:S(2)}, u32[]{:S(2)}) collective-permute-start(f32[4,8,128]{2,1,0:T(8,128)S(1)} %get-tuple-element.22), channel_id=1, source_target_pairs={{0,4},{4,8},{8,12},{12,0},{1,5},{5,9},{9,13},{13,1},{2,6},{6,10},{... | collective-permute-start | bytes 49160 | tf_op jit(solution)/shard_map/ppermute | solution.py:363
  43.5 0.7 %copy-start.1 = (s32[3]{0:T(128)S(1)}, s32[3]{0:T(128)}, u32[]{:S(2)}) copy-start(s32[3]{0:T(128)} %shift_ref.1) | copy-start | bytes 40
  47.2 7.3 %collective-permute-start.4 = (f32[8,128]{1,0:T(8,128)S(1)}, f32[8,128]{1,0:T(8,128)S(1)}, u32[]{:S(2)}, u32[]{:S(2)}) collective-permute-start(f32[8,128]{1,0:T(8,128)S(1)} %get-tuple-element.26), channel_id=1, source_target_pairs={{1,0},{2,1},{3,2},{0,3},{5,4},{6,5},{7,6},{4,7},{9,8},{10,9},{11,1... | collective-permute-start | bytes 12296 | tf_op jit(solution)/shard_map/ppermute | solution.py:362
  48.2 6.3 %collective-permute-start.5 = (f32[8,128]{1,0:T(8,128)S(1)}, f32[8,128]{1,0:T(8,128)S(1)}, u32[]{:S(2)}, u32[]{:S(2)}) collective-permute-start(f32[8,128]{1,0:T(8,128)S(1)} %get-tuple-element.27), channel_id=1, source_target_pairs={{0,1},{1,2},{2,3},{3,0},{4,5},{5,6},{6,7},{7,4},{8,9},{9,10},{10,1... | collective-permute-start | bytes 12296 | tf_op jit(solution)/shard_map/ppermute | solution.py:363

commit v5 on v4

--- a/solution.py
+++ b/solution.py
@@ -32,12 +32,12 @@
     return lax.broadcasted_iota(i32, shape, dim)
 
 
-def axis_table():
-    counter = jnp.arange(NAX, dtype=f32) + 0.5
+def axis_table(shape):
+    counter = iota(shape, 1).astype(f32) + 0.5
     height = 1.0 - 2.0 * counter / NAX
     radius = jnp.sqrt(jnp.maximum(1.0 - height * height, 0.0))
     turning = counter * 2.399963229728653
-    return jnp.stack([radius * jnp.cos(turning), radius * jnp.sin(turning), height])
+    return radius * jnp.cos(turning), radius * jnp.sin(turning), height
 
 
 def split3(value):
@@ -94,7 +94,7 @@
             out_ref[pl.ds(rank * 4 + c, bricks, stride=4 * MOST), :] = value
 
 
-def axes_body(shift_ref, rotation_ref, out_ref, rows):
+def axes_body(shift_ref, rotation_ref, out_ref, units_ref, rows):
     base_x = lax.axis_index("gx") * CX + shift_ref[0]
     base_y = lax.axis_index("gy") * CY + shift_ref[1]
     rows[...] = jnp.zeros(rows.shape, i32)
@@ -109,19 +109,14 @@
     value = pltpu.roll(value, (128 - shift_ref[2]) & 127, 1)
     first = column_as_row(value)
     out_ref[...] = jnp.where(iota(value.shape, 0) == PLANES, first, value)
+    for c, line in enumerate(axis_table((8, 128))):
+        units_ref[c] = line
 
 
 def column_as_row(value):
     column = jnp.broadcast_to(value[:, 0:1], value.shape)
     same = iota(value.shape, 0) == iota(value.shape, 1)
     return jnp.sum(jnp.where(same, column, 0.0), axis=0, keepdims=True)
-
-
-def gather_x_faces(total, c, head_ref, tail_ref):
-    head_ref[c, 0:PY] = total[0:PY]
-    head_ref[c, PY : PY + 1] = total[PLANES:ROWS]
-    tail_ref[c, 0:PY] = total[PLANES - PY : PLANES]
-    tail_ref[c, PY : PY + 1] = total[PLANES:ROWS]
 
 
 DEPOSIT_STEP = 128
@@ -135,20 +130,20 @@
     rows_l[...] = jnp.where(label >= PADROWS * 128, 512, label & 255).astype(f32)
 
 
-def lane_onehot(rows_l, slot):
+def lane_onehot(rows_l, slot, tiles=16):
     step = iota((16, 128), 0).astype(f32).astype(bf16)
     lane = jnp.broadcast_to(rows_l[pl.ds(slot, 1), :], (16, 128)).astype(bf16) - step
     one = jnp.ones((16, 128), bf16)
     zero = jnp.zeros((16, 128), bf16)
-    return jnp.concatenate([jnp.where(lane == float(16 * j), one, zero) for j in range(16)], axis=0)
-
-
-def deposit_body(slots_ref, total_ref, head_ref, tail_ref, acc, rows_q, rows_l):
+    return jnp.concatenate(
+        [jnp.where(lane == float(16 * j), one, zero) for j in range(tiles)], axis=0
+    )
+
+
+def sum_rows(slots_ref, rows_q, rows_l, firsts, apart, tiles, store):
     slots = slots_ref.shape[0] // 4
-    slot_places(slots_ref, rows_q, rows_l)
-    acc[...] = jnp.zeros(acc.shape, f32)
     sub8 = iota((8, 128), 0)
-    half = jnp.where(iota((16, 128), 0) >= 8, 1.0, 0.0).astype(bf16)
+    half = jnp.where(iota((16, 128), 0) >= 8, float(apart), 0.0).astype(bf16)
     zero = jnp.zeros((16, 128), bf16)
 
     def step(i, carry):
@@ -163,22 +158,54 @@
             value = jnp.concatenate([value, value], axis=0).astype(bf16)
             q = jnp.broadcast_to(rows_q[pl.ds(slot, 1), :], (16, 128)).astype(bf16) - half
             weighted.append(
-                jnp.concatenate(
-                    [jnp.where(q == float(2 * j), value, zero) for j in range(12)], axis=0
-                )
+                jnp.concatenate([jnp.where(q == float(j), value, zero) for j in firsts], axis=0)
             )
-            depths.append(lane_onehot(rows_l, slot).astype(jnp.float8_e4m3fn))
-        got = lax.dot_general(
-            jnp.concatenate(weighted, axis=1),
-            jnp.concatenate(depths, axis=1),
-            (((1,), (1,)), ((), ())),
-            preferred_element_type=f32,
-        )
+            depths.append(lane_onehot(rows_l, slot, tiles).astype(jnp.float8_e4m3fn))
+        store(
+            lax.dot_general(
+                jnp.concatenate(weighted, axis=1),
+                jnp.concatenate(depths, axis=1),
+                (((1,), (1,)), ((), ())),
+                preferred_element_type=f32,
+            )
+        )
+        return carry
+
+    lax.fori_loop(0, slots // DEPOSIT_STEP, step, 0)
+
+
+def deposit_faces_body(slots_ref, head_ref, tail_ref, acc, rows_q, rows_l):
+    slots = slots_ref.shape[0] // 4
+    label = slots_ref[pl.ds(3, slots, stride=4), :].astype(i32)
+    rows_q[...] = (label >> 7).astype(f32)
+    rows_l[...] = (label & 127).astype(f32)
+    acc[...] = jnp.zeros(acc.shape, f32)
+
+    def store(got):
+        acc[...] += got
+
+    firsts = [ex * PY for ex in range(PX)] + [PLANES]
+    sum_rows(slots_ref, rows_q, rows_l, firsts, CY, 8, store)
+    for c in range(4):
+        for ref, first in ((head_ref, 0), (tail_ref, 8)):
+            total = acc[pl.ds(first + c, PX, stride=16), :]
+            above = acc[pl.ds(16 * PX + c, 1), :]
+            if c < 3:
+                total = total + acc[pl.ds(first + c + 4, PX, stride=16), :]
+                above = above + acc[pl.ds(16 * PX + c + 4, 1), :]
+            ref[c, 0:PX] = total
+            ref[c, PX : PX + 1] = above
+
+
+def deposit_body(slots_ref, total_ref, acc, rows_q, rows_l):
+    slot_places(slots_ref, rows_q, rows_l)
+    acc[...] = jnp.zeros(acc.shape, f32)
+
+    def store(got):
         acc[0] += got[:, :128]
         acc[1] += got[:, 128:]
-        return carry
-
-    lax.fori_loop(0, slots // DEPOSIT_STEP, step, 0)
+
+    sum_rows(slots_ref, rows_q, rows_l, [2 * j for j in range(12)], 1, 16, store)
     for c in range(4):
         for odd in range(2):
             total = acc[odd, pl.ds(c, Q2, stride=8), :]
@@ -186,13 +213,37 @@
                 total = total + acc[odd, pl.ds(c + 4, Q2, stride=8), :]
             total_ref[c, pl.ds(odd, Q2, stride=2)] = total
         total_ref[c, ROWS:PADROWS] = jnp.zeros((PADROWS - ROWS, 128), f32)
-        gather_x_faces(total_ref[c], c, head_ref, tail_ref)
 
 
 def moved_lanes(row, first, count, shift):
     lane = iota(row.shape, 1)
     rolled = pltpu.roll(row, shift % 128, 1)
     return jnp.where((lane >= first) & (lane < first + count), rolled, 0.0)
+
+
+def fold_y_body(total_ref, up_ref, down_ref, out_ref, head_ref, tail_ref):
+    lane = iota((1, 128), 1)
+    edge = lane % PY
+    for c in range(4):
+        out_ref[c] = total_ref[c]
+        out_ref[c, pl.ds(CY, PX, stride=PY)] = (
+            total_ref[c, pl.ds(CY, PX, stride=PY)] + up_ref[c, 0:PX]
+        )
+        out_ref[c, pl.ds(0, PX, stride=PY)] = (
+            total_ref[c, pl.ds(0, PX, stride=PY)] + down_ref[c, 0:PX]
+        )
+        up = pltpu.roll(up_ref[c, PX : PX + 1], CY, 1)
+        down = pltpu.roll(down_ref[c, PX : PX + 1], 128 - CY, 1)
+        above = (
+            total_ref[c, PLANES:ROWS]
+            + jnp.where((edge == CY) & (lane < PLANES), up, 0.0)
+            + jnp.where((edge == 0) & (lane < PLANES), down, 0.0)
+        )
+        out_ref[c, PLANES:ROWS] = above
+        head_ref[c, 0:PY] = out_ref[c, 0:PY]
+        head_ref[c, PY : PY + 1] = above
+        tail_ref[c, 0:PY] = out_ref[c, PLANES - PY : PLANES]
+        tail_ref[c, PY : PY + 1] = above
 
 
 def fold_x_body(total_ref, up_ref, down_ref, out_ref, head_ref, tail_ref):
@@ -205,30 +256,6 @@
             total_ref[c, PLANES:ROWS]
             + moved_lanes(up_ref[c, PY : PY + 1], last, PY, last)
             + moved_lanes(down_ref[c, PY : PY + 1], 0, PY, -last)
-        )
-        head_ref[c, 0:PX] = out_ref[c, pl.ds(0, PX, stride=PY)]
-        head_ref[c, PX : PX + 1] = out_ref[c, PLANES:ROWS]
-        tail_ref[c, 0:PX] = out_ref[c, pl.ds(CY, PX, stride=PY)]
-        tail_ref[c, PX : PX + 1] = out_ref[c, PLANES:ROWS]
-
-
-def fold_y_body(total_ref, up_ref, down_ref, out_ref, head_ref, tail_ref):
-    lane = iota((1, 128), 1)
-    for c in range(4):
-        out_ref[c] = total_ref[c]
-        out_ref[c, pl.ds(CY, PX, stride=PY)] = (
-            total_ref[c, pl.ds(CY, PX, stride=PY)] + up_ref[c, 0:PX]
-        )
-        out_ref[c, pl.ds(0, PX, stride=PY)] = (
-            total_ref[c, pl.ds(0, PX, stride=PY)] + down_ref[c, 0:PX]
-        )
-        up = pltpu.roll(up_ref[c, PX : PX + 1], CY, 1)
-        down = pltpu.roll(down_ref[c, PX : PX + 1], 128 - CY, 1)
-        edge = lane % PY
-        out_ref[c, PLANES:ROWS] = (
-            total_ref[c, PLANES:ROWS]
-            + jnp.where((edge == CY) & (lane < PLANES), up, 0.0)
-            + jnp.where((edge == 0) & (lane < PLANES), down, 0.0)
         )
         total = out_ref[c]
         head_ref[c : c + 1] = column_as_row(total)
@@ -309,7 +336,7 @@
         low = pltpu.roll(column_as_row(mean), 64, 1)
         rim = jnp.where(iota((1, 128), 1) < 64, mean[PLANES:ROWS], low)
         rims.append(jnp.broadcast_to(rim, (8, 128)))
-    units = [jnp.broadcast_to(units_ref[c : c + 1], (8, 128)) for c in range(3)]
+    units = [units_ref[c] for c in range(3)]
 
     def copy(i):
         part = pl.ds(i * SENDERS, SENDERS)
@@ -388,14 +415,13 @@
             for x in (block_target.reshape(1, -1), jnp.transpose(velocity, (1, 0, 2)), cell_index)
         )
     )
-    axes = call(
+    axes, units = call(
         axes_body,
-        shape((PADROWS, 128), f32),
+        [shape((PADROWS, 128), f32), shape((3, 8, 128), f32)],
         in_specs=[smem, vmem],
         scratch_shapes=[pltpu.VMEM((PADROWS, 128), i32)],
         name="axes",
     )(grid_shift, rotation_axis)
-    units = jnp.pad(axis_table(), ((0, 5), (0, 128 - NAX)))
     slots = lax.all_to_all(
         send.reshape(devices, MOST, 4, 128), ("gx", "gy", "gz"), split_axis=0, concat_axis=0, tiled=True
     ).reshape(devices * MOST * 4, 128)
@@ -403,23 +429,27 @@
     x_face = shape((4, 16, 128), f32)
     y_face = shape((4, 8, 128), f32)
     z_face = shape((8, 128), f32)
-    total, head, tail = call(
+    by_slot = pltpu.VMEM((devices * MOST, 128), f32)
+    head, tail = call(
+        deposit_faces_body,
+        [y_face, y_face],
+        scratch_shapes=[pltpu.VMEM((16 * (PX + 1), 128), f32), by_slot, by_slot],
+        name="deposit_faces",
+    )(slots)
+    slots, head, tail = lax.optimization_barrier((slots, head, tail))
+    up, down = both_ways(head, tail, "gy")
+    total = call(
         deposit_body,
-        [total_shape, x_face, x_face],
-        scratch_shapes=[
-            pltpu.VMEM((2, 192, 128), f32),
-            pltpu.VMEM((devices * MOST, 128), f32),
-            pltpu.VMEM((devices * MOST, 128), f32),
-        ],
+        total_shape,
+        scratch_shapes=[pltpu.VMEM((2, 192, 128), f32), by_slot, by_slot],
         name="deposit",
     )(slots)
+    total, head, tail = call(fold_y_body, [total_shape, x_face, x_face], name="fold_y")(
+        total, up, down
+    )
     up, down = both_ways(head, tail, "gx")
-    total, head, tail = call(fold_x_body, [total_shape, y_face, y_face], name="fold_x")(
-        total, up, down
-    )
-    up, down = both_ways(head, tail, "gy")
     up, down, axes, units = lax.optimization_barrier((up, down, axes, units))
-    total, head, tail = call(fold_y_body, [total_shape, z_face, z_face], name="fold_y")(
+    total, head, tail = call(fold_x_body, [total_shape, z_face, z_face], name="fold_x")(
         total, up, down
     )
     up, down = both_ways(head, tail, "gz")

time: 56.9 us -> 55 us (0.967)
  blocking collectives: 0 us -> 27.3 us
  waiting for transfers between devices: 22.8 us -> 3.08 us
  starting transfers between devices: 15.9 us -> 4.71 us
  Pallas kernels: 16.6 us -> 18.8 us
    all_to_all x0 -> x1, blocking collectives: none -> 27.3 us  [shards(): lax.all_to_all(send.reshape(devices, MOST, 4, 128), ('gx', 'gy', 'gz'), s...]
    all_to_all x1 -> x0, waiting for transfers between devices: 16.3 us -> none  [shards(): lax.all_to_all(send.reshape(devices, MOST, 4, 128), ('gx', 'gy', 'gz'), s...]
    all_to_all x1 -> x0, starting transfers between devices: 11.2 us -> none  [shards(): lax.all_to_all(send.reshape(devices, MOST, 4, 128), ('gx', 'gy', 'gz'), s...]
    pallas_call x4 -> x5, Pallas kernels: 6.62 us -> 9.73 us  [the longest x1 5.48 us: shards(): call(deposit_body, total_shape, scratch_shapes=[pltpu.VMEM((2, 192, 128),...]
    ppermute x3, waiting for transfers between devices: 4.75 us -> 2.97 us  [both_ways(): lax.ppermute(tail, axis, [(i, (i + 1) % count) for i in range(count)])]
    ppermute x3, waiting for transfers between devices: 1.77 us -> 0.11 us  [both_ways(): up = lax.ppermute(head, axis, [((i + 1) % count, i) for i in range(count)])]
    pallas_call x1, Pallas kernels: 2.57 us -> 1.67 us  [shards(): call(pack_body, shape((devices * MOST * 4, 128), f32), in_specs=[hbm, hbm...]
  transfers between devices with their start and end apart: 7 -> 6, of which waited for: 5 -> 2; matrix products, arithmetic and copies ran while one was open for 0% -> 0% of each run, Pallas kernels for 11% -> 21%
where the time goes in v5:
time: 55 us; the launch traced here: 54.9 us
  blocking collectives  27.3 us (50%)
  Pallas kernels  18.8 us (34%)
  starting transfers between devices  4.71 us (9%)
  waiting for transfers between devices  3.08 us (6%)
  between operations  0.88 us (2%)
    all_to_all x1, blocking collectives, shards(): lax.all_to_all(send.reshape(devices, MOST, 4, 128), ('gx', 'gy', 'gz'), s...  27.3 us
    pallas_call x1, Pallas kernels, shards(): call(deposit_body, total_shape, scratch_shapes=[pltpu.VMEM((2, 192, 128),...  5.48 us
    pallas_call x1, Pallas kernels, shards(): call(look_body, shape((devices * MOST * 4, 128), f32), scratch_shapes=[pl...  5.18 us
    pallas_call x1, Pallas kernels, shards(): call(deposit_faces_body, [y_face, y_face], scratch_shapes=[pltpu.VMEM((16...  3.14 us
    ppermute x3, starting transfers between devices, both_ways(): lax.ppermute(tail, axis, [(i, (i + 1) % count) for i in range(count)])  2.98 us
    ppermute x3, waiting for transfers between devices, both_ways(): lax.ppermute(tail, axis, [(i, (i + 1) % count) for i in range(count)])  2.97 us
    pallas_call x1, Pallas kernels, shards(): call(turn_body, [shape((MOST, 3, devices, 128), f32), shape((3, CX, CY, C...  2.2 us
    ppermute x3, starting transfers between devices, both_ways(): up = lax.ppermute(head, axis, [((i + 1) % count, i) for i in range(count)])  1.73 us
  transfers between devices with their start and end apart: 6, of which 2 were waited for; matrix products, arithmetic and copies ran while one was open for 0% of the time, Pallas kernels for 21%

profile of v5, /device:TPU:0, one launch (start us, length us, event | category | flops | bytes accessed | tf_op | source)
XLA Modules:
  0.0 54.9 jit_solution(14760406395260738882)
XLA Ops:
  0.6 1.7 %pack.1 = f32[1536,128]{1,0:T(8,128)S(1)} custom-call(s32[1,256]{1,0:T(1,128)} %bitcast.13, f32[3,256,128]{2,1,0:T(8,128)} %bitcast.12, s32[256,128]{1,0:T(8,128)} %index_hbm.1), custom_call_target="tpu_custom_call" | custom-call | tf_op jit(solution)/shard_map/pack/pallas_call | solution.py:401
  2.3 27.3 %all_to_all.5 = f32[128,3,4,128]{3,2,1,0:T(4,128)S(1)} all-to-all(f32[128,3,4,128]{3,2,1,0:T(4,128)S(1)} %bitcast.11), channel_id=1, replica_groups=mesh['gx'=8,'gy'=4,'gz'=4] {'gx','gy','gz'}, dimensions={0} | all-to-all | bytes 1572864 | tf_op jit(solution)/shard_map/all_to_all | solution.py:425
  29.6 3.1 %deposit_faces.1 = (f32[4,8,128]{2,1,0:T(8,128)S(1)}, f32[4,8,128]{2,1,0:T(8,128)S(1)}) custom-call(f32[1536,128]{1,0:T(8,128)S(1)} %bitcast.7), custom_call_target="tpu_custom_call" | custom-call | tf_op jit(solution)/shard_map/deposit_faces/pallas_call | solution.py:433
  32.8 0.0 copy-start
  32.8 0.4 collective-permute-start
  33.2 1.7 %collective-permute-start.1 = (f32[4,8,128]{2,1,0:T(8,128)S(1)}, f32[4,8,128]{2,1,0:T(8,128)S(1)}, u32[]{:S(2)}, u32[]{:S(2)}) collective-permute-start(f32[4,8,128]{2,1,0:T(8,128)S(1)} %get-tuple-element.25), channel_id=1, source_target_pairs={{0,4},{4,8},{8,12},{12,0},{1,5},{5,9},{9,13},{13,1},{2,6},{6,10},{... | collective-permute-start | bytes 49160 | tf_op jit(solution)/shard_map/ppermute | solution.py:390
  34.9 5.5 %deposit.1.total_ref = f32[4,48,128]{2,1,0:T(8,128)S(1)} custom-call(f32[1536,128]{1,0:T(8,128)S(1)} %bitcast.8), custom_call_target="tpu_custom_call" | custom-call | tf_op jit(solution)/shard_map/deposit/pallas_call | solution.py:441
  40.4 0.0 collective-permute-done.up_ref
  40.4 0.0 collective-permute-done.1.down_ref
  40.4 0.1 fold_y.1
  40.5 0.0 copy-start.1
  40.5 0.0 collective-permute-start.2
  40.5 0.5 collective-permute-start.3
  41.0 0.0 copy-done
  41.0 0.1 copy-done.1
  41.1 0.9 %axes.1 = (f32[48,128]{1,0:T(8,128)S(1)}, f32[3,8,128]{2,1,0:T(8,128)S(1)}) custom-call(s32[3]{0:T(128)S(1)} %copy-done.1, s32[32,32,32]{2,1,0:T(8,128)S(1)} %copy-done), custom_call_target="tpu_custom_call" | custom-call | tf_op jit(solution)/shard_map/axes/pallas_call | solution.py:418
  42.0 0.1 collective-permute-done.2.up_ref
  42.1 3.0 %collective-permute-done.3.down_ref = f32[4,16,128]{2,1,0:T(8,128)S(1)} collective-permute-done((f32[4,16,128]{2,1,0:T(8,128)S(1)}, f32[4,16,128]{2,1,0:T(8,128)S(1)}, u32[]{:S(2)}, u32[]{:S(2)}) %collective-permute-start.3) | collective-permute-done | bytes 32800 | tf_op jit(solution)/shard_map/ppermute | solution.py:390
  45.0 0.2 fold_x.1
  45.2 1.3 %collective-permute-start.4 = (f32[8,128]{1,0:T(8,128)S(1)}, f32[8,128]{1,0:T(8,128)S(1)}, u32[]{:S(2)}, u32[]{:S(2)}) collective-permute-start(f32[8,128]{1,0:T(8,128)S(1)} %get-tuple-element.34), channel_id=1, source_target_pairs={{1,0},{2,1},{3,2},{0,3},{5,4},{6,5},{7,6},{4,7},{9,8},{10,9},{11,1... | collective-permute-start | bytes 12296 | tf_op jit(solution)/shard_map/ppermute | solution.py:389
  46.5 0.8 %collective-permute-start.5 = (f32[8,128]{1,0:T(8,128)S(1)}, f32[8,128]{1,0:T(8,128)S(1)}, u32[]{:S(2)}, u32[]{:S(2)}) collective-permute-start(f32[8,128]{1,0:T(8,128)S(1)} %get-tuple-element.35), channel_id=1, source_target_pairs={{0,1},{1,2},{2,3},{3,0},{4,5},{5,6},{6,7},{7,4},{8,9},{9,10},{10,1... | collective-permute-start | bytes 12296 | tf_op jit(solution)/shard_map/ppermute | solution.py:390
  47.3 5.2 %look.1.found = f32[1536,128]{1,0:T(8,128)S(1)} custom-call(f32[4,48,128]{2,1,0:T(8,128)S(1)} %get-tuple-element.33.total_ref, f32[48,128]{1,0:T(8,128)S(1)} %get-tuple-element.37.axes_ref, f32[1536,128]{1,0:T(8,128)S(1)} %bitcast.9), custom_call_target="tpu_custom_call" | custom-call | tf_op jit(solution)/shard_map/look/pallas_call | solution.py:456
  52.5 0.0 collective-permute-done.4.up_ref
  52.5 0.0 collective-permute-done.5.down_ref
  52.5 2.2 %turn.1 = (f32[3,3,128,128]{3,2,1,0:T(8,128)}, f32[3,4,8,128]{3,2,1,0:T(8,128)}) custom-call(f32[4,48,128]{2,1,0:T(8,128)S(1)} %get-tuple-element.33.total_ref, f32[8,128]{1,0:T(8,128)S(1)} %collective-permute-done.4.up_ref, f32[8,128]{1,0:T(8,128)S(1)} %collective-permute-done.5.down_ref, f32[3,8,128]{2,1,0:T(8,128)S(1)} %get-tuple-element.36.units_ref, ...), custom_call_target="tpu_custom_call" | custom-call | tf_op jit(solution)/shard_map/turn/pallas_call | solution.py:467
Async XLA Ops:
  32.8 8.2 %copy-start = (s32[32,32,32]{2,1,0:T(8,128)S(1)}, s32[32,32,32]{2,1,0:T(8,128)}, u32[]{:S(2)}) copy-start(s32[32,32,32]{2,1,0:T(8,128)} %rotation_ref.1) | copy-start | bytes 393220
  32.8 7.6 %collective-permute-start = (f32[4,8,128]{2,1,0:T(8,128)S(1)}, f32[4,8,128]{2,1,0:T(8,128)S(1)}, u32[]{:S(2)}, u32[]{:S(2)}) collective-permute-start(f32[4,8,128]{2,1,0:T(8,128)S(1)} %get-tuple-element.24), channel_id=1, source_target_pairs={{4,0},{8,4},{12,8},{0,12},{5,1},{9,5},{13,9},{1,13},{6,2},{10,6},{... | collective-permute-start | bytes 49160 | tf_op jit(solution)/shard_map/ppermute | solution.py:389
  33.2 7.2 %collective-permute-start.1 = (f32[4,8,128]{2,1,0:T(8,128)S(1)}, f32[4,8,128]{2,1,0:T(8,128)S(1)}, u32[]{:S(2)}, u32[]{:S(2)}) collective-permute-start(f32[4,8,128]{2,1,0:T(8,128)S(1)} %get-tuple-element.25), channel_id=1, source_target_pairs={{0,4},{4,8},{8,12},{12,0},{1,5},{5,9},{9,13},{13,1},{2,6},{6,10},{... | collective-permute-start | bytes 49160 | tf_op jit(solution)/shard_map/ppermute | solution.py:390
  40.5 0.7 %copy-start.1 = (s32[3]{0:T(128)S(1)}, s32[3]{0:T(128)}, u32[]{:S(2)}) copy-start(s32[3]{0:T(128)} %shift_ref.1) | copy-start | bytes 40
  40.5 1.6 %collective-permute-start.2 = (f32[4,16,128]{2,1,0:T(8,128)S(1)}, f32[4,16,128]{2,1,0:T(8,128)S(1)}, u32[]{:S(2)}, u32[]{:S(2)}) collective-permute-start(f32[4,16,128]{2,1,0:T(8,128)S(1)} %get-tuple-element.27), channel_id=1, source_target_pairs={{16,0},{32,16},{48,32},{64,48},{80,64},{96,80},{112,96},{0,112},{1... | collective-permute-start | bytes 98312 | tf_op jit(solution)/shard_map/ppermute | solution.py:389
  40.5 4.6 %collective-permute-start.3 = (f32[4,16,128]{2,1,0:T(8,128)S(1)}, f32[4,16,128]{2,1,0:T(8,128)S(1)}, u32[]{:S(2)}, u32[]{:S(2)}) collective-permute-start(f32[4,16,128]{2,1,0:T(8,128)S(1)} %get-tuple-element.28), channel_id=1, source_target_pairs={{0,16},{16,32},{32,48},{48,64},{64,80},{80,96},{96,112},{112,0},{1... | collective-permute-start | bytes 98312 | tf_op jit(solution)/shard_map/ppermute | solution.py:390
  45.2 7.3 %collective-permute-start.4 = (f32[8,128]{1,0:T(8,128)S(1)}, f32[8,128]{1,0:T(8,128)S(1)}, u32[]{:S(2)}, u32[]{:S(2)}) collective-permute-start(f32[8,128]{1,0:T(8,128)S(1)} %get-tuple-element.34), channel_id=1, source_target_pairs={{1,0},{2,1},{3,2},{0,3},{5,4},{6,5},{7,6},{4,7},{9,8},{10,9},{11,1... | collective-permute-start | bytes 12296 | tf_op jit(solution)/shard_map/ppermute | solution.py:389
  46.5 6.0 %collective-permute-start.5 = (f32[8,128]{1,0:T(8,128)S(1)}, f32[8,128]{1,0:T(8,128)S(1)}, u32[]{:S(2)}, u32[]{:S(2)}) collective-permute-start(f32[8,128]{1,0:T(8,128)S(1)} %get-tuple-element.35), channel_id=1, source_target_pairs={{0,1},{1,2},{2,3},{3,0},{4,5},{5,6},{6,7},{7,4},{8,9},{9,10},{10,1... | collective-permute-start | bytes 12296 | tf_op jit(solution)/shard_map/ppermute | solution.py:390

commit v6 on v5

--- a/solution.py
+++ b/solution.py
@@ -273,15 +273,38 @@
     return rows[0]
 
 
-def look_body(total_ref, axes_ref, slots_ref, found, cells, wide, rows_q, rows_l):
+INNER = [ex * PY + ey for ex in range(1, CX) for ey in range(1, CY)]
+OUTER = (
+    list(range(PY))
+    + list(range(PLANES - PY, PLANES))
+    + [ex * PY + ey for ex in range(1, CX) for ey in (0, CY)]
+    + [PLANES]
+)
+
+
+def position(row, inner):
+    ex = (row * 57) >> 9
+    ey = row - ex * PY
+    is_inner = (ex >= 1) & (ex < CX) & (ey >= 1) & (ey < CY)
+    if inner:
+        return (ex - 1) * (CY - 1) + ey - 1, is_inner
+    side = 2 * PY + 2 * (ex - 1) + jnp.where(ey == CY, 1, 0)
+    place = jnp.where(ex == 0, ey, jnp.where(ex == CX, PY + ey, side))
+    place = jnp.where(row == PLANES, len(OUTER) - 1, place)
+    return place, jnp.logical_not(is_inner) & (row <= PLANES)
+
+
+def look(total_ref, axes_ref, slots_ref, found, cells, wide, rows_q, rows_l, inner, earlier, after):
     slots = slots_ref.shape[0] // 4
+    listed = INNER if inner else OUTER
+    folded = (len(listed) + 1) // 2
     count = jnp.maximum(total_ref[3], 1.0)
     wide[...] = jnp.zeros(wide.shape, f32)
 
     def tabulate(value, line):
         cells[...] = value
-        for odd in range(2):
-            wide[odd, pl.ds(line, Q2, stride=8), :] = cells[pl.ds(odd, Q2, stride=2)]
+        for p, row in enumerate(listed):
+            wide[p & 1, pl.ds(8 * (p >> 1) + line, 1), :] = cells[pl.ds(row, 1), :]
 
     for c in range(3):
         mean = total_ref[c] / count
@@ -290,7 +313,10 @@
         tabulate(mean - high, c + 4)
     tabulate(axes_ref[...], 3)
     table = jnp.concatenate([wide[0], wide[1]], axis=1).astype(bf16)
-    slot_places(slots_ref, rows_q, rows_l)
+    label = slots_ref[pl.ds(3, slots, stride=4), :].astype(i32)
+    place, here = position(label >> 7, inner)
+    rows_q[...] = place >> 1
+    rows_l[...] = jnp.where(here, (place & 1) * 128 + (label & 127), 512).astype(f32)
     sub8 = iota((8, 128), 0)
     for k in range(slots // 2):
         pair = [2 * k, 2 * k + 1]
@@ -299,18 +325,53 @@
         got = []
         for h in range(2):
             q = jnp.broadcast_to(rows_q[pl.ds(pair[h], 1), :], (8, 128))
-            bits = [(q & (1 << b)) != 0 for b in range(5)]
-            lines = [read[8 * j : 8 * j + 8, 128 * h : 128 * h + 128] for j in range(Q2)]
+            bits = [(q & (1 << b)) != 0 for b in range(4)]
+            lines = [read[8 * j : 8 * j + 8, 128 * h : 128 * h + 128] for j in range(folded)]
             value = select_row(lines, bits)
             got.append(value + pltpu.roll(value, 4, 0))
-        found[pl.ds(8 * k, 8), :] = jnp.where(sub8 < 4, got[0], got[1])
+        value = jnp.where(sub8 < 4, got[0], got[1])
+        if earlier is not None:
+            value = value + earlier[pl.ds(8 * k, 8), :]
+        found[pl.ds(8 * k, 8), :] = value
+        if after is not None:
+            after(k)
+
+
+def look_inner_body(total_ref, axes_ref, slots_ref, found, cells, wide, rows_q, rows_l):
+    look(
+        total_ref, axes_ref, slots_ref, found, cells, wide, rows_q, rows_l, True, None, None
+    )
+
+
+def look_outer_body(
+    total_ref, axes_ref, units_ref, slots_ref, earlier, found, normal_ref, cells, wide, rows_q, rows_l
+):
+    units = [units_ref[c] for c in range(3)]
+    pairs = 4 * MOST
+
+    def normals(g):
+        for rank in range(MOST):
+            place = (g * 8 * MOST + rank) * 4 + 3
+            which = found[pl.ds(place, 8, stride=4 * MOST), :].astype(i32)
+            for c in range(3):
+                normal_ref[rank, c, pl.ds(8 * g, 8), :] = jnp.take_along_axis(
+                    units[c], which, axis=1
+                )
+
+    def after(k):
+        if k % pairs == pairs - 1:
+            normals(k // pairs)
+
+    look(
+        total_ref, axes_ref, slots_ref, found, cells, wide, rows_q, rows_l, False, earlier, after
+    )
 
 
 SENDERS = 32
 
 
 def turn_body(
-    total_ref, up_ref, down_ref, units_ref, slots_ref, found, out_hbm, flow_ref, out_ref, sems
+    total_ref, up_ref, down_ref, normal_ref, slots_ref, found, out_hbm, flow_ref, out_ref, sems
 ):
     devices = out_ref.shape[2]
     shape = (PADROWS, 128)
@@ -336,7 +397,6 @@
         low = pltpu.roll(column_as_row(mean), 64, 1)
         rim = jnp.where(iota((1, 128), 1) < 64, mean[PLANES:ROWS], low)
         rims.append(jnp.broadcast_to(rim, (8, 128)))
-    units = [units_ref[c] for c in range(3)]
 
     def copy(i):
         part = pl.ds(i * SENDERS, SENDERS)
@@ -355,8 +415,7 @@
                 above = q == PLANES
                 below = (l == 0) & (q < PLANES)
                 rim_lane = jnp.where(above, l, (q + 64) & 127)
-                which = found[pl.ds(place + 3, 8, stride=12), :].astype(i32)
-                n = [jnp.take_along_axis(units[c], which, axis=1) for c in range(3)]
+                n = [normal_ref[rank, c, pl.ds(source, 8), :] for c in range(3)]
                 u = [
                     jnp.where(
                         above | below,
@@ -448,22 +507,30 @@
         total, up, down
     )
     up, down = both_ways(head, tail, "gx")
-    up, down, axes, units = lax.optimization_barrier((up, down, axes, units))
+    found_shape = shape((devices * MOST * 4, 128), f32)
+
+    def look_scratch(listed):
+        return [
+            pltpu.VMEM((PADROWS, 128), f32),
+            pltpu.VMEM((2, (len(listed) + 1) // 2 * 8, 128), f32),
+            pltpu.VMEM((devices * MOST, 128), i32),
+            by_slot,
+        ]
+
+    found = call(
+        look_inner_body, found_shape, scratch_shapes=look_scratch(INNER), name="look_inner"
+    )(total, axes, slots)
+    up, down, found, axes, units = lax.optimization_barrier((up, down, found, axes, units))
     total, head, tail = call(fold_x_body, [total_shape, z_face, z_face], name="fold_x")(
         total, up, down
     )
     up, down = both_ways(head, tail, "gz")
-    found = call(
-        look_body,
-        shape((devices * MOST * 4, 128), f32),
-        scratch_shapes=[
-            pltpu.VMEM((PADROWS, 128), f32),
-            pltpu.VMEM((2, Q2 * 8, 128), f32),
-            pltpu.VMEM((devices * MOST, 128), i32),
-            pltpu.VMEM((devices * MOST, 128), f32),
-        ],
-        name="look",
-    )(total, axes, slots)
+    found, normal = call(
+        look_outer_body,
+        [found_shape, shape((MOST, 3, devices, 128), f32)],
+        scratch_shapes=look_scratch(OUTER),
+        name="look_outer",
+    )(total, axes, units, slots, found)
     updated, cell_flow = call(
         turn_body,
         [shape((MOST, 3, devices, 128), f32), shape((3, CX, CY, CZ), f32)],
@@ -473,7 +540,7 @@
             pltpu.SemaphoreType.DMA((devices // SENDERS,)),
         ],
         name="turn",
-    )(total, up, down, units, slots, found)
+    )(total, up, down, normal, slots, found)
     return jnp.transpose(updated, (2, 0, 1, 3))[None], cell_flow
 
 

time: 55 us -> 56.6 us (1.029); the launches traced: 54.9 us -> 55.8 us
  Pallas kernels: 18.8 us -> 22.7 us
  waiting for transfers between devices: 3.08 us -> 0.02 us
    pallas_call x1 -> x2, Pallas kernels: 5.18 us -> 9.26 us  [the longest x1 4.74 us: shards(): call(look_outer_body, [found_shape, shape((MOST, 3, devices, 128), f32)],...]
    ppermute x3, waiting for transfers between devices: 2.97 us -> 0.01 us  [both_ways(): lax.ppermute(tail, axis, [(i, (i + 1) % count) for i in range(count)])]
  transfers between devices with their start and end apart: 6 -> 6, of which waited for: 2 -> 0; matrix products, arithmetic and copies ran while one was open for 0% -> 0% of each run, Pallas kernels for 21% -> 28%
where the time goes in v6:
time: 56.6 us; the launch traced here: 55.8 us
  blocking collectives  27.3 us (48%)
  Pallas kernels  22.7 us (40%)
  starting transfers between devices  4.71 us (8%)
  between operations  0.89 us (2%)
    all_to_all x1, blocking collectives, shards(): lax.all_to_all(send.reshape(devices, MOST, 4, 128), ('gx', 'gy', 'gz'), s...  27.3 us
    pallas_call x1, Pallas kernels, shards(): call(deposit_body, total_shape, scratch_shapes=[pltpu.VMEM((2, 192, 128),...  5.49 us
    pallas_call x1, Pallas kernels, shards(): call(look_outer_body, [found_shape, shape((MOST, 3, devices, 128), f32)],...  4.74 us
    pallas_call x1, Pallas kernels, shards(): call(look_inner_body, found_shape, scratch_shapes=look_scratch(INNER), na...  4.52 us
    pallas_call x1, Pallas kernels, shards(): call(deposit_faces_body, [y_face, y_face], scratch_shapes=[pltpu.VMEM((16...  3.15 us
    ppermute x3, starting transfers between devices, both_ways(): lax.ppermute(tail, axis, [(i, (i + 1) % count) for i in range(count)])  3.01 us
    pallas_call x1, Pallas kernels, shards(): call(turn_body, [shape((MOST, 3, devices, 128), f32), shape((3, CX, CY, C...  2.04 us
    ppermute x3, starting transfers between devices, both_ways(): up = lax.ppermute(head, axis, [((i + 1) % count, i) for i in range(count)])  1.7 us
  transfers between devices with their start and end apart: 6, of which 0 were waited for; matrix products, arithmetic and copies ran while one was open for 0% of the time, Pallas kernels for 28%

profile of v6, /device:TPU:0, one launch (start us, length us, event | category | flops | bytes accessed | tf_op | source)
XLA Modules:
  0.0 55.8 jit_solution(7284449206662081153)
XLA Ops:
  0.6 1.7 %pack.1 = f32[1536,128]{1,0:T(8,128)S(1)} custom-call(s32[1,256]{1,0:T(1,128)} %bitcast.14, f32[3,256,128]{2,1,0:T(8,128)} %bitcast.13, s32[256,128]{1,0:T(8,128)} %index_hbm.1), custom_call_target="tpu_custom_call" | custom-call | tf_op jit(solution)/shard_map/pack/pallas_call | solution.py:460
  2.3 27.3 %all_to_all.5 = f32[128,3,4,128]{3,2,1,0:T(4,128)S(1)} all-to-all(f32[128,3,4,128]{3,2,1,0:T(4,128)S(1)} %bitcast.12), channel_id=1, replica_groups=mesh['gx'=8,'gy'=4,'gz'=4] {'gx','gy','gz'}, dimensions={0} | all-to-all | bytes 1572864 | tf_op jit(solution)/shard_map/all_to_all | solution.py:484
  29.6 3.1 %deposit_faces.1 = (f32[4,8,128]{2,1,0:T(8,128)S(1)}, f32[4,8,128]{2,1,0:T(8,128)S(1)}) custom-call(f32[1536,128]{1,0:T(8,128)S(1)} %bitcast.7), custom_call_target="tpu_custom_call" | custom-call | tf_op jit(solution)/shard_map/deposit_faces/pallas_call | solution.py:492
  32.8 0.0 copy-start
  32.8 0.4 collective-permute-start
  33.2 1.7 %collective-permute-start.1 = (f32[4,8,128]{2,1,0:T(8,128)S(1)}, f32[4,8,128]{2,1,0:T(8,128)S(1)}, u32[]{:S(2)}, u32[]{:S(2)}) collective-permute-start(f32[4,8,128]{2,1,0:T(8,128)S(1)} %get-tuple-element.28), channel_id=1, source_target_pairs={{0,4},{4,8},{8,12},{12,0},{1,5},{5,9},{9,13},{13,1},{2,6},{6,10},{... | collective-permute-start | bytes 49160 | tf_op jit(solution)/shard_map/ppermute | solution.py:449
  34.9 5.5 %deposit.1.total_ref = f32[4,48,128]{2,1,0:T(8,128)S(1)} custom-call(f32[1536,128]{1,0:T(8,128)S(1)} %bitcast.8), custom_call_target="tpu_custom_call" | custom-call | tf_op jit(solution)/shard_map/deposit/pallas_call | solution.py:500
  40.4 0.0 collective-permute-done.up_ref
  40.4 0.0 collective-permute-done.1.down_ref
  40.4 0.1 fold_y.1
  40.5 0.0 copy-start.1
  40.5 0.0 collective-permute-start.2
  40.5 0.5 collective-permute-start.3
  41.0 0.0 copy-done
  41.0 0.1 copy-done.1
  41.1 0.9 %axes.1 = (f32[48,128]{1,0:T(8,128)S(1)}, f32[3,8,128]{2,1,0:T(8,128)S(1)}) custom-call(s32[3]{0:T(128)S(1)} %copy-done.1, s32[32,32,32]{2,1,0:T(8,128)S(1)} %copy-done), custom_call_target="tpu_custom_call" | custom-call | tf_op jit(solution)/shard_map/axes/pallas_call | solution.py:477
  42.0 4.5 %look_inner.1.earlier = f32[1536,128]{1,0:T(8,128)S(1)} custom-call(f32[4,48,128]{2,1,0:T(8,128)S(1)} %get-tuple-element.29.total_ref, f32[48,128]{1,0:T(8,128)S(1)} %get-tuple-element.39.axes_ref, f32[1536,128]{1,0:T(8,128)S(1)} %bitcast.9), custom_call_target="tpu_custom_call" | custom-call | tf_op jit(solution)/shard_map/look_inner/pallas_call | solution.py:520
  46.5 0.0 collective-permute-done.2.up_ref
  46.5 0.0 collective-permute-done.3.down_ref
  46.5 0.2 fold_x.1
  46.7 1.3 %collective-permute-start.4 = (f32[8,128]{1,0:T(8,128)S(1)}, f32[8,128]{1,0:T(8,128)S(1)}, u32[]{:S(2)}, u32[]{:S(2)}) collective-permute-start(f32[8,128]{1,0:T(8,128)S(1)} %get-tuple-element.37), channel_id=1, source_target_pairs={{1,0},{2,1},{3,2},{0,3},{5,4},{6,5},{7,6},{4,7},{9,8},{10,9},{11,1... | collective-permute-start | bytes 12296 | tf_op jit(solution)/shard_map/ppermute | solution.py:448
  48.0 0.8 %collective-permute-start.5 = (f32[8,128]{1,0:T(8,128)S(1)}, f32[8,128]{1,0:T(8,128)S(1)}, u32[]{:S(2)}, u32[]{:S(2)}) collective-permute-start(f32[8,128]{1,0:T(8,128)S(1)} %get-tuple-element.38), channel_id=1, source_target_pairs={{0,1},{1,2},{2,3},{3,0},{4,5},{5,6},{6,7},{7,4},{8,9},{9,10},{10,1... | collective-permute-start | bytes 12296 | tf_op jit(solution)/shard_map/ppermute | solution.py:449
  48.8 4.7 %look_outer.1 = (f32[1536,128]{1,0:T(8,128)S(1)}, f32[3,3,128,128]{3,2,1,0:T(8,128)S(1)}) custom-call(f32[4,48,128]{2,1,0:T(8,128)S(1)} %get-tuple-element.36.total_ref, f32[48,128]{1,0:T(8,128)S(1)} %get-tuple-element.39.axes_ref, f32[3,8,128]{2,1,0:T(8,128)S(1)} %get-tuple-element.40.units_ref, f32[1536,128]{1,0:T(8,128)S(1)} %bitcast.10, ...), custom_call_target="tpu_custom_call" | custom-call | tf_op jit(solution)/shard_map/look_outer/pallas_call | solution.py:528
  53.5 0.0 collective-permute-done.4.up_ref
  53.6 0.0 collective-permute-done.5.down_ref
  53.6 2.0 %turn.1 = (f32[3,3,128,128]{3,2,1,0:T(8,128)}, f32[3,4,8,128]{3,2,1,0:T(8,128)}) custom-call(f32[4,48,128]{2,1,0:T(8,128)S(1)} %get-tuple-element.36.total_ref, f32[8,128]{1,0:T(8,128)S(1)} %collective-permute-done.4.up_ref, f32[8,128]{1,0:T(8,128)S(1)} %collective-permute-done.5.down_ref, f32[3,3,128,128]{3,2,1,0:T(8,128)S(1)} %get-tuple-element.42.normal_ref, ...), custom_call_target="tpu_custom_call" | custom-call | tf_op jit(solution)/shard_map/turn/pallas_call | solution.py:534
Async XLA Ops:
  32.8 8.2 %copy-start = (s32[32,32,32]{2,1,0:T(8,128)S(1)}, s32[32,32,32]{2,1,0:T(8,128)}, u32[]{:S(2)}) copy-start(s32[32,32,32]{2,1,0:T(8,128)} %rotation_ref.1) | copy-start | bytes 393220
  32.8 7.6 %collective-permute-start = (f32[4,8,128]{2,1,0:T(8,128)S(1)}, f32[4,8,128]{2,1,0:T(8,128)S(1)}, u32[]{:S(2)}, u32[]{:S(2)}) collective-permute-start(f32[4,8,128]{2,1,0:T(8,128)S(1)} %get-tuple-element.27), channel_id=1, source_target_pairs={{4,0},{8,4},{12,8},{0,12},{5,1},{9,5},{13,9},{1,13},{6,2},{10,6},{... | collective-permute-start | bytes 49160 | tf_op jit(solution)/shard_map/ppermute | solution.py:448
  33.2 7.2 %collective-permute-start.1 = (f32[4,8,128]{2,1,0:T(8,128)S(1)}, f32[4,8,128]{2,1,0:T(8,128)S(1)}, u32[]{:S(2)}, u32[]{:S(2)}) collective-permute-start(f32[4,8,128]{2,1,0:T(8,128)S(1)} %get-tuple-element.28), channel_id=1, source_target_pairs={{0,4},{4,8},{8,12},{12,0},{1,5},{5,9},{9,13},{13,1},{2,6},{6,10},{... | collective-permute-start | bytes 49160 | tf_op jit(solution)/shard_map/ppermute | solution.py:449
  40.5 0.7 %copy-start.1 = (s32[3]{0:T(128)S(1)}, s32[3]{0:T(128)}, u32[]{:S(2)}) copy-start(s32[3]{0:T(128)} %shift_ref.1) | copy-start | bytes 40
  40.5 6.0 %collective-permute-start.2 = (f32[4,16,128]{2,1,0:T(8,128)S(1)}, f32[4,16,128]{2,1,0:T(8,128)S(1)}, u32[]{:S(2)}, u32[]{:S(2)}) collective-permute-start(f32[4,16,128]{2,1,0:T(8,128)S(1)} %get-tuple-element.30), channel_id=1, source_target_pairs={{16,0},{32,16},{48,32},{64,48},{80,64},{96,80},{112,96},{0,112},{1... | collective-permute-start | bytes 98312 | tf_op jit(solution)/shard_map/ppermute | solution.py:448
  40.5 6.0 %collective-permute-start.3 = (f32[4,16,128]{2,1,0:T(8,128)S(1)}, f32[4,16,128]{2,1,0:T(8,128)S(1)}, u32[]{:S(2)}, u32[]{:S(2)}) collective-permute-start(f32[4,16,128]{2,1,0:T(8,128)S(1)} %get-tuple-element.31), channel_id=1, source_target_pairs={{0,16},{16,32},{32,48},{48,64},{64,80},{80,96},{96,112},{112,0},{1... | collective-permute-start | bytes 98312 | tf_op jit(solution)/shard_map/ppermute | solution.py:449
  46.7 6.8 %collective-permute-start.4 = (f32[8,128]{1,0:T(8,128)S(1)}, f32[8,128]{1,0:T(8,128)S(1)}, u32[]{:S(2)}, u32[]{:S(2)}) collective-permute-start(f32[8,128]{1,0:T(8,128)S(1)} %get-tuple-element.37), channel_id=1, source_target_pairs={{1,0},{2,1},{3,2},{0,3},{5,4},{6,5},{7,6},{4,7},{9,8},{10,9},{11,1... | collective-permute-start | bytes 12296 | tf_op jit(solution)/shard_map/ppermute | solution.py:448
  48.0 5.6 %collective-permute-start.5 = (f32[8,128]{1,0:T(8,128)S(1)}, f32[8,128]{1,0:T(8,128)S(1)}, u32[]{:S(2)}, u32[]{:S(2)}) collective-permute-start(f32[8,128]{1,0:T(8,128)S(1)} %get-tuple-element.38), channel_id=1, source_target_pairs={{0,1},{1,2},{2,3},{3,0},{4,5},{5,6},{6,7},{7,4},{8,9},{9,10},{10,1... | collective-permute-start | bytes 12296 | tf_op jit(solution)/shard_map/ppermute | solution.py:449

commit v7 on v5

--- a/solution.py
+++ b/solution.py
@@ -273,7 +273,9 @@
     return rows[0]
 
 
-def look_body(total_ref, axes_ref, slots_ref, found, cells, wide, rows_q, rows_l):
+def look_body(
+    total_ref, axes_ref, units_ref, slots_ref, found, normal_ref, cells, wide, rows_q, rows_l
+):
     slots = slots_ref.shape[0] // 4
     count = jnp.maximum(total_ref[3], 1.0)
     wide[...] = jnp.zeros(wide.shape, f32)
@@ -304,13 +306,22 @@
             value = select_row(lines, bits)
             got.append(value + pltpu.roll(value, 4, 0))
         found[pl.ds(8 * k, 8), :] = jnp.where(sub8 < 4, got[0], got[1])
+        if (k + 1) % (4 * MOST) == 0:
+            g = k // (4 * MOST)
+            for rank in range(MOST):
+                which = found[pl.ds((g * 8 * MOST + rank) * 4 + 3, 8, stride=4 * MOST), :]
+                for c in range(3):
+                    normal_ref[rank, c, pl.ds(8 * g, 8), :] = jnp.take_along_axis(
+                        units_ref[c], which.astype(i32), axis=1
+                    )
 
 
 SENDERS = 32
 
 
 def turn_body(
-    total_ref, up_ref, down_ref, units_ref, slots_ref, found, out_hbm, flow_ref, out_ref, sems
+    total_ref, up_ref, down_ref, normal_ref, slots_ref, found, out_hbm, flow_hbm,
+    out_ref, flow_ref, sems
 ):
     devices = out_ref.shape[2]
     shape = (PADROWS, 128)
@@ -336,7 +347,9 @@
         low = pltpu.roll(column_as_row(mean), 64, 1)
         rim = jnp.where(iota((1, 128), 1) < 64, mean[PLANES:ROWS], low)
         rims.append(jnp.broadcast_to(rim, (8, 128)))
-    units = [units_ref[c] for c in range(3)]
+    parts = devices // SENDERS
+    flow_copy = pltpu.make_async_copy(flow_ref, flow_hbm, sems.at[parts])
+    flow_copy.start()
 
     def copy(i):
         part = pl.ds(i * SENDERS, SENDERS)
@@ -344,7 +357,7 @@
             out_ref.at[:, :, part, :], out_hbm.at[:, :, part, :], sems.at[i]
         )
 
-    for i in range(devices // SENDERS):
+    for i in range(parts):
         for rank in range(MOST):
             for k in range(SENDERS // 8):
                 source = i * SENDERS + 8 * k
@@ -355,8 +368,7 @@
                 above = q == PLANES
                 below = (l == 0) & (q < PLANES)
                 rim_lane = jnp.where(above, l, (q + 64) & 127)
-                which = found[pl.ds(place + 3, 8, stride=12), :].astype(i32)
-                n = [jnp.take_along_axis(units[c], which, axis=1) for c in range(3)]
+                n = [normal_ref[rank, c, pl.ds(source, 8), :] for c in range(3)]
                 u = [
                     jnp.where(
                         above | below,
@@ -380,8 +392,9 @@
                         + n[c] * inner * (1.0 - angle_cosine)
                     )
         copy(i).start()
-    for i in range(devices // SENDERS):
+    for i in range(parts):
         copy(i).wait()
+    flow_copy.wait()
 
 
 def both_ways(head, tail, axis):
@@ -453,9 +466,9 @@
         total, up, down
     )
     up, down = both_ways(head, tail, "gz")
-    found = call(
+    found, normal = call(
         look_body,
-        shape((devices * MOST * 4, 128), f32),
+        [shape((devices * MOST * 4, 128), f32), shape((MOST, 3, devices, 128), f32)],
         scratch_shapes=[
             pltpu.VMEM((PADROWS, 128), f32),
             pltpu.VMEM((2, Q2 * 8, 128), f32),
@@ -463,17 +476,18 @@
             pltpu.VMEM((devices * MOST, 128), f32),
         ],
         name="look",
-    )(total, axes, slots)
+    )(total, axes, units, slots)
     updated, cell_flow = call(
         turn_body,
         [shape((MOST, 3, devices, 128), f32), shape((3, CX, CY, CZ), f32)],
-        out_specs=[hbm, vmem],
+        out_specs=[hbm, hbm],
         scratch_shapes=[
             pltpu.VMEM((MOST, 3, devices, 128), f32),
-            pltpu.SemaphoreType.DMA((devices // SENDERS,)),
+            pltpu.VMEM((3, CX, CY, CZ), f32),
+            pltpu.SemaphoreType.DMA((devices // SENDERS + 1,)),
         ],
         name="turn",
-    )(total, up, down, units, slots, found)
+    )(total, up, down, normal, slots, found)
     return jnp.transpose(updated, (2, 0, 1, 3))[None], cell_flow
 
 

time: 55 us -> 54.1 us (0.984)
  Pallas kernels: 18.8 us -> 18 us
    pallas_call x1, Pallas kernels: 2.2 us -> 1.41 us  [shards(): call(turn_body, [shape((MOST, 3, devices, 128), f32), shape((3, CX, CY, C...]
where the time goes in v7:
time: 54.1 us; the launch traced here: 54 us
  blocking collectives  27.3 us (50%)
  Pallas kernels  18 us (33%)
  starting transfers between devices  4.71 us (9%)
  waiting for transfers between devices  3.08 us (6%)
  between operations  0.71 us (1%)
    all_to_all x1, blocking collectives, shards(): lax.all_to_all(send.reshape(devices, MOST, 4, 128), ('gx', 'gy', 'gz'), s...  27.3 us
    pallas_call x1, Pallas kernels, shards(): call(deposit_body, total_shape, scratch_shapes=[pltpu.VMEM((2, 192, 128),...  5.49 us
    pallas_call x1, Pallas kernels, shards(): call(look_body, [shape((devices * MOST * 4, 128), f32), shape((MOST, 3, d...  5.24 us
    pallas_call x1, Pallas kernels, shards(): call(deposit_faces_body, [y_face, y_face], scratch_shapes=[pltpu.VMEM((16...  3.14 us
    ppermute x3, starting transfers between devices, both_ways(): lax.ppermute(tail, axis, [(i, (i + 1) % count) for i in range(count)])  2.97 us
    ppermute x3, waiting for transfers between devices, both_ways(): lax.ppermute(tail, axis, [(i, (i + 1) % count) for i in range(count)])  2.97 us
    ppermute x3, starting transfers between devices, both_ways(): up = lax.ppermute(head, axis, [((i + 1) % count, i) for i in range(count)])  1.74 us
    pallas_call x1, Pallas kernels, shards(): call(pack_body, shape((devices * MOST * 4, 128), f32), in_specs=[hbm, hbm...  1.66 us
  transfers between devices with their start and end apart: 6, of which 2 were waited for; matrix products, arithmetic and copies ran while one was open for 0% of the time, Pallas kernels for 21%

profile of v7, /device:TPU:0, one launch (start us, length us, event | category | flops | bytes accessed | tf_op | source)
XLA Modules:
  0.0 54.0 jit_solution(6180618667977424100)
XLA Ops:
  0.6 1.7 %pack.1 = f32[1536,128]{1,0:T(8,128)S(1)} custom-call(s32[1,256]{1,0:T(1,128)} %bitcast.13, f32[3,256,128]{2,1,0:T(8,128)} %bitcast.12, s32[256,128]{1,0:T(8,128)} %index_hbm.1), custom_call_target="tpu_custom_call" | custom-call | tf_op jit(solution)/shard_map/pack/pallas_call | solution.py:414
  2.3 27.3 %all_to_all.5 = f32[128,3,4,128]{3,2,1,0:T(4,128)S(1)} all-to-all(f32[128,3,4,128]{3,2,1,0:T(4,128)S(1)} %bitcast.11), channel_id=1, replica_groups=mesh['gx'=8,'gy'=4,'gz'=4] {'gx','gy','gz'}, dimensions={0} | all-to-all | bytes 1572864 | tf_op jit(solution)/shard_map/all_to_all | solution.py:438
  29.6 3.1 %deposit_faces.1 = (f32[4,8,128]{2,1,0:T(8,128)S(1)}, f32[4,8,128]{2,1,0:T(8,128)S(1)}) custom-call(f32[1536,128]{1,0:T(8,128)S(1)} %bitcast.7), custom_call_target="tpu_custom_call" | custom-call | tf_op jit(solution)/shard_map/deposit_faces/pallas_call | solution.py:446
  32.7 0.0 copy-start
  32.8 0.4 collective-permute-start
  33.2 1.7 %collective-permute-start.1 = (f32[4,8,128]{2,1,0:T(8,128)S(1)}, f32[4,8,128]{2,1,0:T(8,128)S(1)}, u32[]{:S(2)}, u32[]{:S(2)}) collective-permute-start(f32[4,8,128]{2,1,0:T(8,128)S(1)} %get-tuple-element.27), channel_id=1, source_target_pairs={{0,4},{4,8},{8,12},{12,0},{1,5},{5,9},{9,13},{13,1},{2,6},{6,10},{... | collective-permute-start | bytes 49160 | tf_op jit(solution)/shard_map/ppermute | solution.py:403
  34.9 5.5 %deposit.1.total_ref = f32[4,48,128]{2,1,0:T(8,128)S(1)} custom-call(f32[1536,128]{1,0:T(8,128)S(1)} %bitcast.8), custom_call_target="tpu_custom_call" | custom-call | tf_op jit(solution)/shard_map/deposit/pallas_call | solution.py:454
  40.3 0.0 collective-permute-done.up_ref
  40.4 0.0 collective-permute-done.1.down_ref
  40.4 0.1 fold_y.1
  40.4 0.0 copy-start.1
  40.5 0.0 collective-permute-start.2
  40.5 0.5 collective-permute-start.3
  41.0 0.0 copy-done
  41.0 0.1 copy-done.1
  41.1 0.9 %axes.1 = (f32[48,128]{1,0:T(8,128)S(1)}, f32[3,8,128]{2,1,0:T(8,128)S(1)}) custom-call(s32[3]{0:T(128)S(1)} %copy-done.1, s32[32,32,32]{2,1,0:T(8,128)S(1)} %copy-done), custom_call_target="tpu_custom_call" | custom-call | tf_op jit(solution)/shard_map/axes/pallas_call | solution.py:431
  42.0 0.1 collective-permute-done.2.up_ref
  42.1 3.0 %collective-permute-done.3.down_ref = f32[4,16,128]{2,1,0:T(8,128)S(1)} collective-permute-done((f32[4,16,128]{2,1,0:T(8,128)S(1)}, f32[4,16,128]{2,1,0:T(8,128)S(1)}, u32[]{:S(2)}, u32[]{:S(2)}) %collective-permute-start.3) | collective-permute-done | bytes 32800 | tf_op jit(solution)/shard_map/ppermute | solution.py:403
  45.0 0.2 fold_x.1
  45.2 1.3 %collective-permute-start.4 = (f32[8,128]{1,0:T(8,128)S(1)}, f32[8,128]{1,0:T(8,128)S(1)}, u32[]{:S(2)}, u32[]{:S(2)}) collective-permute-start(f32[8,128]{1,0:T(8,128)S(1)} %get-tuple-element.36), channel_id=1, source_target_pairs={{1,0},{2,1},{3,2},{0,3},{5,4},{6,5},{7,6},{4,7},{9,8},{10,9},{11,1... | collective-permute-start | bytes 12296 | tf_op jit(solution)/shard_map/ppermute | solution.py:402
  46.5 0.8 %collective-permute-start.5 = (f32[8,128]{1,0:T(8,128)S(1)}, f32[8,128]{1,0:T(8,128)S(1)}, u32[]{:S(2)}, u32[]{:S(2)}) collective-permute-start(f32[8,128]{1,0:T(8,128)S(1)} %get-tuple-element.37), channel_id=1, source_target_pairs={{0,1},{1,2},{2,3},{3,0},{4,5},{5,6},{6,7},{7,4},{8,9},{9,10},{10,1... | collective-permute-start | bytes 12296 | tf_op jit(solution)/shard_map/ppermute | solution.py:403
  47.3 5.2 %look.1 = (f32[1536,128]{1,0:T(8,128)S(1)}, f32[3,3,128,128]{3,2,1,0:T(8,128)S(1)}) custom-call(f32[4,48,128]{2,1,0:T(8,128)S(1)} %get-tuple-element.35.total_ref, f32[48,128]{1,0:T(8,128)S(1)} %get-tuple-element.38.axes_ref, f32[3,8,128]{2,1,0:T(8,128)S(1)} %get-tuple-element.39.units_ref, f32[1536,128]{1,0:T(8,128)S(1)} %bitcast.9), custom_call_target="tpu_custom_call" | custom-call | tf_op jit(solution)/shard_map/look/pallas_call | solution.py:469
  52.5 0.0 collective-permute-done.4.up_ref
  52.6 0.0 collective-permute-done.5.down_ref
  52.6 1.4 %turn.1 = (f32[3,3,128,128]{3,2,1,0:T(8,128)}, f32[3,4,8,128]{3,2,1,0:T(8,128)}) custom-call(f32[4,48,128]{2,1,0:T(8,128)S(1)} %get-tuple-element.35.total_ref, f32[8,128]{1,0:T(8,128)S(1)} %collective-permute-done.4.up_ref, f32[8,128]{1,0:T(8,128)S(1)} %collective-permute-done.5.down_ref, f32[3,3,128,128]{3,2,1,0:T(8,128)S(1)} %get-tuple-element.40.normal_ref, ...), custom_call_target="tpu_custom_call" | custom-call | tf_op jit(solution)/shard_map/turn/pallas_call | solution.py:480
Async XLA Ops:
  32.7 8.2 %copy-start = (s32[32,32,32]{2,1,0:T(8,128)S(1)}, s32[32,32,32]{2,1,0:T(8,128)}, u32[]{:S(2)}) copy-start(s32[32,32,32]{2,1,0:T(8,128)} %rotation_ref.1) | copy-start | bytes 393220
  32.8 7.6 %collective-permute-start = (f32[4,8,128]{2,1,0:T(8,128)S(1)}, f32[4,8,128]{2,1,0:T(8,128)S(1)}, u32[]{:S(2)}, u32[]{:S(2)}) collective-permute-start(f32[4,8,128]{2,1,0:T(8,128)S(1)} %get-tuple-element.26), channel_id=1, source_target_pairs={{4,0},{8,4},{12,8},{0,12},{5,1},{9,5},{13,9},{1,13},{6,2},{10,6},{... | collective-permute-start | bytes 49160 | tf_op jit(solution)/shard_map/ppermute | solution.py:402
  33.2 7.2 %collective-permute-start.1 = (f32[4,8,128]{2,1,0:T(8,128)S(1)}, f32[4,8,128]{2,1,0:T(8,128)S(1)}, u32[]{:S(2)}, u32[]{:S(2)}) collective-permute-start(f32[4,8,128]{2,1,0:T(8,128)S(1)} %get-tuple-element.27), channel_id=1, source_target_pairs={{0,4},{4,8},{8,12},{12,0},{1,5},{5,9},{9,13},{13,1},{2,6},{6,10},{... | collective-permute-start | bytes 49160 | tf_op jit(solution)/shard_map/ppermute | solution.py:403
  40.4 0.7 %copy-start.1 = (s32[3]{0:T(128)S(1)}, s32[3]{0:T(128)}, u32[]{:S(2)}) copy-start(s32[3]{0:T(128)} %shift_ref.1) | copy-start | bytes 40
  40.5 1.6 %collective-permute-start.2 = (f32[4,16,128]{2,1,0:T(8,128)S(1)}, f32[4,16,128]{2,1,0:T(8,128)S(1)}, u32[]{:S(2)}, u32[]{:S(2)}) collective-permute-start(f32[4,16,128]{2,1,0:T(8,128)S(1)} %get-tuple-element.29), channel_id=1, source_target_pairs={{16,0},{32,16},{48,32},{64,48},{80,64},{96,80},{112,96},{0,112},{1... | collective-permute-start | bytes 98312 | tf_op jit(solution)/shard_map/ppermute | solution.py:402
  40.5 4.6 %collective-permute-start.3 = (f32[4,16,128]{2,1,0:T(8,128)S(1)}, f32[4,16,128]{2,1,0:T(8,128)S(1)}, u32[]{:S(2)}, u32[]{:S(2)}) collective-permute-start(f32[4,16,128]{2,1,0:T(8,128)S(1)} %get-tuple-element.30), channel_id=1, source_target_pairs={{0,16},{16,32},{32,48},{48,64},{64,80},{80,96},{96,112},{112,0},{1... | collective-permute-start | bytes 98312 | tf_op jit(solution)/shard_map/ppermute | solution.py:403
  45.2 7.3 %collective-permute-start.4 = (f32[8,128]{1,0:T(8,128)S(1)}, f32[8,128]{1,0:T(8,128)S(1)}, u32[]{:S(2)}, u32[]{:S(2)}) collective-permute-start(f32[8,128]{1,0:T(8,128)S(1)} %get-tuple-element.36), channel_id=1, source_target_pairs={{1,0},{2,1},{3,2},{0,3},{5,4},{6,5},{7,6},{4,7},{9,8},{10,9},{11,1... | collective-permute-start | bytes 12296 | tf_op jit(solution)/shard_map/ppermute | solution.py:402
  46.5 6.0 %collective-permute-start.5 = (f32[8,128]{1,0:T(8,128)S(1)}, f32[8,128]{1,0:T(8,128)S(1)}, u32[]{:S(2)}, u32[]{:S(2)}) collective-permute-start(f32[8,128]{1,0:T(8,128)S(1)} %get-tuple-element.37), channel_id=1, source_target_pairs={{0,1},{1,2},{2,3},{3,0},{4,5},{5,6},{6,7},{7,4},{8,9},{9,10},{10,1... | collective-permute-start | bytes 12296 | tf_op jit(solution)/shard_map/ppermute | solution.py:403

commit v8 on v7

--- a/solution.py
+++ b/solution.py
@@ -197,22 +197,53 @@
             ref[c, PX : PX + 1] = above
 
 
-def deposit_body(slots_ref, total_ref, acc, rows_q, rows_l):
-    slot_places(slots_ref, rows_q, rows_l)
+def deposit_sides_body(slots_ref, out_ref, acc, rows_q, rows_l):
+    slots = slots_ref.shape[0] // 4
+    label = slots_ref[pl.ds(3, slots, stride=4), :].astype(i32)
+    rows_q[...] = (label >> 7).astype(f32)
+    rows_l[...] = (label & 127).astype(f32)
+    acc[...] = jnp.zeros(acc.shape, f32)
+
+    def store(got):
+        acc[...] += got
+
+    sum_rows(slots_ref, rows_q, rows_l, list(range(1, CY)), CX * PY, 8, store)
+    for c in range(4):
+        for first in (0, 8):
+            total = acc[pl.ds(first + c, CY - 1, stride=16), :]
+            if c < 3:
+                total = total + acc[pl.ds(first + c + 4, CY - 1, stride=16), :]
+            out_ref[c, first : first + CY - 1] = total
+
+
+IN_X = CX - 1
+IN_Y = CY - 1
+IN_HALF = (IN_X * IN_Y + 1) // 2
+
+
+def deposit_inner_body(slots_ref, out_ref, acc, rows_q, rows_l):
+    slots = slots_ref.shape[0] // 4
+    label = slots_ref[pl.ds(3, slots, stride=4), :].astype(i32)
+    row = label >> 7
+    ex = (row * 57) >> 9
+    ey = row - ex * PY
+    here = (ex >= 1) & (ex < CX) & (ey >= 1) & (ey < CY)
+    place = (ex - 1) * IN_Y + ey - 1
+    rows_q[...] = (place >> 1).astype(f32)
+    rows_l[...] = jnp.where(here, (place & 1) * 128 + (label & 127), 512).astype(f32)
     acc[...] = jnp.zeros(acc.shape, f32)
 
     def store(got):
         acc[0] += got[:, :128]
         acc[1] += got[:, 128:]
 
-    sum_rows(slots_ref, rows_q, rows_l, [2 * j for j in range(12)], 1, 16, store)
+    sum_rows(slots_ref, rows_q, rows_l, list(range(0, IN_HALF, 2)), 1, 16, store)
     for c in range(4):
         for odd in range(2):
-            total = acc[odd, pl.ds(c, Q2, stride=8), :]
+            total = acc[odd, pl.ds(c, IN_HALF, stride=8), :]
             if c < 3:
-                total = total + acc[odd, pl.ds(c + 4, Q2, stride=8), :]
-            total_ref[c, pl.ds(odd, Q2, stride=2)] = total
-        total_ref[c, ROWS:PADROWS] = jnp.zeros((PADROWS - ROWS, 128), f32)
+                total = total + acc[odd, pl.ds(c + 4, IN_HALF, stride=8), :]
+            out_ref[c, pl.ds(odd, IN_HALF, stride=2)] = total
 
 
 def moved_lanes(row, first, count, shift):
@@ -221,42 +252,47 @@
     return jnp.where((lane >= first) & (lane < first + count), rolled, 0.0)
 
 
-def fold_y_body(total_ref, up_ref, down_ref, out_ref, head_ref, tail_ref):
+def fold_y_body(
+    own_low, own_high, sides_ref, up_ref, down_ref, low_ref, high_ref, head_ref, tail_ref
+):
     lane = iota((1, 128), 1)
     edge = lane % PY
     for c in range(4):
-        out_ref[c] = total_ref[c]
-        out_ref[c, pl.ds(CY, PX, stride=PY)] = (
-            total_ref[c, pl.ds(CY, PX, stride=PY)] + up_ref[c, 0:PX]
-        )
-        out_ref[c, pl.ds(0, PX, stride=PY)] = (
-            total_ref[c, pl.ds(0, PX, stride=PY)] + down_ref[c, 0:PX]
-        )
+        low_ref[c, 0:PX] = own_low[c, 0:PX] + down_ref[c, 0:PX]
+        high_ref[c, 0:PX] = own_high[c, 0:PX] + up_ref[c, 0:PX]
         up = pltpu.roll(up_ref[c, PX : PX + 1], CY, 1)
         down = pltpu.roll(down_ref[c, PX : PX + 1], 128 - CY, 1)
         above = (
-            total_ref[c, PLANES:ROWS]
+            own_low[c, PX : PX + 1]
             + jnp.where((edge == CY) & (lane < PLANES), up, 0.0)
             + jnp.where((edge == 0) & (lane < PLANES), down, 0.0)
         )
-        out_ref[c, PLANES:ROWS] = above
-        head_ref[c, 0:PY] = out_ref[c, 0:PY]
-        head_ref[c, PY : PY + 1] = above
-        tail_ref[c, 0:PY] = out_ref[c, PLANES - PY : PLANES]
-        tail_ref[c, PY : PY + 1] = above
-
-
-def fold_x_body(total_ref, up_ref, down_ref, out_ref, head_ref, tail_ref):
+        low_ref[c, PX : PX + 1] = above
+        for ref, ex, first in ((head_ref, 0, 0), (tail_ref, CX, 8)):
+            ref[c, 0:1] = low_ref[c, ex : ex + 1]
+            ref[c, 1:CY] = sides_ref[c, first : first + CY - 1]
+            ref[c, CY:PY] = high_ref[c, ex : ex + 1]
+            ref[c, PY : PY + 1] = above
+
+
+def fold_x_body(
+    inner_ref, low_ref, high_ref, own_head, own_tail, up_ref, down_ref, out_ref, head_ref, tail_ref
+):
     last = PLANES - PY
     for c in range(4):
-        out_ref[c] = total_ref[c]
-        out_ref[c, 0:PY] = total_ref[c, 0:PY] + down_ref[c, 0:PY]
-        out_ref[c, last:PLANES] = total_ref[c, last:PLANES] + up_ref[c, 0:PY]
+        out_ref[c, 0:PY] = own_head[c, 0:PY] + down_ref[c, 0:PY]
+        for ex in range(1, CX):
+            row = ex * PY
+            out_ref[c, row : row + 1] = low_ref[c, ex : ex + 1]
+            out_ref[c, row + 1 : row + CY] = inner_ref[c, (ex - 1) * IN_Y : ex * IN_Y]
+            out_ref[c, row + CY : row + PY] = high_ref[c, ex : ex + 1]
+        out_ref[c, last:PLANES] = own_tail[c, 0:PY] + up_ref[c, 0:PY]
         out_ref[c, PLANES:ROWS] = (
-            total_ref[c, PLANES:ROWS]
+            low_ref[c, PX : PX + 1]
             + moved_lanes(up_ref[c, PY : PY + 1], last, PY, last)
             + moved_lanes(down_ref[c, PY : PY + 1], 0, PY, -last)
         )
+        out_ref[c, ROWS:PADROWS] = jnp.zeros((PADROWS - ROWS, 128), f32)
         total = out_ref[c]
         head_ref[c : c + 1] = column_as_row(total)
         tail_ref[c : c + 1] = total[PLANES:ROWS]
@@ -449,21 +485,28 @@
         scratch_shapes=[pltpu.VMEM((16 * (PX + 1), 128), f32), by_slot, by_slot],
         name="deposit_faces",
     )(slots)
+    slots, low, high = lax.optimization_barrier((slots, head, tail))
+    up, down = both_ways(low, high, "gy")
+    sides = call(
+        deposit_sides_body,
+        x_face,
+        scratch_shapes=[pltpu.VMEM((16 * (CY - 1), 128), f32), by_slot, by_slot],
+        name="deposit_sides",
+    )(slots)
+    low, high, head, tail = call(
+        fold_y_body, [y_face, y_face, x_face, x_face], name="fold_y"
+    )(low, high, sides, up, down)
     slots, head, tail = lax.optimization_barrier((slots, head, tail))
-    up, down = both_ways(head, tail, "gy")
-    total = call(
-        deposit_body,
-        total_shape,
-        scratch_shapes=[pltpu.VMEM((2, 192, 128), f32), by_slot, by_slot],
-        name="deposit",
+    up, down = both_ways(head, tail, "gx")
+    inner = call(
+        deposit_inner_body,
+        shape((4, 24, 128), f32),
+        scratch_shapes=[pltpu.VMEM((2, 96, 128), f32), by_slot, by_slot],
+        name="deposit_inner",
     )(slots)
-    total, head, tail = call(fold_y_body, [total_shape, x_face, x_face], name="fold_y")(
-        total, up, down
-    )
-    up, down = both_ways(head, tail, "gx")
-    up, down, axes, units = lax.optimization_barrier((up, down, axes, units))
+    up, down, axes, units, inner = lax.optimization_barrier((up, down, axes, units, inner))
     total, head, tail = call(fold_x_body, [total_shape, z_face, z_face], name="fold_x")(
-        total, up, down
+        inner, low, high, head, tail, up, down
     )
     up, down = both_ways(head, tail, "gz")
     found, normal = call(

time: 54.1 us -> 54.6 us (level); the launches traced: 54 us -> 53.8 us
  waiting for transfers between devices: 3.08 us -> 0.02 us
  Pallas kernels: 18 us -> 20.7 us
    ppermute x3, waiting for transfers between devices: 2.97 us -> 0.01 us  [both_ways(): lax.ppermute(tail, axis, [(i, (i + 1) % count) for i in range(count)])]
    pallas_call x2 -> x3, Pallas kernels: 5.57 us -> 8.19 us  [the longest x1 4.68 us: shards(): call(deposit_inner_body, shape((4, 24, 128), f32), scratch_shapes=[pltpu....]
  transfers between devices with their start and end apart: 6 -> 6, of which waited for: 2 -> 0; matrix products, arithmetic and copies ran while one was open for 0% -> 0% of each run, Pallas kernels for 21% -> 26%
where the time goes in v8:
time: 54.6 us; the launch traced here: 53.8 us
  blocking collectives  27.3 us (50%)
  Pallas kernels  20.7 us (38%)
  starting transfers between devices  4.71 us (9%)
  between operations  0.91 us (2%)
    all_to_all x1, blocking collectives, shards(): lax.all_to_all(send.reshape(devices, MOST, 4, 128), ('gx', 'gy', 'gz'), s...  27.3 us
    pallas_call x1, Pallas kernels, shards(): call(look_body, [shape((devices * MOST * 4, 128), f32), shape((MOST, 3, d...  5.24 us
    pallas_call x1, Pallas kernels, shards(): call(deposit_inner_body, shape((4, 24, 128), f32), scratch_shapes=[pltpu....  4.68 us
    pallas_call x1, Pallas kernels, shards(): call(deposit_sides_body, x_face, scratch_shapes=[pltpu.VMEM((16 * (CY - 1...  3.43 us
    pallas_call x1, Pallas kernels, shards(): call(deposit_faces_body, [y_face, y_face], scratch_shapes=[pltpu.VMEM((16...  3.15 us
    ppermute x3, starting transfers between devices, both_ways(): lax.ppermute(tail, axis, [(i, (i + 1) % count) for i in range(count)])  2.7 us
    ppermute x3, starting transfers between devices, both_ways(): up = lax.ppermute(head, axis, [((i + 1) % count, i) for i in range(count)])  2 us
    pallas_call x1, Pallas kernels, shards(): call(pack_body, shape((devices * MOST * 4, 128), f32), in_specs=[hbm, hbm...  1.67 us
  transfers between devices with their start and end apart: 6, of which 0 were waited for; matrix products, arithmetic and copies ran while one was open for 0% of the time, Pallas kernels for 26%

profile of v8, /device:TPU:0, one launch (start us, length us, event | category | flops | bytes accessed | tf_op | source)
XLA Modules:
  0.0 53.8 jit_solution(11824581894921117506)
XLA Ops:
  0.6 1.7 %pack.1 = f32[1536,128]{1,0:T(8,128)S(1)} custom-call(s32[1,256]{1,0:T(1,128)} %bitcast.14, f32[3,256,128]{2,1,0:T(8,128)} %bitcast.13, s32[256,128]{1,0:T(8,128)} %index_hbm.1), custom_call_target="tpu_custom_call" | custom-call | tf_op jit(solution)/shard_map/pack/pallas_call | solution.py:450
  2.3 27.3 %all_to_all.5 = f32[128,3,4,128]{3,2,1,0:T(4,128)S(1)} all-to-all(f32[128,3,4,128]{3,2,1,0:T(4,128)S(1)} %bitcast.12), channel_id=1, replica_groups=mesh['gx'=8,'gy'=4,'gz'=4] {'gx','gy','gz'}, dimensions={0} | all-to-all | bytes 1572864 | tf_op jit(solution)/shard_map/all_to_all | solution.py:474
  29.6 3.1 %deposit_faces.1 = (f32[4,8,128]{2,1,0:T(8,128)S(1)}, f32[4,8,128]{2,1,0:T(8,128)S(1)}) custom-call(f32[1536,128]{1,0:T(8,128)S(1)} %bitcast.7), custom_call_target="tpu_custom_call" | custom-call | tf_op jit(solution)/shard_map/deposit_faces/pallas_call | solution.py:482
  32.8 0.0 copy-start
  32.8 0.4 collective-permute-start
  33.2 1.7 %collective-permute-start.1 = (f32[4,8,128]{2,1,0:T(8,128)S(1)}, f32[4,8,128]{2,1,0:T(8,128)S(1)}, u32[]{:S(2)}, u32[]{:S(2)}) collective-permute-start(f32[4,8,128]{2,1,0:T(8,128)S(1)} %get-tuple-element.32.own_high), channel_id=1, source_target_pairs={{0,4},{4,8},{8,12},{12,0},{1,5},{5,9},{9,13},{13,1},{2,6},{6,10},{... | collective-permute-start | bytes 49160 | tf_op jit(solution)/shard_map/ppermute | solution.py:439
  34.9 3.4 %deposit_sides.1.sides_ref = f32[4,16,128]{2,1,0:T(8,128)S(1)} custom-call(f32[1536,128]{1,0:T(8,128)S(1)} %bitcast.8), custom_call_target="tpu_custom_call" | custom-call | tf_op jit(solution)/shard_map/deposit_sides/pallas_call | solution.py:490
  38.3 0.0 collective-permute-done.up_ref
  38.3 0.0 collective-permute-done.1.down_ref
  38.3 0.1 fold_y.1
  38.4 0.0 copy-start.1
  38.4 0.0 collective-permute-start.2
  38.5 0.5 collective-permute-start.3
  38.9 0.0 copy-done
  39.0 0.1 copy-done.1
  39.1 0.9 %axes.1 = (f32[48,128]{1,0:T(8,128)S(1)}, f32[3,8,128]{2,1,0:T(8,128)S(1)}) custom-call(s32[3]{0:T(128)S(1)} %copy-done.1, s32[32,32,32]{2,1,0:T(8,128)S(1)} %copy-done), custom_call_target="tpu_custom_call" | custom-call | tf_op jit(solution)/shard_map/axes/pallas_call | solution.py:467
  39.9 4.7 %deposit_inner.1.inner_ref = f32[4,24,128]{2,1,0:T(8,128)S(1)} custom-call(f32[1536,128]{1,0:T(8,128)S(1)} %bitcast.9), custom_call_target="tpu_custom_call" | custom-call | tf_op jit(solution)/shard_map/deposit_inner/pallas_call | solution.py:501
  44.6 0.0 collective-permute-done.2.up_ref
  44.6 0.0 collective-permute-done.3.down_ref
  44.7 0.2 fold_x.1
  44.8 1.6 %collective-permute-start.4 = (f32[8,128]{1,0:T(8,128)S(1)}, f32[8,128]{1,0:T(8,128)S(1)}, u32[]{:S(2)}, u32[]{:S(2)}) collective-permute-start(f32[8,128]{1,0:T(8,128)S(1)} %get-tuple-element.46), channel_id=1, source_target_pairs={{1,0},{2,1},{3,2},{0,3},{5,4},{6,5},{7,6},{4,7},{9,8},{10,9},{11,1... | collective-permute-start | bytes 12296 | tf_op jit(solution)/shard_map/ppermute | solution.py:438
  46.4 0.5 collective-permute-start.5
  46.9 5.2 %look.1 = (f32[1536,128]{1,0:T(8,128)S(1)}, f32[3,3,128,128]{3,2,1,0:T(8,128)S(1)}) custom-call(f32[4,48,128]{2,1,0:T(8,128)S(1)} %get-tuple-element.45.total_ref, f32[48,128]{1,0:T(8,128)S(1)} %get-tuple-element.48.axes_ref, f32[3,8,128]{2,1,0:T(8,128)S(1)} %get-tuple-element.49.units_ref, f32[1536,128]{1,0:T(8,128)S(1)} %bitcast.10), custom_call_target="tpu_custom_call" | custom-call | tf_op jit(solution)/shard_map/look/pallas_call | solution.py:512
  52.2 0.0 collective-permute-done.4.up_ref
  52.2 0.0 collective-permute-done.5.down_ref
  52.2 1.4 %turn.1 = (f32[3,3,128,128]{3,2,1,0:T(8,128)}, f32[3,4,8,128]{3,2,1,0:T(8,128)}) custom-call(f32[4,48,128]{2,1,0:T(8,128)S(1)} %get-tuple-element.45.total_ref, f32[8,128]{1,0:T(8,128)S(1)} %collective-permute-done.4.up_ref, f32[8,128]{1,0:T(8,128)S(1)} %collective-permute-done.5.down_ref, f32[3,3,128,128]{3,2,1,0:T(8,128)S(1)} %get-tuple-element.50.normal_ref, ...), custom_call_target="tpu_custom_call" | custom-call | tf_op jit(solution)/shard_map/turn/pallas_call | solution.py:523
Async XLA Ops:
  32.8 6.2 %copy-start = (s32[32,32,32]{2,1,0:T(8,128)S(1)}, s32[32,32,32]{2,1,0:T(8,128)}, u32[]{:S(2)}) copy-start(s32[32,32,32]{2,1,0:T(8,128)} %rotation_ref.1) | copy-start | bytes 393220
  32.8 5.5 %collective-permute-start = (f32[4,8,128]{2,1,0:T(8,128)S(1)}, f32[4,8,128]{2,1,0:T(8,128)S(1)}, u32[]{:S(2)}, u32[]{:S(2)}) collective-permute-start(f32[4,8,128]{2,1,0:T(8,128)S(1)} %get-tuple-element.31.own_low), channel_id=1, source_target_pairs={{4,0},{8,4},{12,8},{0,12},{5,1},{9,5},{13,9},{1,13},{6,2},{10,6},{... | collective-permute-start | bytes 49160 | tf_op jit(solution)/shard_map/ppermute | solution.py:438
  33.2 5.1 %collective-permute-start.1 = (f32[4,8,128]{2,1,0:T(8,128)S(1)}, f32[4,8,128]{2,1,0:T(8,128)S(1)}, u32[]{:S(2)}, u32[]{:S(2)}) collective-permute-start(f32[4,8,128]{2,1,0:T(8,128)S(1)} %get-tuple-element.32.own_high), channel_id=1, source_target_pairs={{0,4},{4,8},{8,12},{12,0},{1,5},{5,9},{9,13},{13,1},{2,6},{6,10},{... | collective-permute-start | bytes 49160 | tf_op jit(solution)/shard_map/ppermute | solution.py:439
  38.4 0.7 %copy-start.1 = (s32[3]{0:T(128)S(1)}, s32[3]{0:T(128)}, u32[]{:S(2)}) copy-start(s32[3]{0:T(128)} %shift_ref.1) | copy-start | bytes 40
  38.4 6.2 %collective-permute-start.2 = (f32[4,16,128]{2,1,0:T(8,128)S(1)}, f32[4,16,128]{2,1,0:T(8,128)S(1)}, u32[]{:S(2)}, u32[]{:S(2)}) collective-permute-start(f32[4,16,128]{2,1,0:T(8,128)S(1)} %get-tuple-element.35.own_head), channel_id=1, source_target_pairs={{16,0},{32,16},{48,32},{64,48},{80,64},{96,80},{112,96},{0,112},{1... | collective-permute-start | bytes 98312 | tf_op jit(solution)/shard_map/ppermute | solution.py:438
  38.5 6.2 %collective-permute-start.3 = (f32[4,16,128]{2,1,0:T(8,128)S(1)}, f32[4,16,128]{2,1,0:T(8,128)S(1)}, u32[]{:S(2)}, u32[]{:S(2)}) collective-permute-start(f32[4,16,128]{2,1,0:T(8,128)S(1)} %get-tuple-element.36.own_tail), channel_id=1, source_target_pairs={{0,16},{16,32},{32,48},{48,64},{64,80},{80,96},{96,112},{112,0},{1... | collective-permute-start | bytes 98312 | tf_op jit(solution)/shard_map/ppermute | solution.py:439
  44.8 7.3 %collective-permute-start.4 = (f32[8,128]{1,0:T(8,128)S(1)}, f32[8,128]{1,0:T(8,128)S(1)}, u32[]{:S(2)}, u32[]{:S(2)}) collective-permute-start(f32[8,128]{1,0:T(8,128)S(1)} %get-tuple-element.46), channel_id=1, source_target_pairs={{1,0},{2,1},{3,2},{0,3},{5,4},{6,5},{7,6},{4,7},{9,8},{10,9},{11,1... | collective-permute-start | bytes 12296 | tf_op jit(solution)/shard_map/ppermute | solution.py:438
  46.4 5.8 %collective-permute-start.5 = (f32[8,128]{1,0:T(8,128)S(1)}, f32[8,128]{1,0:T(8,128)S(1)}, u32[]{:S(2)}, u32[]{:S(2)}) collective-permute-start(f32[8,128]{1,0:T(8,128)S(1)} %get-tuple-element.47), channel_id=1, source_target_pairs={{0,1},{1,2},{2,3},{3,0},{4,5},{5,6},{6,7},{7,4},{8,9},{9,10},{10,1... | collective-permute-start | bytes 12296 | tf_op jit(solution)/shard_map/ppermute | solution.py:439

commit v9 on v7

--- a/solution.py
+++ b/solution.py
@@ -56,7 +56,9 @@
     )
 
 
-def pack_body(target_hbm, velocity_hbm, index_hbm, out_ref, target_ref, velocity_ref, index_ref, sems):
+def pack_body(
+    target_hbm, velocity_hbm, index_hbm, out_ref, units_ref, target_ref, velocity_ref, index_ref, sems
+):
     sources = (target_hbm, index_hbm, velocity_hbm)
     sinks = (target_ref, index_ref, velocity_ref)
     copies = [
@@ -65,6 +67,8 @@
     ]
     for copy in copies:
         copy.start()
+    for c, line in enumerate(axis_table((8, 128))):
+        units_ref[c] = line
     bricks = 128
     blocks = target_ref.shape[1]
     copies[0].wait()
@@ -94,7 +98,7 @@
             out_ref[pl.ds(rank * 4 + c, bricks, stride=4 * MOST), :] = value
 
 
-def axes_body(shift_ref, rotation_ref, out_ref, units_ref, rows):
+def axes_body(shift_ref, rotation_ref, out_ref, rows):
     base_x = lax.axis_index("gx") * CX + shift_ref[0]
     base_y = lax.axis_index("gy") * CY + shift_ref[1]
     rows[...] = jnp.zeros(rows.shape, i32)
@@ -109,8 +113,6 @@
     value = pltpu.roll(value, (128 - shift_ref[2]) & 127, 1)
     first = column_as_row(value)
     out_ref[...] = jnp.where(iota(value.shape, 0) == PLANES, first, value)
-    for c, line in enumerate(axis_table((8, 128))):
-        units_ref[c] = line
 
 
 def column_as_row(value):
@@ -147,15 +149,19 @@
     zero = jnp.zeros((16, 128), bf16)
 
     def step(i, carry):
-        weighted, depths = [], []
+        weighted, depths, values = [], [], []
+        for k in range(DEPOSIT_STEP // 2):
+            own = slots_ref[pl.ds(pl.multiple_of(i * DEPOSIT_STEP * 4, 8) + 8 * k, 8), :]
+            high = own.astype(bf16).astype(f32)
+            low = own - high
+            first = jnp.where(sub8 < 4, high, pltpu.roll(low, 4, 0))
+            second = jnp.where(sub8 < 4, pltpu.roll(high, 4, 0), low)
+            for value in (first, second):
+                value = jnp.where(sub8 == 3, 1.0, value).astype(bf16)
+                values.append(jnp.concatenate([value, value], axis=0))
         for k in range(DEPOSIT_STEP):
             slot = i * DEPOSIT_STEP + k
-            own = slots_ref[pl.ds(pl.multiple_of(i * DEPOSIT_STEP * 4, 8) + 4 * k, 4), :]
-            own = jnp.concatenate([own, own], axis=0)
-            high = own.astype(bf16).astype(f32)
-            value = jnp.where(sub8 < 4, high, own - high)
-            value = jnp.where(sub8 == 3, 1.0, jnp.where(sub8 == 7, 0.0, value))
-            value = jnp.concatenate([value, value], axis=0).astype(bf16)
+            value = values[k]
             q = jnp.broadcast_to(rows_q[pl.ds(slot, 1), :], (16, 128)).astype(bf16) - half
             weighted.append(
                 jnp.concatenate([jnp.where(q == float(j), value, zero) for j in firsts], axis=0)
@@ -411,9 +417,9 @@
     smem = pl.BlockSpec(memory_space=pltpu.SMEM)
     hbm = pl.BlockSpec(memory_space=pltpu.HBM)
     blocks = velocity.shape[0]
-    send = call(
+    send, units = call(
         pack_body,
-        shape((devices * MOST * 4, 128), f32),
+        [shape((devices * MOST * 4, 128), f32), shape((3, 8, 128), f32)],
         in_specs=[hbm, hbm, hbm],
         scratch_shapes=[
             pltpu.VMEM((1, blocks), i32),
@@ -428,9 +434,9 @@
             for x in (block_target.reshape(1, -1), jnp.transpose(velocity, (1, 0, 2)), cell_index)
         )
     )
-    axes, units = call(
+    axes = call(
         axes_body,
-        [shape((PADROWS, 128), f32), shape((3, 8, 128), f32)],
+        shape((PADROWS, 128), f32),
         in_specs=[smem, vmem],
         scratch_shapes=[pltpu.VMEM((PADROWS, 128), i32)],
         name="axes",
@@ -461,7 +467,7 @@
         total, up, down
     )
     up, down = both_ways(head, tail, "gx")
-    up, down, axes, units = lax.optimization_barrier((up, down, axes, units))
+    up, down, axes = lax.optimization_barrier((up, down, axes))
     total, head, tail = call(fold_x_body, [total_shape, z_face, z_face], name="fold_x")(
         total, up, down
     )

time: 54.1 us -> 54.1 us (level)
  transfers between devices with their start and end apart: 6 -> 6, of which waited for: 2 -> 2; matrix products, arithmetic and copies ran while one was open for 0% -> 0% of each run, Pallas kernels for 21% -> 22%
where the time goes in v9:
time: 54.1 us; the launch traced here: 53.9 us
  blocking collectives  27.3 us (50%)
  Pallas kernels  18 us (33%)
  starting transfers between devices  4.71 us (9%)
  waiting for transfers between devices  3.08 us (6%)
  between operations  0.72 us (1%)
    all_to_all x1, blocking collectives, shards(): lax.all_to_all(send.reshape(devices, MOST, 4, 128), ('gx', 'gy', 'gz'), s...  27.3 us
    pallas_call x1, Pallas kernels, shards(): call(deposit_body, total_shape, scratch_shapes=[pltpu.VMEM((2, 192, 128),...  5.48 us
    pallas_call x1, Pallas kernels, shards(): call(look_body, [shape((devices * MOST * 4, 128), f32), shape((MOST, 3, d...  5.25 us
    pallas_call x1, Pallas kernels, shards(): call(deposit_faces_body, [y_face, y_face], scratch_shapes=[pltpu.VMEM((16...  3.05 us
    ppermute x3, starting transfers between devices, both_ways(): lax.ppermute(tail, axis, [(i, (i + 1) % count) for i in range(count)])  2.98 us
    ppermute x3, waiting for transfers between devices, both_ways(): lax.ppermute(tail, axis, [(i, (i + 1) % count) for i in range(count)])  2.97 us
    ppermute x3, starting transfers between devices, both_ways(): up = lax.ppermute(head, axis, [((i + 1) % count, i) for i in range(count)])  1.72 us
    pallas_call x1, Pallas kernels, shards(): call(pack_body, [shape((devices * MOST * 4, 128), f32), shape((3, 8, 128)...  1.66 us
  transfers between devices with their start and end apart: 6, of which 2 were waited for; matrix products, arithmetic and copies ran while one was open for 0% of the time, Pallas kernels for 22%

profile of v9, /device:TPU:0, one launch (start us, length us, event | category | flops | bytes accessed | tf_op | source)
XLA Modules:
  0.0 53.9 jit_solution(6921860090133661811)
XLA Ops:
  0.6 1.7 %pack.1 = (f32[1536,128]{1,0:T(8,128)S(1)}, f32[3,8,128]{2,1,0:T(8,128)S(1)}) custom-call(s32[1,256]{1,0:T(1,128)} %bitcast.13, f32[3,256,128]{2,1,0:T(8,128)} %bitcast.12, s32[256,128]{1,0:T(8,128)} %index_hbm.1), custom_call_target="tpu_custom_call" | custom-call | tf_op jit(solution)/shard_map/pack/pallas_call | solution.py:420
  2.3 27.3 %all_to_all.5 = f32[128,3,4,128]{3,2,1,0:T(4,128)S(1)} all-to-all(f32[128,3,4,128]{3,2,1,0:T(4,128)S(1)} %bitcast.11), channel_id=1, replica_groups=mesh['gx'=8,'gy'=4,'gz'=4] {'gx','gy','gz'}, dimensions={0} | all-to-all | bytes 1572864 | tf_op jit(solution)/shard_map/all_to_all | solution.py:444
  29.6 3.1 %deposit_faces.1 = (f32[4,8,128]{2,1,0:T(8,128)S(1)}, f32[4,8,128]{2,1,0:T(8,128)S(1)}) custom-call(f32[1536,128]{1,0:T(8,128)S(1)} %bitcast.7), custom_call_target="tpu_custom_call" | custom-call | tf_op jit(solution)/shard_map/deposit_faces/pallas_call | solution.py:452
  32.7 0.0 copy-start
  32.7 0.4 collective-permute-start
  33.1 1.7 %collective-permute-start.1 = (f32[4,8,128]{2,1,0:T(8,128)S(1)}, f32[4,8,128]{2,1,0:T(8,128)S(1)}, u32[]{:S(2)}, u32[]{:S(2)}) collective-permute-start(f32[4,8,128]{2,1,0:T(8,128)S(1)} %get-tuple-element.27), channel_id=1, source_target_pairs={{0,4},{4,8},{8,12},{12,0},{1,5},{5,9},{9,13},{13,1},{2,6},{6,10},{... | collective-permute-start | bytes 49160 | tf_op jit(solution)/shard_map/ppermute | solution.py:409
  34.8 5.5 %deposit.1.total_ref = f32[4,48,128]{2,1,0:T(8,128)S(1)} custom-call(f32[1536,128]{1,0:T(8,128)S(1)} %bitcast.8), custom_call_target="tpu_custom_call" | custom-call | tf_op jit(solution)/shard_map/deposit/pallas_call | solution.py:460
  40.3 0.0 collective-permute-done.up_ref
  40.3 0.0 collective-permute-done.1.down_ref
  40.3 0.1 fold_y.1
  40.4 0.0 copy-start.1
  40.4 0.0 collective-permute-start.2
  40.4 0.5 collective-permute-start.3
  40.9 0.0 copy-done
  40.9 0.1 copy-done.1
  41.0 0.9 %axes.1.axes_ref = f32[48,128]{1,0:T(8,128)S(1)} custom-call(s32[3]{0:T(128)S(1)} %copy-done.1, s32[32,32,32]{2,1,0:T(8,128)S(1)} %copy-done), custom_call_target="tpu_custom_call" | custom-call | tf_op jit(solution)/shard_map/axes/pallas_call | solution.py:437
  41.9 0.1 collective-permute-done.2.up_ref
  42.0 3.0 %collective-permute-done.3.down_ref = f32[4,16,128]{2,1,0:T(8,128)S(1)} collective-permute-done((f32[4,16,128]{2,1,0:T(8,128)S(1)}, f32[4,16,128]{2,1,0:T(8,128)S(1)}, u32[]{:S(2)}, u32[]{:S(2)}) %collective-permute-start.3) | collective-permute-done | bytes 32800 | tf_op jit(solution)/shard_map/ppermute | solution.py:409
  45.0 0.2 fold_x.1
  45.1 1.3 %collective-permute-start.4 = (f32[8,128]{1,0:T(8,128)S(1)}, f32[8,128]{1,0:T(8,128)S(1)}, u32[]{:S(2)}, u32[]{:S(2)}) collective-permute-start(f32[8,128]{1,0:T(8,128)S(1)} %get-tuple-element.34), channel_id=1, source_target_pairs={{1,0},{2,1},{3,2},{0,3},{5,4},{6,5},{7,6},{4,7},{9,8},{10,9},{11,1... | collective-permute-start | bytes 12296 | tf_op jit(solution)/shard_map/ppermute | solution.py:408
  46.4 0.8 %collective-permute-start.5 = (f32[8,128]{1,0:T(8,128)S(1)}, f32[8,128]{1,0:T(8,128)S(1)}, u32[]{:S(2)}, u32[]{:S(2)}) collective-permute-start(f32[8,128]{1,0:T(8,128)S(1)} %get-tuple-element.35), channel_id=1, source_target_pairs={{0,1},{1,2},{2,3},{3,0},{4,5},{5,6},{6,7},{7,4},{8,9},{9,10},{10,1... | collective-permute-start | bytes 12296 | tf_op jit(solution)/shard_map/ppermute | solution.py:409
  47.2 5.2 %look.1 = (f32[1536,128]{1,0:T(8,128)S(1)}, f32[3,3,128,128]{3,2,1,0:T(8,128)S(1)}) custom-call(f32[4,48,128]{2,1,0:T(8,128)S(1)} %get-tuple-element.33.total_ref, f32[48,128]{1,0:T(8,128)S(1)} %axes.1.axes_ref, f32[3,8,128]{2,1,0:T(8,128)S(1)} %get-tuple-element.37.units_ref, f32[1536,128]{1,0:T(8,128)S(1)} %bitcast.9), custom_call_target="tpu_custom_call" | custom-call | tf_op jit(solution)/shard_map/look/pallas_call | solution.py:475
  52.5 0.0 collective-permute-done.4.up_ref
  52.5 0.0 collective-permute-done.5.down_ref
  52.5 1.4 %turn.1 = (f32[3,3,128,128]{3,2,1,0:T(8,128)}, f32[3,4,8,128]{3,2,1,0:T(8,128)}) custom-call(f32[4,48,128]{2,1,0:T(8,128)S(1)} %get-tuple-element.33.total_ref, f32[8,128]{1,0:T(8,128)S(1)} %collective-permute-done.4.up_ref, f32[8,128]{1,0:T(8,128)S(1)} %collective-permute-done.5.down_ref, f32[3,3,128,128]{3,2,1,0:T(8,128)S(1)} %get-tuple-element.38.normal_ref, ...), custom_call_target="tpu_custom_call" | custom-call | tf_op jit(solution)/shard_map/turn/pallas_call | solution.py:486
Async XLA Ops:
  32.7 8.2 %copy-start = (s32[32,32,32]{2,1,0:T(8,128)S(1)}, s32[32,32,32]{2,1,0:T(8,128)}, u32[]{:S(2)}) copy-start(s32[32,32,32]{2,1,0:T(8,128)} %rotation_ref.1) | copy-start | bytes 393220
  32.7 7.6 %collective-permute-start = (f32[4,8,128]{2,1,0:T(8,128)S(1)}, f32[4,8,128]{2,1,0:T(8,128)S(1)}, u32[]{:S(2)}, u32[]{:S(2)}) collective-permute-start(f32[4,8,128]{2,1,0:T(8,128)S(1)} %get-tuple-element.26), channel_id=1, source_target_pairs={{4,0},{8,4},{12,8},{0,12},{5,1},{9,5},{13,9},{1,13},{6,2},{10,6},{... | collective-permute-start | bytes 49160 | tf_op jit(solution)/shard_map/ppermute | solution.py:408
  33.1 7.2 %collective-permute-start.1 = (f32[4,8,128]{2,1,0:T(8,128)S(1)}, f32[4,8,128]{2,1,0:T(8,128)S(1)}, u32[]{:S(2)}, u32[]{:S(2)}) collective-permute-start(f32[4,8,128]{2,1,0:T(8,128)S(1)} %get-tuple-element.27), channel_id=1, source_target_pairs={{0,4},{4,8},{8,12},{12,0},{1,5},{5,9},{9,13},{13,1},{2,6},{6,10},{... | collective-permute-start | bytes 49160 | tf_op jit(solution)/shard_map/ppermute | solution.py:409
  40.4 0.7 %copy-start.1 = (s32[3]{0:T(128)S(1)}, s32[3]{0:T(128)}, u32[]{:S(2)}) copy-start(s32[3]{0:T(128)} %shift_ref.1) | copy-start | bytes 40
  40.4 1.6 %collective-permute-start.2 = (f32[4,16,128]{2,1,0:T(8,128)S(1)}, f32[4,16,128]{2,1,0:T(8,128)S(1)}, u32[]{:S(2)}, u32[]{:S(2)}) collective-permute-start(f32[4,16,128]{2,1,0:T(8,128)S(1)} %get-tuple-element.29), channel_id=1, source_target_pairs={{16,0},{32,16},{48,32},{64,48},{80,64},{96,80},{112,96},{0,112},{1... | collective-permute-start | bytes 98312 | tf_op jit(solution)/shard_map/ppermute | solution.py:408
  40.4 4.6 %collective-permute-start.3 = (f32[4,16,128]{2,1,0:T(8,128)S(1)}, f32[4,16,128]{2,1,0:T(8,128)S(1)}, u32[]{:S(2)}, u32[]{:S(2)}) collective-permute-start(f32[4,16,128]{2,1,0:T(8,128)S(1)} %get-tuple-element.30), channel_id=1, source_target_pairs={{0,16},{16,32},{32,48},{48,64},{64,80},{80,96},{96,112},{112,0},{1... | collective-permute-start | bytes 98312 | tf_op jit(solution)/shard_map/ppermute | solution.py:409
  45.1 7.3 %collective-permute-start.4 = (f32[8,128]{1,0:T(8,128)S(1)}, f32[8,128]{1,0:T(8,128)S(1)}, u32[]{:S(2)}, u32[]{:S(2)}) collective-permute-start(f32[8,128]{1,0:T(8,128)S(1)} %get-tuple-element.34), channel_id=1, source_target_pairs={{1,0},{2,1},{3,2},{0,3},{5,4},{6,5},{7,6},{4,7},{9,8},{10,9},{11,1... | collective-permute-start | bytes 12296 | tf_op jit(solution)/shard_map/ppermute | solution.py:408
  46.4 6.1 %collective-permute-start.5 = (f32[8,128]{1,0:T(8,128)S(1)}, f32[8,128]{1,0:T(8,128)S(1)}, u32[]{:S(2)}, u32[]{:S(2)}) collective-permute-start(f32[8,128]{1,0:T(8,128)S(1)} %get-tuple-element.35), channel_id=1, source_target_pairs={{0,1},{1,2},{2,3},{3,0},{4,5},{5,6},{6,7},{7,4},{8,9},{9,10},{10,1... | collective-permute-start | bytes 12296 | tf_op jit(solution)/shard_map/ppermute | solution.py:409

commit v10 on v9

--- a/solution.py
+++ b/solution.py
@@ -121,7 +121,7 @@
     return jnp.sum(jnp.where(same, column, 0.0), axis=0, keepdims=True)
 
 
-DEPOSIT_STEP = 128
+DEPOSIT_STEP = 384
 Q2 = ROWS // 2
 
 

time: 54.1 us -> 53.5 us (0.989)
  Pallas kernels: 18 us -> 17.3 us
  transfers between devices with their start and end apart: 6 -> 6, of which waited for: 2 -> 2; matrix products, arithmetic and copies ran while one was open for 0% -> 0% of each run, Pallas kernels for 22% -> 21%
where the time goes in v10:
time: 53.5 us; the launch traced here: 53.4 us
  blocking collectives  27.3 us (51%)
  Pallas kernels  17.3 us (32%)
  starting transfers between devices  4.71 us (9%)
  waiting for transfers between devices  3.08 us (6%)
  between operations  0.88 us (2%)
    all_to_all x1, blocking collectives, shards(): lax.all_to_all(send.reshape(devices, MOST, 4, 128), ('gx', 'gy', 'gz'), s...  27.3 us
    pallas_call x1, Pallas kernels, shards(): call(look_body, [shape((devices * MOST * 4, 128), f32), shape((MOST, 3, d...  5.24 us
    pallas_call x1, Pallas kernels, shards(): call(deposit_body, total_shape, scratch_shapes=[pltpu.VMEM((2, 192, 128),...  5.06 us
    ppermute x3, starting transfers between devices, both_ways(): lax.ppermute(tail, axis, [(i, (i + 1) % count) for i in range(count)])  2.99 us
    ppermute x3, waiting for transfers between devices, both_ways(): lax.ppermute(tail, axis, [(i, (i + 1) % count) for i in range(count)])  2.97 us
    pallas_call x1, Pallas kernels, shards(): call(deposit_faces_body, [y_face, y_face], scratch_shapes=[pltpu.VMEM((16...  2.8 us
    ppermute x3, starting transfers between devices, both_ways(): up = lax.ppermute(head, axis, [((i + 1) % count, i) for i in range(count)])  1.72 us
    pallas_call x1, Pallas kernels, shards(): call(pack_body, [shape((devices * MOST * 4, 128), f32), shape((3, 8, 128)...  1.67 us
  transfers between devices with their start and end apart: 6, of which 2 were waited for; matrix products, arithmetic and copies ran while one was open for 0% of the time, Pallas kernels for 21%

profile of v10, /device:TPU:0, one launch (start us, length us, event | category | flops | bytes accessed | tf_op | source)
XLA Modules:
  0.0 53.4 jit_solution(8956206100139375947)
XLA Ops:
  0.6 1.7 %pack.1 = (f32[1536,128]{1,0:T(8,128)S(1)}, f32[3,8,128]{2,1,0:T(8,128)S(1)}) custom-call(s32[1,256]{1,0:T(1,128)} %bitcast.13, f32[3,256,128]{2,1,0:T(8,128)} %bitcast.12, s32[256,128]{1,0:T(8,128)} %index_hbm.1), custom_call_target="tpu_custom_call" | custom-call | tf_op jit(solution)/shard_map/pack/pallas_call | solution.py:420
  2.3 27.3 %all_to_all.5 = f32[128,3,4,128]{3,2,1,0:T(4,128)S(1)} all-to-all(f32[128,3,4,128]{3,2,1,0:T(4,128)S(1)} %bitcast.11), channel_id=1, replica_groups=mesh['gx'=8,'gy'=4,'gz'=4] {'gx','gy','gz'}, dimensions={0} | all-to-all | bytes 1572864 | tf_op jit(solution)/shard_map/all_to_all | solution.py:444
  29.6 2.8 %deposit_faces.1 = (f32[4,8,128]{2,1,0:T(8,128)S(1)}, f32[4,8,128]{2,1,0:T(8,128)S(1)}) custom-call(f32[1536,128]{1,0:T(8,128)S(1)} %bitcast.7), custom_call_target="tpu_custom_call" | custom-call | tf_op jit(solution)/shard_map/deposit_faces/pallas_call | solution.py:452
  32.4 0.0 copy-start
  32.4 0.4 collective-permute-start
  32.8 1.7 %collective-permute-start.1 = (f32[4,8,128]{2,1,0:T(8,128)S(1)}, f32[4,8,128]{2,1,0:T(8,128)S(1)}, u32[]{:S(2)}, u32[]{:S(2)}) collective-permute-start(f32[4,8,128]{2,1,0:T(8,128)S(1)} %get-tuple-element.27), channel_id=1, source_target_pairs={{0,4},{4,8},{8,12},{12,0},{1,5},{5,9},{9,13},{13,1},{2,6},{6,10},{... | collective-permute-start | bytes 49160 | tf_op jit(solution)/shard_map/ppermute | solution.py:409
  34.5 5.1 %deposit.1.total_ref = f32[4,48,128]{2,1,0:T(8,128)S(1)} custom-call(f32[1536,128]{1,0:T(8,128)S(1)} %bitcast.8), custom_call_target="tpu_custom_call" | custom-call | tf_op jit(solution)/shard_map/deposit/pallas_call | solution.py:460
  39.6 0.0 collective-permute-done.up_ref
  39.6 0.0 collective-permute-done.1.down_ref
  39.6 0.1 fold_y.1
  39.7 0.0 copy-start.1
  39.7 0.0 collective-permute-start.2
  39.7 0.5 collective-permute-start.3
  40.2 0.0 copy-done
  40.2 0.1 copy-done.1
  40.3 0.9 %axes.1.axes_ref = f32[48,128]{1,0:T(8,128)S(1)} custom-call(s32[3]{0:T(128)S(1)} %copy-done.1, s32[32,32,32]{2,1,0:T(8,128)S(1)} %copy-done), custom_call_target="tpu_custom_call" | custom-call | tf_op jit(solution)/shard_map/axes/pallas_call | solution.py:437
  41.2 0.1 collective-permute-done.2.up_ref
  41.3 3.0 %collective-permute-done.3.down_ref = f32[4,16,128]{2,1,0:T(8,128)S(1)} collective-permute-done((f32[4,16,128]{2,1,0:T(8,128)S(1)}, f32[4,16,128]{2,1,0:T(8,128)S(1)}, u32[]{:S(2)}, u32[]{:S(2)}) %collective-permute-start.3) | collective-permute-done | bytes 32800 | tf_op jit(solution)/shard_map/ppermute | solution.py:409
  44.3 0.2 fold_x.1
  44.4 1.3 %collective-permute-start.4 = (f32[8,128]{1,0:T(8,128)S(1)}, f32[8,128]{1,0:T(8,128)S(1)}, u32[]{:S(2)}, u32[]{:S(2)}) collective-permute-start(f32[8,128]{1,0:T(8,128)S(1)} %get-tuple-element.34), channel_id=1, source_target_pairs={{1,0},{2,1},{3,2},{0,3},{5,4},{6,5},{7,6},{4,7},{9,8},{10,9},{11,1... | collective-permute-start | bytes 12296 | tf_op jit(solution)/shard_map/ppermute | solution.py:408
  45.7 0.8 %collective-permute-start.5 = (f32[8,128]{1,0:T(8,128)S(1)}, f32[8,128]{1,0:T(8,128)S(1)}, u32[]{:S(2)}, u32[]{:S(2)}) collective-permute-start(f32[8,128]{1,0:T(8,128)S(1)} %get-tuple-element.35), channel_id=1, source_target_pairs={{0,1},{1,2},{2,3},{3,0},{4,5},{5,6},{6,7},{7,4},{8,9},{9,10},{10,1... | collective-permute-start | bytes 12296 | tf_op jit(solution)/shard_map/ppermute | solution.py:409
  46.5 5.2 %look.1 = (f32[1536,128]{1,0:T(8,128)S(1)}, f32[3,3,128,128]{3,2,1,0:T(8,128)S(1)}) custom-call(f32[4,48,128]{2,1,0:T(8,128)S(1)} %get-tuple-element.33.total_ref, f32[48,128]{1,0:T(8,128)S(1)} %axes.1.axes_ref, f32[3,8,128]{2,1,0:T(8,128)S(1)} %get-tuple-element.37.units_ref, f32[1536,128]{1,0:T(8,128)S(1)} %bitcast.9), custom_call_target="tpu_custom_call" | custom-call | tf_op jit(solution)/shard_map/look/pallas_call | solution.py:475
  51.8 0.0 collective-permute-done.4.up_ref
  51.8 0.0 collective-permute-done.5.down_ref
  51.8 1.4 %turn.1 = (f32[3,3,128,128]{3,2,1,0:T(8,128)}, f32[3,4,8,128]{3,2,1,0:T(8,128)}) custom-call(f32[4,48,128]{2,1,0:T(8,128)S(1)} %get-tuple-element.33.total_ref, f32[8,128]{1,0:T(8,128)S(1)} %collective-permute-done.4.up_ref, f32[8,128]{1,0:T(8,128)S(1)} %collective-permute-done.5.down_ref, f32[3,3,128,128]{3,2,1,0:T(8,128)S(1)} %get-tuple-element.38.normal_ref, ...), custom_call_target="tpu_custom_call" | custom-call | tf_op jit(solution)/shard_map/turn/pallas_call | solution.py:486
Async XLA Ops:
  32.4 7.8 %copy-start = (s32[32,32,32]{2,1,0:T(8,128)S(1)}, s32[32,32,32]{2,1,0:T(8,128)}, u32[]{:S(2)}) copy-start(s32[32,32,32]{2,1,0:T(8,128)} %rotation_ref.1) | copy-start | bytes 393220
  32.4 7.2 %collective-permute-start = (f32[4,8,128]{2,1,0:T(8,128)S(1)}, f32[4,8,128]{2,1,0:T(8,128)S(1)}, u32[]{:S(2)}, u32[]{:S(2)}) collective-permute-start(f32[4,8,128]{2,1,0:T(8,128)S(1)} %get-tuple-element.26), channel_id=1, source_target_pairs={{4,0},{8,4},{12,8},{0,12},{5,1},{9,5},{13,9},{1,13},{6,2},{10,6},{... | collective-permute-start | bytes 49160 | tf_op jit(solution)/shard_map/ppermute | solution.py:408
  32.8 6.8 %collective-permute-start.1 = (f32[4,8,128]{2,1,0:T(8,128)S(1)}, f32[4,8,128]{2,1,0:T(8,128)S(1)}, u32[]{:S(2)}, u32[]{:S(2)}) collective-permute-start(f32[4,8,128]{2,1,0:T(8,128)S(1)} %get-tuple-element.27), channel_id=1, source_target_pairs={{0,4},{4,8},{8,12},{12,0},{1,5},{5,9},{9,13},{13,1},{2,6},{6,10},{... | collective-permute-start | bytes 49160 | tf_op jit(solution)/shard_map/ppermute | solution.py:409
  39.7 0.7 %copy-start.1 = (s32[3]{0:T(128)S(1)}, s32[3]{0:T(128)}, u32[]{:S(2)}) copy-start(s32[3]{0:T(128)} %shift_ref.1) | copy-start | bytes 40
  39.7 1.6 %collective-permute-start.2 = (f32[4,16,128]{2,1,0:T(8,128)S(1)}, f32[4,16,128]{2,1,0:T(8,128)S(1)}, u32[]{:S(2)}, u32[]{:S(2)}) collective-permute-start(f32[4,16,128]{2,1,0:T(8,128)S(1)} %get-tuple-element.29), channel_id=1, source_target_pairs={{16,0},{32,16},{48,32},{64,48},{80,64},{96,80},{112,96},{0,112},{1... | collective-permute-start | bytes 98312 | tf_op jit(solution)/shard_map/ppermute | solution.py:408
  39.7 4.6 %collective-permute-start.3 = (f32[4,16,128]{2,1,0:T(8,128)S(1)}, f32[4,16,128]{2,1,0:T(8,128)S(1)}, u32[]{:S(2)}, u32[]{:S(2)}) collective-permute-start(f32[4,16,128]{2,1,0:T(8,128)S(1)} %get-tuple-element.30), channel_id=1, source_target_pairs={{0,16},{16,32},{32,48},{48,64},{64,80},{80,96},{96,112},{112,0},{1... | collective-permute-start | bytes 98312 | tf_op jit(solution)/shard_map/ppermute | solution.py:409
  44.4 7.3 %collective-permute-start.4 = (f32[8,128]{1,0:T(8,128)S(1)}, f32[8,128]{1,0:T(8,128)S(1)}, u32[]{:S(2)}, u32[]{:S(2)}) collective-permute-start(f32[8,128]{1,0:T(8,128)S(1)} %get-tuple-element.34), channel_id=1, source_target_pairs={{1,0},{2,1},{3,2},{0,3},{5,4},{6,5},{7,6},{4,7},{9,8},{10,9},{11,1... | collective-permute-start | bytes 12296 | tf_op jit(solution)/shard_map/ppermute | solution.py:408
  45.7 6.1 %collective-permute-start.5 = (f32[8,128]{1,0:T(8,128)S(1)}, f32[8,128]{1,0:T(8,128)S(1)}, u32[]{:S(2)}, u32[]{:S(2)}) collective-permute-start(f32[8,128]{1,0:T(8,128)S(1)} %get-tuple-element.35), channel_id=1, source_target_pairs={{0,1},{1,2},{2,3},{3,0},{4,5},{5,6},{6,7},{7,4},{8,9},{9,10},{10,1... | collective-permute-start | bytes 12296 | tf_op jit(solution)/shard_map/ppermute | solution.py:409
